TPU v7x, 128 devices: a whole 4x4x4 slice. The times are simulated.
128 devices in a mesh: gx: 16 (over x, z), gy: 8 (over y, core).
Axes of the slice: x: 4, y: 4, z: 4, core: 2. Of those that a mesh axis runs over, the one named last changes fastest.
Arguments:
- velocity: float32 [3, 256, 256, 256], P(None, 'gx', 'gy'), may hold values from -6 to 6
- owner_block: int32 [262144, 1], P(('gx', 'gy')), may hold values from 0 to 127, as said below
- base_x: int32 [262144], P(('gx', 'gy')), may hold values from 0 to 16
- base_y: int32 [262144], P(('gx', 'gy')), may hold values from 0 to 32
- base_z: int32 [262144], P(('gx', 'gy')), may hold values from 0 to 255
- delta_weights: float32 [12, 262144], P(None, ('gx', 'gy')), may hold values from 0.1 to 1
- marker_offset: float32 [3, 262144], P(None, ('gx', 'gy')), may hold values from -4 to 4
- sphere_motion: float32 [6, 256], P(None, ('gx', 'gy')), may hold values from -6 to 6
- contact_sphere: int32 [512], P(('gx', 'gy')), may hold values from 0 to 255, as said below
- contact_partner: int32 [512], P(('gx', 'gy')), may hold values from 0 to 255
Outputs:
- velocity_star: float32 [3, 256, 256, 256], P(None, 'gx', 'gy')
- new_motion: float32 [6, 256], P(None, ('gx', 'gy'))
Inputs may be any that keep to these rules, and one draw needn't show every extreme that they name: `owner_block`: block b stands at gx index b // 8 and gy index b % 8. Each marker's owner block is the block of the device that holds the marker or one of the eight blocks beside it (periodic along gx, none beyond the walls along gy). Among the markers of one device, at most 256 have any one owner block other than that device's own, and in every device exactly 256 have one such block. `contact_sphere`: entry k names one of the 2 spheres k // 4 * 2 and after, those of the device that holds entry k.
All inputs are finite; a program needn't handle non-finite values.
Results may differ from a plain program's by a relative error of at most 0.0003.
Values sent between devices are 32-bit elements; how exact they have to be, the bound alone decides.
A program may use at most 64 MiB of HBM per device.

v0:
```python
import jax
import jax.numpy as jnp
from jax import lax
from jax.sharding import PartitionSpec as P

ITERS = 4


DIFFUSION = 1.0
RESPONSE = 0.5
DASHPOT = 0.1


def with_halo(array, sides, width):
    for axis, dim in sides:
        size, length = (lax.axis_size(axis), array.shape[dim])
        up = [(i, (i + 1) % size) for i in range(size)]
        down = [(j, i) for i, j in up]
        last = lax.slice_in_dim(array, length - width, length, axis=dim)
        leading = lax.slice_in_dim(array, 0, width, axis=dim)
        before = lax.ppermute(last, axis, up)
        after = lax.ppermute(leading, axis, down)
        array = jnp.concatenate([before, array, after], axis=dim)
    return array


def weight_table(start, weights, extent, wrapped):
    positions = jnp.arange(extent, dtype=jnp.int32)[:, None]
    table = jnp.zeros((extent, start.shape[0]), jnp.float32)
    for offset in range(4):
        target_cell = start + offset
        if wrapped:
            target_cell = target_cell % extent
        table = table + weights[offset][None, :] * (positions == target_cell[None, :]).astype(
            jnp.float32
        )
    return table


def sample_field(field, table_x, table_y, table_z):
    extent_z = field.shape[3]
    partial_z = jnp.dot(field.reshape(-1, extent_z), table_z, precision=lax.Precision.HIGHEST)
    partial_z = partial_z.reshape(3, field.shape[1], field.shape[2], -1)
    partial_y = jnp.sum(partial_z * table_y[None, None, :, :], axis=2)
    return jnp.sum(partial_y * table_x[None, :, :], axis=1)


def deposit_field(forces, table_x, table_y, table_z):
    spread_xy = forces[:, None, None, :] * table_x[None, :, None, :] * table_y[None, None, :, :]
    count = forces.shape[1]
    flat = lax.dot_general(
        spread_xy.reshape(-1, count),
        table_z,
        (((1,), (1,)), ((), ())),
        precision=lax.Precision.HIGHEST,
    )
    return flat.reshape(3, table_x.shape[0], table_y.shape[0], table_z.shape[0])


def wall_mask(row_index, row_count, span_y, margin):
    rows_ext = jnp.arange(span_y + 2 * margin, dtype=jnp.int32)
    global_row = row_index * span_y - margin + rows_ext
    inside = jnp.logical_and(global_row >= 0, global_row < span_y * row_count)
    return inside.astype(jnp.float32)


def faces(state, margin, row_index, row_count):
    grown = with_halo(state, (("gx", 1), ("gy", 2)), margin)
    return grown * wall_mask(row_index, row_count, state.shape[2], margin)[None, None, :, None]


def relax(grown, rhs_part):
    center = grown[:, 1:-1, 1:-1]
    beside_all = grown[:, 2:, 1:-1] + grown[:, :-2, 1:-1] + grown[:, 1:-1, 2:] + grown[:, 1:-1, :-2]
    beside_all = beside_all + jnp.roll(center, -1, 3) + jnp.roll(center, 1, 3)
    return (rhs_part + DIFFUSION * beside_all) / (1.0 + 6.0 * DIFFUSION)


def send_requests(buffer):
    width_rows = buffer.shape[0]
    grown = with_halo(buffer.reshape(width_rows, 3, 3, -1), (("gx", 1), ("gy", 2)), 1)
    return grown[:, 0::2, 0::2].reshape(width_rows, -1)


def send_force_replies(buffer):
    grown = with_halo(buffer.reshape(3, 3, 3, -1), (("gx", 1), ("gy", 2)), 1)
    return grown[:, 0::2, 0::2].reshape(3, -1)


def on_device(
    velocity,
    owner_block,
    base_x,
    base_y,
    base_z,
    delta_weights,
    marker_offset,
    sphere_motion,
    contact_sphere,
    contact_partner,
):
    span_x = velocity.shape[1]
    span_y = velocity.shape[2]
    extent_z = velocity.shape[3]
    row_count = lax.axis_size("gy")
    column_count = lax.axis_size("gx")
    here = lax.axis_index(("gx", "gy"))
    row_index = lax.axis_index("gy")
    column_index = lax.axis_index("gx")
    grown_field = with_halo(velocity, (("gx", 1), ("gy", 2)), 2)
    grown_field = grown_field * wall_mask(row_index, row_count, span_y, 2)[None, None, :, None]
    markers = base_x.shape[0]
    spheres_here = sphere_motion.shape[1]
    per_sphere = markers // spheres_here
    capacity = markers // 8
    owner = owner_block[:, 0]
    at_home = owner == here
    home_weight = at_home.astype(jnp.float32)
    lanes = 9
    step_x = (owner // row_count - column_index + 1 + column_count) % column_count
    step_y = owner % row_count - row_index + 1
    lane = step_x * 3 + step_y
    hits = (lane[:, None] == jnp.arange(lanes, dtype=jnp.int32)[None, :]).astype(jnp.int32)
    hits = hits * (1 - at_home.astype(jnp.int32))[:, None]
    ranked = jnp.sum((jnp.cumsum(hits, axis=0) - hits) * hits, axis=1)
    total_slots = lanes * capacity
    slots = jnp.where(at_home, total_slots, lane * capacity + ranked)
    fetch_slots = jnp.minimum(slots, total_slots - 1)
    linear = sphere_motion[0:3]
    angular = sphere_motion[3:6]
    marker_linear = jnp.broadcast_to(linear[:, :, None], (3, spheres_here, per_sphere)).reshape(
        3, markers
    )
    marker_angular = jnp.broadcast_to(angular[:, :, None], (3, spheres_here, per_sphere)).reshape(
        3, markers
    )
    target = marker_linear + jnp.cross(marker_angular, marker_offset, axis=0)
    coords = jnp.stack([base_x, base_y, base_z]).astype(jnp.float32)
    payload = jnp.concatenate([delta_weights, coords, target], axis=0)
    width_rows = payload.shape[0]
    outgoing = (
        jnp.zeros((width_rows, total_slots), jnp.float32).at[:, slots].set(payload, mode="drop")
    )
    arrived = send_requests(outgoing)
    cell_start = arrived[12:15].astype(jnp.int32)
    start_x = jnp.concatenate([base_x, cell_start[0]])
    start_y = jnp.concatenate([base_y, cell_start[1]])
    start_z = jnp.concatenate([base_z, cell_start[2]])
    weights_all = jnp.concatenate([delta_weights, arrived[0:12]], axis=1)
    table_x = weight_table(start_x, weights_all[0:4], span_x + 4, False)
    table_y = weight_table(start_y, weights_all[4:8], span_y + 4, False)
    table_z = weight_table(start_z, weights_all[8:12], extent_z, True)
    sampled_all = sample_field(grown_field, table_x, table_y, table_z)
    sampled_home = sampled_all[:, :markers]
    sampled = sampled_all[:, markers:]
    slot_force = arrived[15:18] - sampled
    returned = send_force_replies(slot_force)
    force = jnp.where(at_home[None, :], target - sampled_home, returned[:, fetch_slots])
    forces_all = jnp.concatenate([force * home_weight[None, :], slot_force], axis=1)
    spread = deposit_field(forces_all, table_x, table_y, table_z)
    rims = with_halo(spread, (("gx", 1), ("gy", 2)), 2)
    lower = (row_index > 0).astype(jnp.float32)
    upper = (row_index < row_count - 1).astype(jnp.float32)
    source = spread[:, 2 : span_x + 2, 2 : span_y + 2]
    source = source.at[:, 0:2].add(rims[:, 0:2, 4 : span_y + 4])
    source = source.at[:, span_x - 2 :].add(rims[:, span_x + 6 :, 4 : span_y + 4])
    source = source.at[:, :, 0:2].add(lower * rims[:, 4 : span_x + 4, 0:2])
    source = source.at[:, :, span_y - 2 :].add(upper * rims[:, 4 : span_x + 4, span_y + 6 :])
    source = source.at[:, 0:2, 0:2].add(lower * rims[:, 0:2, 0:2])
    source = source.at[:, 0:2, span_y - 2 :].add(upper * rims[:, 0:2, span_y + 6 :])
    source = source.at[:, span_x - 2 :, 0:2].add(lower * rims[:, span_x + 6 :, 0:2])
    source = source.at[:, span_x - 2 :, span_y - 2 :].add(
        upper * rims[:, span_x + 6 :, span_y + 6 :]
    )
    push = jnp.sum(force.reshape(3, spheres_here, per_sphere), axis=-1) / per_sphere
    twist = (
        jnp.sum(
            jnp.cross(marker_offset, force, axis=0).reshape(3, spheres_here, per_sphere), axis=-1
        )
        / per_sphere
    )
    moved = linear - RESPONSE * push
    turned = angular - RESPONSE * twist
    everyone = lax.all_gather(moved, ("gx", "gy"), axis=1, tiled=True)
    all_spheres = everyone.shape[1]
    pick_partner = (
        contact_partner[:, None] == jnp.arange(all_spheres, dtype=jnp.int32)[None, :]
    ).astype(jnp.float32)
    partner_moved = jnp.dot(everyone, pick_partner.T, precision=lax.Precision.HIGHEST)
    local_sphere = contact_sphere - here * spheres_here
    pick_own = (jnp.arange(spheres_here, dtype=jnp.int32)[:, None] == local_sphere[None, :]).astype(
        jnp.float32
    )
    own_moved = jnp.dot(moved, pick_own, precision=lax.Precision.HIGHEST)
    spring = jnp.dot(partner_moved - own_moved, pick_own.T, precision=lax.Precision.HIGHEST)
    settled = moved + DASHPOT * spring
    new_motion = jnp.concatenate([settled, turned], axis=0)
    rhs = velocity + source
    state = rhs
    rhs_cycle = rhs
    for sweep_pair in range(ITERS // 2):
        grown = faces(state, 2, row_index, row_count)
        if sweep_pair == 0:
            rhs_cycle = grown[:, 1:-1, 1:-1]
        middle = relax(grown, rhs_cycle)
        middle = middle * wall_mask(row_index, row_count, span_y, 1)[None, None, :, None]
        state = relax(middle, rhs)
    return (state, new_motion)


def solution(mesh):
    placed = (
        P(None, "gx", "gy", None),
        P(("gx", "gy"), None),
        P(("gx", "gy")),
        P(("gx", "gy")),
        P(("gx", "gy")),
        P(None, ("gx", "gy")),
        P(None, ("gx", "gy")),
        P(None, ("gx", "gy")),
        P(("gx", "gy")),
        P(("gx", "gy")),
    )
    return jax.shard_map(
        on_device,
        mesh=mesh,
        in_specs=placed,
        out_specs=(P(None, "gx", "gy", None), P(None, ("gx", "gy"))),
        check_vma=False,
    )
```

profile of v0, /device:TPU:1, one launch (start us, length us, event | category | flops | bytes accessed | tf_op | source)
XLA Modules:
  0.0 262.9 jit_solution(7945562148109077479)
XLA Ops:
  0.7 1.8 fusion.94
  2.5 6.8 %collective-permute-start.1 = (f32[3,2,32,256]{3,2,1,0:T(8,128)}, f32[3,2,32,256]{3,2,1,0:T(8,128)}, u32[]{:S(2)}, u32[]{:S(2)}) collective-permute-start(f32[3,2,32,256]{3,2,1,0:T(8,128)} %get-tuple-element.145), channel_id=1, source_target_pairs={{8,0},{16,8},{24,16},{32,24},{40,32},{48,40},{56,48},{64,56},{72,6... | collective-permute-start | bytes 589832 | tf_op jit(solution)/shard_map/ppermute | solution.py:22
  9.3 0.8 fusion.99
  10.5 0.8 fusion.68
  11.3 2.6 reduce-window.6
  14.6 0.7 compare_select_fusion
  16.0 5.9 %scatter_custom_fusion = f32[18,2304]{0,1:T(8,128)S(1)} fusion(s32[2048]{0:T(1024)S(1)} %bitcast.93, f32[2048,18]{1,0:T(8,128)S(1)} %copy.59, f32[]{:T(128)} %constant.346.clone.1), kind=kCustom, calls=%fused_computation.79 | custom fusion | bytes 165892 | tf_op jit(solution)/shard_map/scatter | solution.py:142
  22.5 4.8 %collective-permute-start.5 = (f32[18,1,3,256]{3,2,1,0:T(4,128)S(1)}, f32[18,1,3,256]{3,2,1,0:T(4,128)S(1)}, u32[]{:S(2)}, u32[]{:S(2)}) collective-permute-start(f32[18,1,3,256]{3,2,1,0:T(4,128)S(1)} %get-tuple-element.152), channel_id=1, source_target_pairs={{8,0},{16,8},{24,16},{32,24},{40,32},{48,40},{56,48},{64,56},{72,6... | collective-permute-start | bytes 165896 | tf_op jit(solution)/shard_map/ppermute | solution.py:22
  27.3 0.6 fusion.79
  28.0 0.6 constant_dynamic-update-slice_fusion.3
  29.1 0.8 and_reduce_fusion
  29.9 0.6 fusion.100
  30.6 2.7 %collective-permute-start.6 = (f32[18,5,1,256]{3,2,1,0:T(1,128)S(1)}, f32[18,5,1,256]{3,2,1,0:T(1,128)S(1)}, u32[]{:S(2)}, u32[]{:S(2)}) collective-permute-start(f32[18,5,1,256]{3,2,1,0:T(1,128)S(1)} %get-tuple-element.147), channel_id=1, source_target_pairs={{0,1},{1,2},{2,3},{3,4},{4,5},{5,6},{6,7},{7,0},{8,9},{9,10},{10,1... | collective-permute-start | bytes 276488 | tf_op jit(solution)/shard_map/ppermute | solution.py:21
  33.4 1.6 collective-permute-done.6
  34.9 2.4 collective-permute-done.7
  37.6 2.1 slice.631
  41.0 0.9 constant_dynamic-update-slice_fusion.2
  42.1 0.9 constant_dynamic-update-slice_fusion
  43.7 0.8 add_select_fusion.3
  44.5 0.6 collective-permute-done.2
  45.1 2.7 %collective-permute-done.3 = f32[3,20,2,256]{3,2,1,0:T(2,128)S(1)} collective-permute-done((f32[3,20,2,256]{3,2,1,0:T(2,128)S(1)}, f32[3,20,2,256]{3,2,1,0:T(2,128)S(1)}, u32[]{:S(2)}, u32[]{:S(2)}) %collective-permute-start.3) | collective-permute-done | bytes 122912 | tf_op jit(solution)/shard_map/ppermute | solution.py:22
  48.3 46.2 %multiply_reduce_fusion = f32[3,20,4352]{2,1,0:T(8,128)S(1)} fusion(f32[36,4352]{1,0:T(8,128)S(1)} %select_add_fusion.3, f32[4352]{0:T(1024)S(1)} %get-tuple-element.107, s32[4352]{0:T(1024)S(1)} %get-tuple-element.172, f32[4352]{0:T(1024)S(1)} %get-tuple-element.108, s32[4352]{0:T(1024)S(1)} %get-tuple-element.171, f32[4352]{0:T(1024)S(1)} %get-tuple-element.109, ...), kind=kOutput, calls=%fused_computation.4 | convolution fusion | flops 28908576768 | bytes 4022272 | tf_op jit(solution)/shard_map/dot_general | solution.py:42
  94.9 0.6 and_select_fusion.3
  95.4 4.8 %collective-permute-start.9 = (f32[3,1,3,256]{3,2,1,0:T(4,128)S(1)}, f32[3,1,3,256]{3,2,1,0:T(4,128)S(1)}, u32[]{:S(2)}, u32[]{:S(2)}) collective-permute-start(f32[3,1,3,256]{3,2,1,0:T(4,128)S(1)} %get-tuple-element.161), channel_id=1, source_target_pairs={{8,0},{16,8},{24,16},{32,24},{40,32},{48,40},{56,48},{64,56},{72,6... | collective-permute-start | bytes 27656 | tf_op jit(solution)/shard_map/ppermute | solution.py:22
  101.1 0.8 collective-permute-start.10
  101.9 1.3 collective-permute-start.11
  103.2 3.6 %fusion.112 = f32[256,4352,1,1]{1,0,3,2:T(8,128)} fusion(f32[4352]{0:T(1024)S(1)} %get-tuple-element.107, s32[4352]{0:T(1024)S(1)} %get-tuple-element.172, f32[4352]{0:T(1024)S(1)} %get-tuple-element.108, s32[4352]{0:T(1024)S(1)} %get-tuple-element.171, f32[4352]{0:T(1024)S(1)} %get-tuple-element.109, s32[4352]{0:T(1024)S(1)} %get-tuple-element.170, ...), kind=kLoop, calls=%fused_computation.7.clone.2 | loop fusion | flops 12255232 | bytes 4595712 | tf_op jit(solution)/shard_map/dot_general | solution.py:51
  107.3 5.5 %gather_fusion = f32[2048,3]{1,0:T(8,128)S(1)} fusion(f32[3,2304]{0,1:T(8,128)S(1)} %bitcast.73, s32[2048]{0:T(1024)S(1)} %broadcast_clamp_fusion), kind=kCustom, calls=%fused_computation | custom fusion | bytes 57344 | tf_op jit(solution)/shard_map/gather | solution.py:158
  113.1 0.7 broadcast_multiply_fusion.1
  114.0 35.6 %fusion = f32[3,20,36,256]{3,2,1,0:T(8,128)S(1)} fusion(f32[3,20,4352]{2,1,0:T(8,128)S(1)} %broadcast_multiply_fusion, f32[36,4352]{1,0:T(8,128)S(1)} %select_add_fusion.3, f32[256,4352,1,1]{1,0,3,2:T(8,128)} %fusion.112), kind=kOutput, calls=%fused_computation.2 | convolution fusion | flops 28887183360 | bytes 8339456 | tf_op jit(solution)/shard_map/dot_general | solution.py:51
  149.6 1.4 slice.786
  151.2 5.8 %collective-permute-start.13 = (f32[3,2,36,256]{3,2,1,0:T(8,128)S(1)}, f32[3,2,36,256]{3,2,1,0:T(8,128)S(1)}, u32[]{:S(2)}, u32[]{:S(2)}) collective-permute-start(f32[3,2,36,256]{3,2,1,0:T(8,128)S(1)} %get-tuple-element.125), channel_id=1, source_target_pairs={{8,0},{16,8},{24,16},{32,24},{40,32},{48,40},{56,48},{64,56},{72,6... | collective-permute-start | bytes 663560 | tf_op jit(solution)/shard_map/ppermute | solution.py:22
  157.3 2.9 %collective-permute-done.13 = f32[3,2,36,256]{3,2,1,0:T(8,128)S(1)} collective-permute-done((f32[3,2,36,256]{3,2,1,0:T(8,128)S(1)}, f32[3,2,36,256]{3,2,1,0:T(8,128)S(1)}, u32[]{:S(2)}, u32[]{:S(2)}) %collective-permute-start.13) | collective-permute-done | bytes 221216 | tf_op jit(solution)/shard_map/ppermute | solution.py:22
  160.2 5.2 %collective-permute-done.12 = f32[3,2,36,256]{3,2,1,0:T(8,128)S(1)} collective-permute-done((f32[3,2,36,256]{3,2,1,0:T(8,128)S(1)}, f32[3,2,36,256]{3,2,1,0:T(8,128)S(1)}, u32[]{:S(2)}, u32[]{:S(2)}) %collective-permute-start.12) | collective-permute-done | bytes 221216 | tf_op jit(solution)/shard_map/ppermute | solution.py:21
  165.5 4.4 %collective-permute-start.15 = (f32[3,24,2,256]{3,2,1,0:T(2,128)S(1)}, f32[3,24,2,256]{3,2,1,0:T(2,128)S(1)}, u32[]{:S(2)}, u32[]{:S(2)}) collective-permute-start(f32[3,24,2,256]{3,2,1,0:T(2,128)S(1)} %get-tuple-element.115), channel_id=1, source_target_pairs={{1,0},{2,1},{3,2},{4,3},{5,4},{6,5},{7,6},{0,7},{9,8},{10,9},{11,1... | collective-permute-start | bytes 442376 | tf_op jit(solution)/shard_map/ppermute | solution.py:22
  169.9 0.7 fusion.49
  170.6 1.6 fusion.48
  172.2 1.7 fusion.54
  173.9 1.7 fusion.52
  175.6 1.4 fusion.66
  177.0 2.7 %add_select_fusion.4 = f32[3,2,2,256]{3,2,1,0:T(2,128)S(1)} fusion(f32[3,24,2,256]{3,2,1,0:T(2,128)S(1)} %collective-permute-done.15, f32[3,16,32,256]{3,2,1,0:T(8,128)} %fusion.66, s32[]{:T(128)} %bitcast.22, s32[]{:T(128)} %bitcast.23, pred[]{:T(512)} %and_reduce_fusion, f32[]{:T(128)S(6)} %convert_element_type.60), kind=kLoop, calls=%fused_computation.159 | loop fusion | flops 9216 | bytes 36877 | tf_op jit(solution)/shard_map/select.13
  179.8 2.7 %scatter-add.35 = f32[3,16,32,256]{3,2,1,0:T(8,128)} dynamic-update-slice(f32[3,16,32,256]{3,2,1,0:T(8,128)} %fusion.66, f32[3,2,2,256]{3,2,1,0:T(2,128)S(1)} %add_select_fusion.4, s32[]{:T(128)} %constant.344.clone.1, s32[]{:T(128)} %bitcast.22, s32[]{:T(128)} %bitcast.23, s32[]{:T(128)} %constant.344.clone.1) | dynamic-update-slice | bytes 24580 | tf_op jit(solution)/shard_map/scatter-add | solution.py:170
  182.5 1.4 fusion.64
  183.9 1.4 fusion.62
  185.3 2.2 add.428
  187.6 4.8 %collective-permute-start.17 = (f32[3,2,32,256]{3,2,1,0:T(8,128)S(1)}, f32[3,2,32,256]{3,2,1,0:T(8,128)S(1)}, u32[]{:S(2)}, u32[]{:S(2)}) collective-permute-start(f32[3,2,32,256]{3,2,1,0:T(8,128)S(1)} %get-tuple-element.144), channel_id=1, source_target_pairs={{8,0},{16,8},{24,16},{32,24},{40,32},{48,40},{56,48},{64,56},{72,6... | collective-permute-start | bytes 589832 | tf_op jit(solution)/shard_map/ppermute | solution.py:22
  192.5 37.0 %all-gather = f32[128,2,3]{2,1,0:T(2,128)S(1)} all-gather(f32[1,2,3]{2,1,0:T(2,128)S(1)} %get-tuple-element.178), channel_id=1, replica_groups=mesh['gx'=16,'gy'=8] {'gx','gy'}, dimensions={0}, use_global_device_ids=true | all-gather | bytes 3096 | tf_op jit(solution)/shard_map/all_gather | solution.py:184
  230.4 1.1 collective-permute-done.18
  231.5 2.7 %collective-permute-done.19 = f32[3,20,2,256]{3,2,1,0:T(2,128)S(1)} collective-permute-done((f32[3,20,2,256]{3,2,1,0:T(2,128)S(1)}, f32[3,20,2,256]{3,2,1,0:T(2,128)S(1)}, u32[]{:S(2)}, u32[]{:S(2)}) %collective-permute-start.19) | collective-permute-done | bytes 122912 | tf_op jit(solution)/shard_map/ppermute | solution.py:22
  235.1 0.8 fusion.85
  236.0 2.2 fusion.35
  238.5 0.7 fusion.90
  239.2 0.9 fusion.43
  240.2 1.5 collective-permute-start.20
  241.7 3.5 %collective-permute-start.21 = (f32[3,2,32,256]{3,2,1,0:T(8,128)S(1)}, f32[3,2,32,256]{3,2,1,0:T(8,128)S(1)}, u32[]{:S(2)}, u32[]{:S(2)}) collective-permute-start(f32[3,2,32,256]{3,2,1,0:T(8,128)S(1)} %get-tuple-element.142), channel_id=1, source_target_pairs={{8,0},{16,8},{24,16},{32,24},{40,32},{48,40},{56,48},{64,56},{72,6... | collective-permute-start | bytes 589832 | tf_op jit(solution)/shard_map/ppermute | solution.py:22
  245.4 3.6 %collective-permute-done.20 = f32[3,2,32,256]{3,2,1,0:T(8,128)S(1)} collective-permute-done((f32[3,2,32,256]{3,2,1,0:T(8,128)S(1)}, f32[3,2,32,256]{3,2,1,0:T(8,128)S(1)}, u32[]{:S(2)}, u32[]{:S(2)}) %collective-permute-start.20) | collective-permute-done | bytes 196640 | tf_op jit(solution)/shard_map/ppermute | solution.py:21
  249.1 1.8 collective-permute-start.22
  251.2 0.7 pad_maximum_fusion.16
  251.8 0.9 collective-permute-done.22
  252.7 2.7 %collective-permute-done.23 = f32[3,20,2,256]{3,2,1,0:T(2,128)S(1)} collective-permute-done((f32[3,20,2,256]{3,2,1,0:T(2,128)S(1)}, f32[3,20,2,256]{3,2,1,0:T(2,128)S(1)}, u32[]{:S(2)}, u32[]{:S(2)}) %collective-permute-start.23) | collective-permute-done | bytes 122912 | tf_op jit(solution)/shard_map/ppermute | solution.py:22
  256.3 0.8 fusion.83
  257.2 2.5 fusion.31
  259.9 0.7 fusion.88
  260.6 2.1 fusion.39
  (153 shorter events, 12.3 us)
Async XLA Ops:
  0.6 14.7 %copy-start.3 = (f32[3,2048]{1,0:T(4,128)S(1)}, f32[3,2048]{1,0:T(4,128)}, u32[]{:S(2)}) copy-start(f32[3,2048]{1,0:T(4,128)} %param.34) | copy-start | bytes 73732
  0.6 14.8 %copy-start.6 = (s32[2048]{0:T(1024)S(1)}, s32[2048]{0:T(1024)}, u32[]{:S(2)}) copy-start(s32[2048]{0:T(1024)} %param.30) | copy-start | bytes 24580
  0.7 14.8 %copy-start.7 = (s32[2048]{0:T(1024)S(1)}, s32[2048]{0:T(1024)}, u32[]{:S(2)}) copy-start(s32[2048]{0:T(1024)} %param.31) | copy-start | bytes 24580
  0.7 14.8 %copy-start.8 = (s32[2048]{0:T(1024)S(1)}, s32[2048]{0:T(1024)}, u32[]{:S(2)}) copy-start(s32[2048]{0:T(1024)} %param.32) | copy-start | bytes 24580
  0.7 14.8 %copy-start.1 = (f32[12,2048]{1,0:T(8,128)S(1)}, f32[12,2048]{1,0:T(8,128)}, u32[]{:S(2)}) copy-start(f32[12,2048]{1,0:T(8,128)} %param.33) | copy-start | bytes 294916
  2.5 39.6 %collective-permute-start.1 = (f32[3,2,32,256]{3,2,1,0:T(8,128)}, f32[3,2,32,256]{3,2,1,0:T(8,128)}, u32[]{:S(2)}, u32[]{:S(2)}) collective-permute-start(f32[3,2,32,256]{3,2,1,0:T(8,128)} %get-tuple-element.145), channel_id=1, source_target_pairs={{8,0},{16,8},{24,16},{32,24},{40,32},{48,40},{56,48},{64,56},{72,6... | collective-permute-start | bytes 589832 | tf_op jit(solution)/shard_map/ppermute | solution.py:22
  9.3 31.7 %collective-permute-start = (f32[3,2,32,256]{3,2,1,0:T(8,128)}, f32[3,2,32,256]{3,2,1,0:T(8,128)}, u32[]{:S(2)}, u32[]{:S(2)}) collective-permute-start(f32[3,2,32,256]{3,2,1,0:T(8,128)} %get-tuple-element.146), channel_id=1, source_target_pairs={{0,8},{8,16},{16,24},{24,32},{32,40},{40,48},{48,56},{56,64},{64,7... | collective-permute-start | bytes 589832 | tf_op jit(solution)/shard_map/ppermute | solution.py:21
  15.5 11.8 %copy-start.2 = (s32[2048,1]{0,1:T(1,128)S(1)}, s32[2048,1]{0,1:T(1,128)}, u32[]{:S(2)}) copy-start(s32[2048,1]{0,1:T(1,128)} %param.29) | copy-start | bytes 24580
  15.6 13.0 %copy-start.16 = (s32[4]{0:T(128)S(1)}, s32[4]{0:T(128)}, u32[]{:S(2)}) copy-start(s32[4]{0:T(128)} %param.36) | copy-start | bytes 52
  15.6 13.5 %copy-start.15 = (s32[4]{0:T(128)S(1)}, s32[4]{0:T(128)}, u32[]{:S(2)}) copy-start(s32[4]{0:T(128)} %constant.361.clone.1) | copy-start | bytes 52
  22.4 8.1 %collective-permute-start.4 = (f32[18,1,3,256]{3,2,1,0:T(4,128)S(1)}, f32[18,1,3,256]{3,2,1,0:T(4,128)S(1)}, u32[]{:S(2)}, u32[]{:S(2)}) collective-permute-start(f32[18,1,3,256]{3,2,1,0:T(4,128)S(1)} %get-tuple-element.151), channel_id=1, source_target_pairs={{0,8},{8,16},{16,24},{24,32},{32,40},{40,48},{48,56},{56,64},{64,7... | collective-permute-start | bytes 165896 | tf_op jit(solution)/shard_map/ppermute | solution.py:21
  22.5 8.0 %collective-permute-start.5 = (f32[18,1,3,256]{3,2,1,0:T(4,128)S(1)}, f32[18,1,3,256]{3,2,1,0:T(4,128)S(1)}, u32[]{:S(2)}, u32[]{:S(2)}) collective-permute-start(f32[18,1,3,256]{3,2,1,0:T(4,128)S(1)} %get-tuple-element.152), channel_id=1, source_target_pairs={{8,0},{16,8},{24,16},{32,24},{40,32},{48,40},{56,48},{64,56},{72,6... | collective-permute-start | bytes 165896 | tf_op jit(solution)/shard_map/ppermute | solution.py:22
  30.6 4.3 %collective-permute-start.6 = (f32[18,5,1,256]{3,2,1,0:T(1,128)S(1)}, f32[18,5,1,256]{3,2,1,0:T(1,128)S(1)}, u32[]{:S(2)}, u32[]{:S(2)}) collective-permute-start(f32[18,5,1,256]{3,2,1,0:T(1,128)S(1)} %get-tuple-element.147), channel_id=1, source_target_pairs={{0,1},{1,2},{2,3},{3,4},{4,5},{5,6},{6,7},{7,0},{8,9},{9,10},{10,1... | collective-permute-start | bytes 276488 | tf_op jit(solution)/shard_map/ppermute | solution.py:21
  33.4 4.0 %collective-permute-start.7 = (f32[18,5,1,256]{3,2,1,0:T(1,128)S(1)}, f32[18,5,1,256]{3,2,1,0:T(1,128)S(1)}, u32[]{:S(2)}, u32[]{:S(2)}) collective-permute-start(f32[18,5,1,256]{3,2,1,0:T(1,128)S(1)} %get-tuple-element.148), channel_id=1, source_target_pairs={{1,0},{2,1},{3,2},{4,3},{5,4},{6,5},{7,6},{0,7},{9,8},{10,9},{11,1... | collective-permute-start | bytes 276488 | tf_op jit(solution)/shard_map/ppermute | solution.py:22
  33.4 14.4 %copy-start.11 = (f32[36]{0:T(128)}, f32[36]{0:T(128)S(1)}, u32[]{:S(2)}) copy-start(f32[36]{0:T(128)S(1)} %and_convert_fusion) | copy-start | bytes 436
  37.6 4.4 %copy-start = (f32[3,16,32,256]{3,2,1,0:T(8,128)S(1)}, f32[3,16,32,256]{3,2,1,0:T(8,128)}, u32[]{:S(2)}) copy-start(f32[3,16,32,256]{3,2,1,0:T(8,128)} %param.28) | copy-start | bytes 4718596
  39.7 1.3 copy-start.4
  41.0 2.1 copy-start.5
  43.2 1.9 collective-permute-start.2
  43.2 4.6 %collective-permute-start.3 = (f32[3,20,2,256]{3,2,1,0:T(2,128)S(1)}, f32[3,20,2,256]{3,2,1,0:T(2,128)S(1)}, u32[]{:S(2)}, u32[]{:S(2)}) collective-permute-start(f32[3,20,2,256]{3,2,1,0:T(2,128)S(1)} %get-tuple-element.140), channel_id=1, source_target_pairs={{1,0},{2,1},{3,2},{4,3},{5,4},{6,5},{7,6},{0,7},{9,8},{10,9},{11,1... | collective-permute-start | bytes 368648 | tf_op jit(solution)/shard_map/ppermute | solution.py:22
  48.3 47.2 %copy-start.9 = (pred[2048]{0:T(1024)(128)(4,1)S(1)}, pred[2048]{0:T(1024)(128)(4,1)}, u32[]{:S(2)}) copy-start(pred[2048]{0:T(1024)(128)(4,1)} %fusion.79) | copy-start | bytes 6148
  94.8 5.9 %collective-permute-start.8 = (f32[3,1,3,256]{3,2,1,0:T(4,128)S(1)}, f32[3,1,3,256]{3,2,1,0:T(4,128)S(1)}, u32[]{:S(2)}, u32[]{:S(2)}) collective-permute-start(f32[3,1,3,256]{3,2,1,0:T(4,128)S(1)} %get-tuple-element.162), channel_id=1, source_target_pairs={{0,8},{8,16},{16,24},{24,32},{32,40},{40,48},{48,56},{56,64},{64,7... | collective-permute-start | bytes 27656 | tf_op jit(solution)/shard_map/ppermute | solution.py:21
  95.4 5.6 %collective-permute-start.9 = (f32[3,1,3,256]{3,2,1,0:T(4,128)S(1)}, f32[3,1,3,256]{3,2,1,0:T(4,128)S(1)}, u32[]{:S(2)}, u32[]{:S(2)}) collective-permute-start(f32[3,1,3,256]{3,2,1,0:T(4,128)S(1)} %get-tuple-element.161), channel_id=1, source_target_pairs={{8,0},{16,8},{24,16},{32,24},{40,32},{48,40},{56,48},{64,56},{72,6... | collective-permute-start | bytes 27656 | tf_op jit(solution)/shard_map/ppermute | solution.py:22
  101.1 5.7 %collective-permute-start.10 = (f32[3,5,1,256]{3,2,1,0:T(1,128)S(1)}, f32[3,5,1,256]{3,2,1,0:T(1,128)S(1)}, u32[]{:S(2)}, u32[]{:S(2)}) collective-permute-start(f32[3,5,1,256]{3,2,1,0:T(1,128)S(1)} %get-tuple-element.159), channel_id=1, source_target_pairs={{0,1},{1,2},{2,3},{3,4},{4,5},{5,6},{6,7},{7,0},{8,9},{9,10},{10,1... | collective-permute-start | bytes 46088 | tf_op jit(solution)/shard_map/ppermute | solution.py:21
  101.9 4.9 %collective-permute-start.11 = (f32[3,5,1,256]{3,2,1,0:T(1,128)S(1)}, f32[3,5,1,256]{3,2,1,0:T(1,128)S(1)}, u32[]{:S(2)}, u32[]{:S(2)}) collective-permute-start(f32[3,5,1,256]{3,2,1,0:T(1,128)S(1)} %get-tuple-element.160), channel_id=1, source_target_pairs={{1,0},{2,1},{3,2},{4,3},{5,4},{6,5},{7,6},{0,7},{9,8},{10,9},{11,1... | collective-permute-start | bytes 46088 | tf_op jit(solution)/shard_map/ppermute | solution.py:22
  151.2 8.9 %collective-permute-start.13 = (f32[3,2,36,256]{3,2,1,0:T(8,128)S(1)}, f32[3,2,36,256]{3,2,1,0:T(8,128)S(1)}, u32[]{:S(2)}, u32[]{:S(2)}) collective-permute-start(f32[3,2,36,256]{3,2,1,0:T(8,128)S(1)} %get-tuple-element.125), channel_id=1, source_target_pairs={{8,0},{16,8},{24,16},{32,24},{40,32},{48,40},{56,48},{64,56},{72,6... | collective-permute-start | bytes 663560 | tf_op jit(solution)/shard_map/ppermute | solution.py:22
  157.0 8.4 %collective-permute-start.12 = (f32[3,2,36,256]{3,2,1,0:T(8,128)S(1)}, f32[3,2,36,256]{3,2,1,0:T(8,128)S(1)}, u32[]{:S(2)}, u32[]{:S(2)}) collective-permute-start(f32[3,2,36,256]{3,2,1,0:T(8,128)S(1)} %get-tuple-element.126), channel_id=1, source_target_pairs={{0,8},{8,16},{16,24},{24,32},{32,40},{40,48},{48,56},{56,64},{64,7... | collective-permute-start | bytes 663560 | tf_op jit(solution)/shard_map/ppermute | solution.py:21
  165.5 8.4 %collective-permute-start.15 = (f32[3,24,2,256]{3,2,1,0:T(2,128)S(1)}, f32[3,24,2,256]{3,2,1,0:T(2,128)S(1)}, u32[]{:S(2)}, u32[]{:S(2)}) collective-permute-start(f32[3,24,2,256]{3,2,1,0:T(2,128)S(1)} %get-tuple-element.115), channel_id=1, source_target_pairs={{1,0},{2,1},{3,2},{4,3},{5,4},{6,5},{7,6},{0,7},{9,8},{10,9},{11,1... | collective-permute-start | bytes 442376 | tf_op jit(solution)/shard_map/ppermute | solution.py:22
  169.9 2.4 collective-permute-start.14
  185.3 7.1 %copy-start.10 = (f32[6,2]{0,1:T(2,128)S(1)}, f32[6,2]{0,1:T(2,128)}, u32[]{:S(2)}) copy-start(f32[6,2]{0,1:T(2,128)} %param.35) | copy-start | bytes 148
  187.5 42.6 %copy-start.14 = (s32[4]{0:T(128)S(1)}, s32[4]{0:T(128)}, u32[]{:S(2)}) copy-start(s32[4]{0:T(128)} %param.37) | copy-start | bytes 52
  187.5 46.8 %copy-start.12 = (f32[36]{0:T(128)S(1)}, f32[36]{0:T(128)}, u32[]{:S(2)}) copy-start(f32[36]{0:T(128)} %copy-done.11) | copy-start | bytes 436
  187.6 42.0 %collective-permute-start.16 = (f32[3,2,32,256]{3,2,1,0:T(8,128)S(1)}, f32[3,2,32,256]{3,2,1,0:T(8,128)S(1)}, u32[]{:S(2)}, u32[]{:S(2)}) collective-permute-start(f32[3,2,32,256]{3,2,1,0:T(8,128)S(1)} %get-tuple-element.143), channel_id=1, source_target_pairs={{0,8},{8,16},{16,24},{24,32},{32,40},{40,48},{48,56},{56,64},{64,7... | collective-permute-start | bytes 589832 | tf_op jit(solution)/shard_map/ppermute | solution.py:21
  187.6 41.9 %collective-permute-start.17 = (f32[3,2,32,256]{3,2,1,0:T(8,128)S(1)}, f32[3,2,32,256]{3,2,1,0:T(8,128)S(1)}, u32[]{:S(2)}, u32[]{:S(2)}) collective-permute-start(f32[3,2,32,256]{3,2,1,0:T(8,128)S(1)} %get-tuple-element.144), channel_id=1, source_target_pairs={{8,0},{16,8},{24,16},{32,24},{40,32},{48,40},{56,48},{64,56},{72,6... | collective-permute-start | bytes 589832 | tf_op jit(solution)/shard_map/ppermute | solution.py:22
  229.6 1.9 collective-permute-start.18
  229.6 4.6 %collective-permute-start.19 = (f32[3,20,2,256]{3,2,1,0:T(2,128)S(1)}, f32[3,20,2,256]{3,2,1,0:T(2,128)S(1)}, u32[]{:S(2)}, u32[]{:S(2)}) collective-permute-start(f32[3,20,2,256]{3,2,1,0:T(2,128)S(1)} %get-tuple-element.138), channel_id=1, source_target_pairs={{1,0},{2,1},{3,2},{4,3},{5,4},{6,5},{7,6},{0,7},{9,8},{10,9},{11,1... | collective-permute-start | bytes 368648 | tf_op jit(solution)/shard_map/ppermute | solution.py:22
  235.1 0.8 copy-start.13
  239.2 6.0 %copy-start.17 = (s32[4]{0:T(128)S(1)}, s32[4]{0:T(128)}, u32[]{:S(2)}) copy-start(s32[4]{0:T(128)} %broadcast_subtract_fusion) | copy-start | bytes 52
  240.2 8.8 %collective-permute-start.20 = (f32[3,2,32,256]{3,2,1,0:T(8,128)S(1)}, f32[3,2,32,256]{3,2,1,0:T(8,128)S(1)}, u32[]{:S(2)}, u32[]{:S(2)}) collective-permute-start(f32[3,2,32,256]{3,2,1,0:T(8,128)S(1)} %get-tuple-element.141), channel_id=1, source_target_pairs={{0,8},{8,16},{16,24},{24,32},{32,40},{40,48},{48,56},{56,64},{64,7... | collective-permute-start | bytes 589832 | tf_op jit(solution)/shard_map/ppermute | solution.py:21
  241.7 7.3 %collective-permute-start.21 = (f32[3,2,32,256]{3,2,1,0:T(8,128)S(1)}, f32[3,2,32,256]{3,2,1,0:T(8,128)S(1)}, u32[]{:S(2)}, u32[]{:S(2)}) collective-permute-start(f32[3,2,32,256]{3,2,1,0:T(8,128)S(1)} %get-tuple-element.142), channel_id=1, source_target_pairs={{8,0},{16,8},{24,16},{32,24},{40,32},{48,40},{56,48},{64,56},{72,6... | collective-permute-start | bytes 589832 | tf_op jit(solution)/shard_map/ppermute | solution.py:22
  249.1 3.6 %collective-permute-start.22 = (f32[3,20,2,256]{3,2,1,0:T(2,128)S(1)}, f32[3,20,2,256]{3,2,1,0:T(2,128)S(1)}, u32[]{:S(2)}, u32[]{:S(2)}) collective-permute-start(f32[3,20,2,256]{3,2,1,0:T(2,128)S(1)} %get-tuple-element.135), channel_id=1, source_target_pairs={{0,1},{1,2},{2,3},{3,4},{4,5},{5,6},{6,7},{7,0},{8,9},{9,10},{10,1... | collective-permute-start | bytes 368648 | tf_op jit(solution)/shard_map/ppermute | solution.py:21
  250.9 4.6 %collective-permute-start.23 = (f32[3,20,2,256]{3,2,1,0:T(2,128)S(1)}, f32[3,20,2,256]{3,2,1,0:T(2,128)S(1)}, u32[]{:S(2)}, u32[]{:S(2)}) collective-permute-start(f32[3,20,2,256]{3,2,1,0:T(2,128)S(1)} %get-tuple-element.136), channel_id=1, source_target_pairs={{1,0},{2,1},{3,2},{4,3},{5,4},{6,5},{7,6},{0,7},{9,8},{10,9},{11,1... | collective-permute-start | bytes 368648 | tf_op jit(solution)/shard_map/ppermute | solution.py:22
where the time goes:
time: 268 us; the launch traced here: 263 us
  matrix products  82.3 us (31%)
  starting transfers between devices  44.4 us (17%)
  other arithmetic  38.6 us (14%)
  blocking collectives  37 us (14%)
  local copies, waits for them, and re-layouts  31.5 us (12%)
  waiting for transfers between devices  27.4 us (10%)
    dot_general x1, matrix products, sample_field(): jnp.dot(field.reshape(-1, extent_z), table_z, precision=lax.Precision.HIG...  46.2 us
    ppermute x12, starting transfers between devices, with_halo(): after = lax.ppermute(leading, axis, down)  37.3 us
    all_gather x1, blocking collectives, on_device(): everyone = lax.all_gather(moved, ('gx', 'gy'), axis=1, tiled=True)  37 us
    dot_general x1, matrix products, deposit_field(): lax.dot_general(spread_xy.reshape(-1, count), table_z, (((1,), (1,)), (()...  35.6 us
    ppermute x12, waiting for transfers between devices, with_halo(): after = lax.ppermute(leading, axis, down)  13.8 us
    ppermute x12, waiting for transfers between devices, with_halo(): before = lax.ppermute(last, axis, up)  13.5 us
    ppermute x12, starting transfers between devices, with_halo(): before = lax.ppermute(last, axis, up)  7.09 us
    another operation x6, other arithmetic  6.33 us
  transfers between devices with their start and end apart: 24, of which 13 were waited for; matrix products, arithmetic and copies ran while one was open for 12% of the time, Pallas kernels for 0%

commit v1 on v0

v1 whole, which is shorter than its diff:
```python
import functools

import jax
import jax.numpy as jnp
from jax import lax
from jax.experimental import pallas as pl
from jax.experimental.pallas import tpu as pltpu
from jax.sharding import PartitionSpec as P

F32 = jnp.float32
BF16 = jnp.bfloat16
I32 = jnp.int32
MESH = pl.DeviceIdType.MESH

ITERS = 4
DIFFUSION = 1.0
RESPONSE = 0.5
DASHPOT = 0.1

TILE = 256
ROWS = 40
HALO = 4
LANES = [(dx, dy) for dx in (-1, 0, 1) for dy in (-1, 0, 1) if (dx, dy) != (0, 0)]
GROUPS = [(0, 1, 2, 17, 18, 19), (3, 4, 5, 14, 15, 16), (6, 7, 8, 9, 10, 11, 12, 13)]
RUNS = [((0, 3), (17, 3)), ((3, 3), (14, 3)), ((6, 8),)]


def split(values):
    high = values.astype(BF16)
    low = (values - high.astype(F32)).astype(BF16)
    return high, low


def pick(distance, weights):
    result = jnp.where(distance == 3, weights[3], 0.0)
    for k in (2, 1, 0):
        result = jnp.where(distance == k, weights[k], result)
    return result


def cross(a, b):
    return (
        a[1] * b[2] - a[2] * b[1],
        a[2] * b[0] - a[0] * b[2],
        a[0] * b[1] - a[1] * b[0],
    )


def kernel(
    n_gx,
    n_gy,
    v_ref,
    int_ref,
    dw_ref,
    off_ref,
    mot_ref,
    cs_ref,
    cp_ref,
    out_ref,
    nm_ref,
    hx,
    hy,
    hc,
    pay,
    pay3,
    own_sq,
    slot_b,
    snd,
    mk,
    frame,
    fhl,
    tz,
    ty_s,
    tx_s,
    sums,
    ret,
    agx,
    agy,
    ag1,
    moved_s,
    rhs,
    state_a,
    state_b,
    ybuf,
    xbuf,
    halo_send,
    halo_recv,
    pay_send,
    pay_recv,
    ret_send,
    ret_recv,
    agx_send,
    agx_recv,
    agy_send,
    agy_recv,
    y_send,
    y_recv,
    x_send,
    x_recv,
):
    gx = lax.axis_index("gx")
    gy = lax.axis_index("gy")
    here = gx * n_gy + gy
    markers = dw_ref.shape[1]
    home_tiles = markers // TILE
    tiles = home_tiles + 8
    span_x = v_ref.shape[1]
    span_y = v_ref.shape[2]
    extent_z = v_ref.shape[3]
    planes = span_x + 4

    def at(dx, dy):
        return (lax.rem(gx + (dx + n_gx), n_gx), lax.rem(gy + (dy + n_gy), n_gy))

    barrier = pltpu.get_barrier_semaphore()
    peers = (
        [at(k, 0) for k in range(1, n_gx)]
        + [at(0, k) for k in range(1, n_gy)]
        + [at(dx, dy) for dx in (-1, 1) for dy in (-1, 1)]
    )
    for peer in peers:
        pl.semaphore_signal(barrier, inc=1, device_id=peer, device_id_type=MESH)

    def remote(src, dst, send, recv, peer):
        return pltpu.make_async_remote_copy(
            src_ref=src,
            dst_ref=dst,
            send_sem=send,
            recv_sem=recv,
            device_id=peer,
            device_id_type=MESH,
        )

    pay[0:12, :] = dw_ref[...]
    pay[12:15, :] = int_ref[1:4, :].astype(F32)
    per_sphere = markers // 2
    second = (lax.broadcasted_iota(I32, (1, markers), 1) >= per_sphere).astype(F32)
    pay[15:16, :] = second
    motion = [mot_ref[c, 0] * (1.0 - second) + mot_ref[c, 1] * second for c in range(6)]
    offset = [off_ref[c : c + 1, :] for c in range(3)]
    swing = cross(motion[3:6], offset)
    for c in range(3):
        pay[16 + c : 17 + c, :] = motion[c] + swing[c]
        pay[19 + c : 20 + c, :] = offset[c]
    pay[22:32, :] = jnp.zeros((10, markers), F32)
    whole = pay[...]
    rest = whole
    for term in range(3):
        part = rest.astype(BF16)
        pay3[32 * term : 32 * term + 32, :] = part
        rest = rest - part.astype(F32)
    at_home = (int_ref[0:1, :] == here).astype(F32)
    for t in range(home_tiles):
        cols = slice(t * TILE, (t + 1) * TILE)
        here_t = at_home[:, cols]
        mk[t, 0:4, :] = pay[0:4, cols] * here_t
        mk[t, 4:16, :] = pay[4:16, cols]
        mk[t, 16:19, :] = pay[16:19, cols] * here_t
        mk[t, 19:24, :] = pay[19:24, cols]

    pl.semaphore_wait(barrier, len(peers))
    last = span_x - 2
    top = span_y - 8
    halo = []
    halo.append(remote(v_ref.at[:, 0:2], hx.at[1], halo_send.at[0], halo_recv.at[0], at(-1, 0)))
    halo.append(
        remote(v_ref.at[:, last:span_x], hx.at[0], halo_send.at[1], halo_recv.at[1], at(1, 0))
    )
    halo.append(
        remote(v_ref.at[:, :, 0:8], hy.at[1], halo_send.at[2], halo_recv.at[2], at(0, -1))
    )
    halo.append(
        remote(v_ref.at[:, :, top:span_y], hy.at[0], halo_send.at[3], halo_recv.at[3], at(0, 1))
    )
    k = 4
    for dx in (-1, 1):
        for dy in (-1, 1):
            x0 = 0 if dx < 0 else last
            y0 = 0 if dy < 0 else top
            slot = (1 if dx < 0 else 0) * 2 + (1 if dy < 0 else 0)
            halo.append(
                remote(
                    v_ref.at[:, x0 : x0 + 2, y0 : y0 + 8],
                    hc.at[slot],
                    halo_send.at[k],
                    halo_recv.at[k],
                    at(dx, dy),
                )
            )
            k += 1
    for copy in halo:
        copy.start()

    own_sq[...] = jnp.zeros_like(own_sq)
    for q in range(markers // 128):
        own_sq[q : q + 1, :] = int_ref[0:1, q * 128 : (q + 1) * 128].astype(F32)
    columns = own_sq[...].T.astype(I32)
    lane_id = lax.broadcasted_iota(I32, (TILE, 128), 1)
    lower = (
        lax.broadcasted_iota(I32, (TILE, TILE), 0) > lax.broadcasted_iota(I32, (TILE, TILE), 1)
    ).astype(BF16)
    carry = jnp.zeros((1, 128), F32)
    for q in range(home_tiles):
        owner = jnp.concatenate(
            [columns[:, 2 * q : 2 * q + 1], columns[:, 2 * q + 1 : 2 * q + 2]], axis=0
        )
        owner_x = lax.shift_right_logical(owner, n_gy.bit_length() - 1)
        owner_y = owner & (n_gy - 1)
        step_x = (owner_x - gx + 1) & (n_gx - 1)
        lane = step_x * 3 + (owner_y - gy + 1)
        lane = jnp.where(owner == here, -1, jnp.where(lane > 4, lane - 1, lane))
        hit = lane_id == lane
        hits = hit.astype(F32)
        ranked = jnp.dot(lower, hits.astype(BF16), preferred_element_type=F32) + carry
        carry = carry + jnp.sum(hits, axis=0, keepdims=True)
        wanted = jnp.sum(
            jnp.where(hit, ranked + (lane_id * TILE).astype(F32), 0.0), axis=1, keepdims=True
        )
        slot = jnp.where(lane < 0, -1, wanted.astype(I32))
        slot_b[q * TILE : (q + 1) * TILE, :] = jnp.broadcast_to(slot, (TILE, 128))

    def compact(n, _):
        slots = slot_b[...] - n * TILE
        low = (slots == lax.broadcasted_iota(I32, (markers, 128), 1)).astype(F32)
        high = (slots == lax.broadcasted_iota(I32, (markers, 128), 1) + 128).astype(F32)
        chosen = jnp.concatenate([low.astype(BF16), high.astype(BF16)], axis=1)
        moved = jnp.dot(pay3[...], chosen, preferred_element_type=F32)
        moved = moved[0:32] + moved[32:64] + moved[64:96]
        snd[n] = moved[0:24]
        return 0

    lax.fori_loop(0, 8, compact, 0)

    requests = [
        remote(snd.at[n], mk.at[home_tiles + n], pay_send.at[n], pay_recv.at[n], at(dx, dy))
        for n, (dx, dy) in enumerate(LANES)
    ]
    for copy in requests:
        copy.start()

    inner_low = jnp.where(gy > 0, 1.0, 0.0).astype(F32)
    inner_high = jnp.where(gy < n_gy - 1, 1.0, 0.0).astype(F32)

    def clear(p, _):
        frame[p] = jnp.zeros((3, ROWS, extent_z), F32)
        rhs[p] = jnp.zeros((3, ROWS, extent_z), F32)
        return 0

    lax.fori_loop(0, planes + 4, clear, 0)

    def place(x, _):
        for c in range(3):
            plane = v_ref[c, x]
            frame[x + 2, c, 4 : 4 + span_y, :] = plane
            rhs[x + 4, c, 4 : 4 + span_y, :] = plane
        return 0

    lax.fori_loop(0, span_x, place, 0)
    for copy in halo:
        copy.wait()

    def rims(x, _):
        for c in range(3):
            frame[x + 2, c, 2:4, :] = hy[0, c, x, 6:8, :] * inner_low
            frame[x + 2, c, 36:38, :] = hy[1, c, x, 0:2, :] * inner_high
        return 0

    lax.fori_loop(0, span_x, rims, 0)
    for side in range(2):
        for i in range(2):
            p = (0 if side == 0 else planes - 2) + i
            for c in range(3):
                frame[p, c, 4 : 4 + span_y, :] = hx[side, c, i]
                frame[p, c, 2:4, :] = hc[side * 2, c, i, 6:8, :] * inner_low
                frame[p, c, 36:38, :] = hc[side * 2 + 1, c, i, 0:2, :] * inner_high

    def halve(p, _):
        high, low = split(frame[p].reshape(3 * ROWS, extent_z))
        fhl[p, :, 0:extent_z] = high
        fhl[p, :, extent_z : 2 * extent_z] = low
        return 0

    lax.fori_loop(0, planes, halve, 0)

    def sample(t, _):
        @pl.when(t == home_tiles)
        def _arrivals():
            for copy in requests:
                copy.wait()

        m = mk[t]
        cell_x = m[12:13].astype(I32)
        cell_y = m[13:14].astype(I32)
        cell_z = m[14:15].astype(I32)
        z = lax.broadcasted_iota(I32, (extent_z, TILE), 0)
        table = pick((z - cell_z) & (extent_z - 1), [m[8 + i : 9 + i] for i in range(4)])
        high, low = split(table)
        tz[t, 0] = high
        tz[t, 1] = low
        y = lax.broadcasted_iota(I32, (ROWS, TILE), 0) - 2
        table_y = pick(y - cell_y, [m[4 + i : 5 + i] for i in range(4)])
        ty_s[t] = table_y
        x = lax.broadcasted_iota(I32, (24, TILE), 0)
        table_x = pick(x - cell_x, [m[i : i + 1] for i in range(4)])
        tx_s[t] = table_x
        both = fhl[...].reshape(planes * 3 * ROWS, 2 * extent_z)
        left = jnp.concatenate([both, both[:, 0:extent_z]], axis=1)
        right = jnp.concatenate([high, high, low], axis=0)
        part = jnp.dot(left, right, preferred_element_type=F32)
        part = part.reshape(planes, 3, ROWS // 8, 8, TILE)
        folded_y = table_y.reshape(ROWS // 8, 8, TILE)
        totals = []
        for c in range(3):
            total = jnp.zeros((8, TILE), F32)
            for p in range(planes):
                total = total + jnp.sum(part[p, c] * folded_y, axis=0) * table_x[p : p + 1]
            totals.append(jnp.sum(total, axis=0, keepdims=True))
        force = [m[16 + c : 17 + c] - totals[c] for c in range(3)]
        torque = cross([m[19 + c : 20 + c] for c in range(3)], force)
        for c in range(3):
            mk[t, 16 + c : 17 + c, :] = force[c]
        acting = jnp.concatenate(force + list(torque) + [jnp.zeros((2, TILE), F32)], axis=0)
        on_second = m[15:16]
        first_sum = jnp.sum(acting * (1.0 - on_second), axis=1, keepdims=True)
        second_sum = jnp.sum(acting * on_second, axis=1, keepdims=True)
        lanes = lax.broadcasted_iota(I32, (8, 128), 1)
        sums[t] = jnp.where(lanes == 0, first_sum, jnp.where(lanes == 1, second_sum, 0.0))
        return 0

    lax.fori_loop(0, tiles, sample, 0)

    replies = [
        remote(sums.at[home_tiles + n], ret.at[n], ret_send.at[n], ret_recv.at[n], at(-dx, -dy))
        for n, (dx, dy) in enumerate(LANES)
    ]
    for copy in replies:
        copy.start()

    lanes = lax.broadcasted_iota(I32, (8, 128), 1)
    row_id = lax.broadcasted_iota(I32, (8, 128), 0)

    def along_x(k):
        return remote(ag1.at[0], agx.at[k], agx_send.at[k], agx_recv.at[k], at(k, 0))

    def along_y(k):
        return remote(ag1.at[1], agy.at[k], agy_send.at[k], agy_recv.at[k], at(0, k))

    def sphere_step_one():
        for copy in replies:
            copy.wait()
        total = jnp.zeros((8, 128), F32)
        for t in range(home_tiles):
            total = total + sums[t]
        for n in range(8):
            total = total + ret[n]
        start = jnp.zeros((8, 128), F32)
        for c in range(6):
            for s in range(2):
                start = jnp.where((row_id == c) & (lanes == s), mot_ref[c, s], start)
        moved = start - total * (RESPONSE / per_sphere)
        moved_s[...] = moved
        first = jnp.broadcast_to(moved[:, 0:1], (8, 128))
        other = pltpu.roll(jnp.broadcast_to(moved[:, 1:2], (8, 128)), 3, 0)
        ag1[0] = jnp.where(lanes == here, jnp.where(row_id < 3, first, other), 0.0)
        for k in range(1, n_gx):
            along_x(k).start()

    def sphere_step_two():
        for k in range(1, n_gx):
            along_x(k).wait()
        total = ag1[0]
        for k in range(1, n_gx):
            total = total + agx[k]
        ag1[1] = total
        for k in range(1, n_gy):
            along_y(k).start()

    def sphere_step_three():
        for k in range(1, n_gy):
            along_y(k).wait()
        total = ag1[1]
        for k in range(1, n_gy):
            total = total + agy[k]
        moved = moved_s[...]
        pull = jnp.zeros((8, 128), F32)
        for k in range(cs_ref.shape[0]):
            partner = cp_ref[k]
            own = cs_ref[k] - 2 * here
            chosen = jnp.sum(
                jnp.where(lanes == lax.shift_right_logical(partner, 1), total, 0.0),
                axis=1,
                keepdims=True,
            )
            chosen = jnp.broadcast_to(chosen, (8, 128))
            odd = jnp.broadcast_to(partner & 1, (8, 128)) == 1
            chosen = jnp.where(odd, pltpu.roll(chosen, 5, 0), chosen)
            pull = pull + jnp.where((lanes == own) & (row_id < 3), chosen - moved, 0.0)
        nm_ref[...] = (moved + DASHPOT * pull)[0:6, 0:2]

    def y_copies(g):
        copies = []
        for r, (first, count) in enumerate(RUNS[g]):
            lo = first + 2
            base = 4 * g + 2 * r
            copies.append(
                remote(
                    rhs.at[pl.ds(lo, count), :, pl.ds(0, 8)],
                    ybuf.at[1, pl.ds(first, count)],
                    y_send.at[base],
                    y_recv.at[base],
                    at(0, -1),
                )
            )
            copies.append(
                remote(
                    rhs.at[pl.ds(lo, count), :, pl.ds(ROWS - 8, 8)],
                    ybuf.at[0, pl.ds(first, count)],
                    y_send.at[base + 1],
                    y_recv.at[base + 1],
                    at(0, 1),
                )
            )
        return copies

    def x_copies(g):
        low = 3 * g
        high = planes - 3 - 3 * g
        return [
            remote(
                rhs.at[pl.ds(low + 2, 3)],
                xbuf.at[1, pl.ds(low, 3)],
                x_send.at[2 * g],
                x_recv.at[2 * g],
                at(-1, 0),
            ),
            remote(
                rhs.at[pl.ds(high + 2, 3)],
                xbuf.at[0, pl.ds(3 - low, 3)],
                x_send.at[2 * g + 1],
                x_recv.at[2 * g + 1],
                at(1, 0),
            ),
        ]

    def finish_y(g):
        for copy in y_copies(g):
            copy.wait()
        for p in GROUPS[g]:
            rhs[p + 2, :, 0:8, :] = rhs[p + 2, :, 0:8, :] + ybuf[0, p] * inner_low
            rhs[p + 2, :, ROWS - 8 : ROWS, :] = (
                rhs[p + 2, :, ROWS - 8 : ROWS, :] + ybuf[1, p] * inner_high
            )

    def deposit(g, t):
        m = mk[t]
        table_y = ty_s[t]
        table_x = tx_s[t]
        rows = []
        for p in GROUPS[g]:
            strength = m[16:19] * table_x[p : p + 1]
            for c in range(3):
                rows.append(strength[c : c + 1] * table_y)
        high, low = split(jnp.concatenate(rows, axis=0))
        left = jnp.concatenate([high, low, high], axis=1)
        right = jnp.concatenate([tz[t, 0], tz[t, 0], tz[t, 1]], axis=1)
        added = lax.dot_general(
            left, right, (((1,), (1,)), ((), ())), preferred_element_type=F32
        ).reshape(len(GROUPS[g]), 3, ROWS, extent_z)
        for i, p in enumerate(GROUPS[g]):
            rhs[p + 2] = rhs[p + 2] + added[i]

    def group_zero(t, _):
        deposit(0, t)
        return 0

    lax.fori_loop(0, tiles, group_zero, 0)
    for copy in y_copies(0):
        copy.start()
    sphere_step_one()

    def group_one(t, _):
        deposit(1, t)

        @pl.when(t == 5)
        def _send():
            finish_y(0)
            for copy in x_copies(0):
                copy.start()

        return 0

    lax.fori_loop(0, tiles, group_one, 0)
    for copy in y_copies(1):
        copy.start()
    sphere_step_two()

    def group_two(t, _):
        deposit(2, t)

        @pl.when(t == 4)
        def _send():
            finish_y(1)
            for copy in x_copies(1):
                copy.start()

        return 0

    lax.fori_loop(0, tiles, group_two, 0)
    for copy in y_copies(2):
        copy.start()
    sphere_step_three()
    finish_y(2)
    for g in range(2):
        for copy in x_copies(g):
            copy.wait()

    y = lax.broadcasted_iota(I32, (ROWS, extent_z), 0)
    low_edge = jnp.where(gy > 0, 0, HALO)
    high_edge = jnp.where(gy < n_gy - 1, ROWS, HALO + span_y)
    inside = jnp.where((y >= low_edge) & (y < high_edge), 1.0, 0.0).astype(F32)
    inside = jnp.concatenate([inside] * 3, axis=0)
    scale = inside * (1.0 / (1.0 + 6.0 * DIFFUSION))
    flat = (3 * ROWS, extent_z)

    for i in range(6):
        rhs[i] = rhs[i] + xbuf[0, i]
        rhs[planes - 2 + i] = rhs[planes - 2 + i] + xbuf[1, i]

    def begin(x, _):
        state_a[x] = (rhs[x].reshape(flat) * inside).reshape(3, ROWS, extent_z)
        return 0

    lax.fori_loop(0, planes + 4, begin, 0)

    def sweep(source, x):
        centre = source[x].reshape(flat)
        total = rhs[x].reshape(flat) + source[x - 1].reshape(flat) + source[x + 1].reshape(flat)
        total = total + pltpu.roll(centre, 1, 0) + pltpu.roll(centre, 3 * ROWS - 1, 0)
        total = total + pltpu.roll(centre, 1, 1) + pltpu.roll(centre, extent_z - 1, 1)
        return total * scale

    buffers = (state_a, state_b)
    for k in range(ITERS - 1):
        source, target = buffers[k % 2], buffers[(k + 1) % 2]

        def step(x, _, source=source, target=target):
            target[x] = sweep(source, x).reshape(3, ROWS, extent_z)
            return 0

        lax.fori_loop(k + 1, planes + 3 - k, step, 0)
    source = buffers[(ITERS - 1) % 2]

    def final(x, _):
        result = sweep(source, x + HALO).reshape(3, ROWS, extent_z)
        for c in range(3):
            out_ref[c, x] = result[c, HALO : HALO + span_y, :]
        return 0

    lax.fori_loop(0, span_x, final, 0)


def on_device(n_gx, n_gy, velocity, owner_block, base_x, base_y, base_z, delta_weights, marker_offset, sphere_motion, contact_sphere, contact_partner):
    span_x, span_y, extent_z = velocity.shape[1:]
    markers = base_x.shape[0]
    ints = jnp.stack([owner_block[:, 0], base_x, base_y, base_z])
    tiles = markers // TILE + 8
    planes = span_x + 4
    vmem = pl.BlockSpec(memory_space=pltpu.VMEM)
    smem = pl.BlockSpec(memory_space=pltpu.SMEM)
    dma = pltpu.SemaphoreType.DMA
    return pl.pallas_call(
        functools.partial(kernel, n_gx, n_gy),
        out_shape=(
            jax.ShapeDtypeStruct(velocity.shape, F32),
            jax.ShapeDtypeStruct(sphere_motion.shape, F32),
        ),
        in_specs=[vmem, vmem, vmem, vmem, smem, smem, smem],
        out_specs=(vmem, vmem),
        scratch_shapes=[
            pltpu.VMEM((2, 3, 2, span_y, extent_z), F32),
            pltpu.VMEM((2, 3, span_x, 8, extent_z), F32),
            pltpu.VMEM((4, 3, 2, 8, extent_z), F32),
            pltpu.VMEM((32, markers), F32),
            pltpu.VMEM((96, markers), BF16),
            pltpu.VMEM((128, 128), F32),
            pltpu.VMEM((markers, 128), I32),
            pltpu.VMEM((8, 24, TILE), F32),
            pltpu.VMEM((tiles, 24, TILE), F32),
            pltpu.VMEM((planes + 4, 3, ROWS, extent_z), F32),
            pltpu.VMEM((planes, 3 * ROWS, 2 * extent_z), BF16),
            pltpu.VMEM((tiles, 2, extent_z, TILE), BF16),
            pltpu.VMEM((tiles, ROWS, TILE), F32),
            pltpu.VMEM((tiles, 24, TILE), F32),
            pltpu.VMEM((tiles, 8, 128), F32),
            pltpu.VMEM((8, 8, 128), F32),
            pltpu.VMEM((n_gx, 8, 128), F32),
            pltpu.VMEM((n_gy, 8, 128), F32),
            pltpu.VMEM((2, 8, 128), F32),
            pltpu.VMEM((8, 128), F32),
            pltpu.VMEM((planes + 4, 3, ROWS, extent_z), F32),
            pltpu.VMEM((planes + 4, 3, ROWS, extent_z), F32),
            pltpu.VMEM((planes + 4, 3, ROWS, extent_z), F32),
            pltpu.VMEM((2, planes, 3, 8, extent_z), F32),
            pltpu.VMEM((2, 6, 3, ROWS, extent_z), F32),
            dma((8,)),
            dma((8,)),
            dma((8,)),
            dma((8,)),
            dma((8,)),
            dma((8,)),
            dma((n_gx,)),
            dma((n_gx,)),
            dma((n_gy,)),
            dma((n_gy,)),
            dma((12,)),
            dma((12,)),
            dma((4,)),
            dma((4,)),
        ],
        compiler_params=pltpu.CompilerParams(
            collective_id=0, has_side_effects=True, vmem_limit_bytes=62 << 20
        ),
        name="substep",
    )(velocity, ints, delta_weights, marker_offset, sphere_motion, contact_sphere, contact_partner)


def solution(mesh):
    placed = (
        P(None, "gx", "gy", None),
        P(("gx", "gy"), None),
        P(("gx", "gy")),
        P(("gx", "gy")),
        P(("gx", "gy")),
        P(None, ("gx", "gy")),
        P(None, ("gx", "gy")),
        P(None, ("gx", "gy")),
        P(("gx", "gy")),
        P(("gx", "gy")),
    )
    return jax.shard_map(
        functools.partial(on_device, mesh.shape["gx"], mesh.shape["gy"]),
        mesh=mesh,
        in_specs=placed,
        out_specs=(P(None, "gx", "gy", None), P(None, ("gx", "gy"))),
        check_vma=False,
    )
```

time: 268 us -> 96.1 us (0.36); the launches traced: 263 us -> 95.5 us
  Pallas kernels: 0 us -> 88 us
  matrix products: 82.3 us -> 0 us
  starting transfers between devices: 44.4 us -> 0 us
  other arithmetic: 38.6 us -> 1.39 us
  blocking collectives: 37 us -> 0 us
  waiting for transfers between devices: 27.4 us -> 0 us
  local copies, waits for them, and re-layouts: 31.5 us -> 5.39 us
    pallas_call x0 -> x1, Pallas kernels: none -> 88 us  [on_device(): pl.pallas_call(functools.partial(kernel, n_gx, n_gy), out_shape=(jax.Shap...]
    dot_general x5 -> x0, matrix products: 82.3 us -> none  [the longest x1 46.2 us: sample_field(): jnp.dot(field.reshape(-1, extent_z), table_z, precision=lax.Precision.HIG...]
    ppermute x24 -> x0, starting transfers between devices: 44.4 us -> none  [the longest x12 37.3 us: with_halo(): after = lax.ppermute(leading, axis, down)]
    all_gather x1 -> x0, blocking collectives: 37 us -> none  [on_device(): everyone = lax.all_gather(moved, ('gx', 'gy'), axis=1, tiled=True)]
    ppermute x24 -> x0, waiting for transfers between devices: 27.4 us -> none  [the longest x12 13.8 us: with_halo(): after = lax.ppermute(leading, axis, down)]
    slice x28 -> x0, local copies, waits for them, and re-layouts: 12 us -> none  [the longest x8 4.37 us: relax(): beside_all = beside_all + jnp.roll(center, -1, 3) + jnp.roll(center, 1, 3)]
    scatter-add x7 -> x0, other arithmetic: 9.96 us -> none  [the longest x1 1.7 us: on_device(): source.at[:, :, span_y - 2:].add(upper * rims[:, 4:span_x + 4, span_y + 6:])]
    mul x8 -> x0, other arithmetic: 7.07 us -> none  [the longest x3 5.28 us: on_device(): middle * wall_mask(row_index, row_count, span_y, 1)[None, None, :, None]]
  transfers between devices with their start and end apart: 24 -> 0, of which waited for: 13 -> 0; matrix products, arithmetic and copies ran while one was open for 12% -> 0% of each run, Pallas kernels for 0% -> 0%
where the time goes in v1:
time: 96.1 us; the launch traced here: 95.5 us
  Pallas kernels  88 us (92%)
  local copies, waits for them, and re-layouts  5.39 us (6%)
  other arithmetic  1.39 us (1%)
    pallas_call x1, Pallas kernels, on_device(): pl.pallas_call(functools.partial(kernel, n_gx, n_gy), out_shape=(jax.Shap...  88 us
    unnamed x2, local copies, waits for them, and re-layouts  4.08 us

profile of v1, /device:TPU:1, one launch (start us, length us, event | category | flops | bytes accessed | tf_op | source)
XLA Modules:
  0.0 95.5 jit_solution(6642727277981770340)
XLA Ops:
  0.6 1.4 %copy.12.mot_ref = f32[6,2]{1,0:T(8,128)} copy(f32[6,2]{0,1:T(2,128)} %param.17) | data formatting | bytes 96 | tf_op args[7]
  2.0 1.4 %pad_add_fusion.int_ref = s32[4,2048]{1,0:T(4,128)} fusion(s32[1,2048]{1,0:T(1,128)} %bitcast.4, s32[1,2048]{1,0:T(1,128)} %bitcast.5, s32[1,2048]{1,0:T(1,128)} %bitcast.6, s32[1,2048]{1,0:T(1,128)} %bitcast.7), kind=kLoop, calls=%fused_computation | loop fusion | flops 24576 | bytes 65536 | tf_op jit(solution)/shard_map/stack | solution.py:565
  3.4 88.0 %substep.1 = (f32[3,16,32,256]{3,2,1,0:T(8,128)}, f32[6,2]{1,0:T(8,128)}) custom-call(f32[3,16,32,256]{3,2,1,0:T(8,128)} %v_ref.1, s32[4,2048]{1,0:T(4,128)} %pad_add_fusion.int_ref, f32[12,2048]{1,0:T(8,128)} %dw_ref.1, f32[3,2048]{1,0:T(4,128)} %off_ref.1, f32[6,2]{1,0:T(8,128)} %copy.12.mot_ref, s32[4]{0:T(128)} %cs_ref.1, s32[4]{0:T(128)} %cp_ref.1), custom_call_target="tpu_custom_call" | custom-call | tf_op jit(solution)/shard_map/substep/pallas_call | solution.py:571
  91.4 1.3 %copy.13 = f32[6,2]{0,1:T(2,128)} copy(f32[6,2]{1,0:T(8,128)} %get-tuple-element.3) | data formatting | bytes 96 | tf_op jit(solution)/shard_map/substep/pallas_call | solution.py:571
  92.7 2.7 %copy.15 = f32[3,16,32,256]{3,2,1,0:T(8,128)} copy(f32[3,16,32,256]{3,2,1,0:T(8,128)} %get-tuple-element.6) | data formatting | bytes 3145728

commit v2 on v1

--- a/solution.py
+++ b/solution.py
@@ -18,6 +18,7 @@
 DASHPOT = 0.1
 
 TILE = 256
+UNROLL = 4
 ROWS = 40
 HALO = 4
 LANES = [(dx, dy) for dx in (-1, 0, 1) for dy in (-1, 0, 1) if (dx, dy) != (0, 0)]
@@ -50,13 +51,16 @@
     n_gx,
     n_gy,
     v_ref,
-    int_ref,
+    own_ref,
+    bx_ref,
+    by_ref,
+    bz_ref,
     dw_ref,
     off_ref,
     mot_ref,
     cs_ref,
     cp_ref,
-    out_ref,
+    rhs,
     nm_ref,
     hx,
     hy,
@@ -78,9 +82,6 @@
     agy,
     ag1,
     moved_s,
-    rhs,
-    state_a,
-    state_b,
     ybuf,
     xbuf,
     halo_send,
@@ -132,11 +133,13 @@
         )
 
     pay[0:12, :] = dw_ref[...]
-    pay[12:15, :] = int_ref[1:4, :].astype(F32)
+    pay[12:13, :] = bx_ref[...].astype(F32)
+    pay[13:14, :] = by_ref[...].astype(F32)
+    pay[14:15, :] = bz_ref[...].astype(F32)
     per_sphere = markers // 2
     second = (lax.broadcasted_iota(I32, (1, markers), 1) >= per_sphere).astype(F32)
     pay[15:16, :] = second
-    motion = [mot_ref[c, 0] * (1.0 - second) + mot_ref[c, 1] * second for c in range(6)]
+    motion = [mot_ref[0, c] * (1.0 - second) + mot_ref[1, c] * second for c in range(6)]
     offset = [off_ref[c : c + 1, :] for c in range(3)]
     swing = cross(motion[3:6], offset)
     for c in range(3):
@@ -149,7 +152,7 @@
         part = rest.astype(BF16)
         pay3[32 * term : 32 * term + 32, :] = part
         rest = rest - part.astype(F32)
-    at_home = (int_ref[0:1, :] == here).astype(F32)
+    at_home = (own_ref[...] == here).astype(F32)
     for t in range(home_tiles):
         cols = slice(t * TILE, (t + 1) * TILE)
         here_t = at_home[:, cols]
@@ -193,7 +196,7 @@
 
     own_sq[...] = jnp.zeros_like(own_sq)
     for q in range(markers // 128):
-        own_sq[q : q + 1, :] = int_ref[0:1, q * 128 : (q + 1) * 128].astype(F32)
+        own_sq[q : q + 1, :] = own_ref[:, q * 128 : (q + 1) * 128].astype(F32)
     columns = own_sq[...].T.astype(I32)
     lane_id = lax.broadcasted_iota(I32, (TILE, 128), 1)
     lower = (
@@ -282,12 +285,7 @@
 
     lax.fori_loop(0, planes, halve, 0)
 
-    def sample(t, _):
-        @pl.when(t == home_tiles)
-        def _arrivals():
-            for copy in requests:
-                copy.wait()
-
+    def sample(t):
         m = mk[t]
         cell_x = m[12:13].astype(I32)
         cell_y = m[13:14].astype(I32)
@@ -325,9 +323,18 @@
         second_sum = jnp.sum(acting * on_second, axis=1, keepdims=True)
         lanes = lax.broadcasted_iota(I32, (8, 128), 1)
         sums[t] = jnp.where(lanes == 0, first_sum, jnp.where(lanes == 1, second_sum, 0.0))
-        return 0
-
-    lax.fori_loop(0, tiles, sample, 0)
+
+    def sample_some(step, _):
+        @pl.when(step == home_tiles // UNROLL)
+        def _arrivals():
+            for copy in requests:
+                copy.wait()
+
+        for u in range(UNROLL):
+            sample(step * UNROLL + u)
+        return 0
+
+    lax.fori_loop(0, tiles // UNROLL, sample_some, 0)
 
     replies = [
         remote(sums.at[home_tiles + n], ret.at[n], ret_send.at[n], ret_recv.at[n], at(-dx, -dy))
@@ -356,7 +363,7 @@
         start = jnp.zeros((8, 128), F32)
         for c in range(6):
             for s in range(2):
-                start = jnp.where((row_id == c) & (lanes == s), mot_ref[c, s], start)
+                start = jnp.where((row_id == c) & (lanes == s), mot_ref[s, c], start)
         moved = start - total * (RESPONSE / per_sphere)
         moved_s[...] = moved
         first = jnp.broadcast_to(moved[:, 0:1], (8, 128))
@@ -395,7 +402,10 @@
             odd = jnp.broadcast_to(partner & 1, (8, 128)) == 1
             chosen = jnp.where(odd, pltpu.roll(chosen, 5, 0), chosen)
             pull = pull + jnp.where((lanes == own) & (row_id < 3), chosen - moved, 0.0)
-        nm_ref[...] = (moved + DASHPOT * pull)[0:6, 0:2]
+        settled = jnp.concatenate(
+            [moved + DASHPOT * pull, jnp.zeros((120, 128), F32)], axis=0
+        )
+        nm_ref[...] = settled.T[0:2, 0:6]
 
     def y_copies(g):
         copies = []
@@ -451,21 +461,26 @@
                 rhs[p + 2, :, ROWS - 8 : ROWS, :] + ybuf[1, p] * inner_high
             )
 
-    def deposit(g, t):
-        m = mk[t]
-        table_y = ty_s[t]
-        table_x = tx_s[t]
-        rows = []
-        for p in GROUPS[g]:
-            strength = m[16:19] * table_x[p : p + 1]
-            for c in range(3):
-                rows.append(strength[c : c + 1] * table_y)
-        high, low = split(jnp.concatenate(rows, axis=0))
-        left = jnp.concatenate([high, low, high], axis=1)
-        right = jnp.concatenate([tz[t, 0], tz[t, 0], tz[t, 1]], axis=1)
-        added = lax.dot_general(
-            left, right, (((1,), (1,)), ((), ())), preferred_element_type=F32
-        ).reshape(len(GROUPS[g]), 3, ROWS, extent_z)
+    def deposit(g, step):
+        added = None
+        for u in range(UNROLL):
+            t = step * UNROLL + u
+            m = mk[t]
+            table_y = ty_s[t]
+            table_x = tx_s[t]
+            rows = []
+            for p in GROUPS[g]:
+                strength = m[16:19] * table_x[p : p + 1]
+                for c in range(3):
+                    rows.append(strength[c : c + 1] * table_y)
+            high, low = split(jnp.concatenate(rows, axis=0))
+            left = jnp.concatenate([high, low, high], axis=1)
+            right = jnp.concatenate([tz[t, 0], tz[t, 0], tz[t, 1]], axis=1)
+            part = lax.dot_general(
+                left, right, (((1,), (1,)), ((), ())), preferred_element_type=F32
+            )
+            added = part if added is None else added + part
+        added = added.reshape(len(GROUPS[g]), 3, ROWS, extent_z)
         for i, p in enumerate(GROUPS[g]):
             rhs[p + 2] = rhs[p + 2] + added[i]
 
@@ -473,7 +488,7 @@
         deposit(0, t)
         return 0
 
-    lax.fori_loop(0, tiles, group_zero, 0)
+    lax.fori_loop(0, tiles // UNROLL, group_zero, 0)
     for copy in y_copies(0):
         copy.start()
     sphere_step_one()
@@ -481,7 +496,7 @@
     def group_one(t, _):
         deposit(1, t)
 
-        @pl.when(t == 5)
+        @pl.when(t == 1)
         def _send():
             finish_y(0)
             for copy in x_copies(0):
@@ -489,7 +504,7 @@
 
         return 0
 
-    lax.fori_loop(0, tiles, group_one, 0)
+    lax.fori_loop(0, tiles // UNROLL, group_one, 0)
     for copy in y_copies(1):
         copy.start()
     sphere_step_two()
@@ -497,7 +512,7 @@
     def group_two(t, _):
         deposit(2, t)
 
-        @pl.when(t == 4)
+        @pl.when(t == 1)
         def _send():
             finish_y(1)
             for copy in x_copies(1):
@@ -505,7 +520,7 @@
 
         return 0
 
-    lax.fori_loop(0, tiles, group_two, 0)
+    lax.fori_loop(0, tiles // UNROLL, group_two, 0)
     for copy in y_copies(2):
         copy.start()
     sphere_step_three()
@@ -514,6 +529,17 @@
         for copy in x_copies(g):
             copy.wait()
 
+    for i in range(6):
+        rhs[i] = rhs[i] + xbuf[0, i]
+        rhs[planes - 2 + i] = rhs[planes - 2 + i] + xbuf[1, i]
+
+
+def relax_kernel(n_gy, rhs, out_ref, state_a, state_b, staged, sems):
+    gy = lax.axis_index("gy")
+    extent_z = rhs.shape[3]
+    planes = rhs.shape[0] - 4
+    span_x = planes - 4
+    span_y = out_ref.shape[2]
     y = lax.broadcasted_iota(I32, (ROWS, extent_z), 0)
     low_edge = jnp.where(gy > 0, 0, HALO)
     high_edge = jnp.where(gy < n_gy - 1, ROWS, HALO + span_y)
@@ -522,10 +548,6 @@
     scale = inside * (1.0 / (1.0 + 6.0 * DIFFUSION))
     flat = (3 * ROWS, extent_z)
 
-    for i in range(6):
-        rhs[i] = rhs[i] + xbuf[0, i]
-        rhs[planes - 2 + i] = rhs[planes - 2 + i] + xbuf[1, i]
-
     def begin(x, _):
         state_a[x] = (rhs[x].reshape(flat) * inside).reshape(3, ROWS, extent_z)
         return 0
@@ -543,38 +565,49 @@
     for k in range(ITERS - 1):
         source, target = buffers[k % 2], buffers[(k + 1) % 2]
 
-        def step(x, _, source=source, target=target):
-            target[x] = sweep(source, x).reshape(3, ROWS, extent_z)
+        def step(s, _, source=source, target=target, first=k + 1):
+            for u in range(2):
+                x = first + 2 * s + u
+                target[x] = sweep(source, x).reshape(3, ROWS, extent_z)
             return 0
 
-        lax.fori_loop(k + 1, planes + 3 - k, step, 0)
+        lax.fori_loop(0, (planes + 2 - 2 * k) // 2, step, 0)
     source = buffers[(ITERS - 1) % 2]
 
-    def final(x, _):
-        result = sweep(source, x + HALO).reshape(3, ROWS, extent_z)
-        for c in range(3):
-            out_ref[c, x] = result[c, HALO : HALO + span_y, :]
-        return 0
-
-    lax.fori_loop(0, span_x, final, 0)
+    def store(s):
+        return pltpu.make_async_copy(
+            staged.at[:, pl.ds(2 * s, 2)], out_ref.at[:, pl.ds(2 * s, 2)], sems.at[s]
+        )
+
+    def final(s, _):
+        for u in range(2):
+            x = 2 * s + u
+            result = sweep(source, x + HALO).reshape(3, ROWS, extent_z)
+            for c in range(3):
+                staged[c, x] = result[c, HALO : HALO + span_y, :]
+        store(s).start()
+        return 0
+
+    lax.fori_loop(0, span_x // 2, final, 0)
+    for s in range(span_x // 2):
+        store(s).wait()
 
 
 def on_device(n_gx, n_gy, velocity, owner_block, base_x, base_y, base_z, delta_weights, marker_offset, sphere_motion, contact_sphere, contact_partner):
     span_x, span_y, extent_z = velocity.shape[1:]
     markers = base_x.shape[0]
-    ints = jnp.stack([owner_block[:, 0], base_x, base_y, base_z])
     tiles = markers // TILE + 8
     planes = span_x + 4
     vmem = pl.BlockSpec(memory_space=pltpu.VMEM)
     smem = pl.BlockSpec(memory_space=pltpu.SMEM)
     dma = pltpu.SemaphoreType.DMA
-    return pl.pallas_call(
+    rhs, new_motion = pl.pallas_call(
         functools.partial(kernel, n_gx, n_gy),
         out_shape=(
-            jax.ShapeDtypeStruct(velocity.shape, F32),
-            jax.ShapeDtypeStruct(sphere_motion.shape, F32),
+            jax.ShapeDtypeStruct((planes + 4, 3, ROWS, extent_z), F32),
+            jax.ShapeDtypeStruct(sphere_motion.shape[::-1], F32),
         ),
-        in_specs=[vmem, vmem, vmem, vmem, smem, smem, smem],
+        in_specs=[vmem] * 7 + [smem] * 3,
         out_specs=(vmem, vmem),
         scratch_shapes=[
             pltpu.VMEM((2, 3, 2, span_y, extent_z), F32),
@@ -597,9 +630,6 @@
             pltpu.VMEM((n_gy, 8, 128), F32),
             pltpu.VMEM((2, 8, 128), F32),
             pltpu.VMEM((8, 128), F32),
-            pltpu.VMEM((planes + 4, 3, ROWS, extent_z), F32),
-            pltpu.VMEM((planes + 4, 3, ROWS, extent_z), F32),
-            pltpu.VMEM((planes + 4, 3, ROWS, extent_z), F32),
             pltpu.VMEM((2, planes, 3, 8, extent_z), F32),
             pltpu.VMEM((2, 6, 3, ROWS, extent_z), F32),
             dma((8,)),
@@ -618,10 +648,36 @@
             dma((4,)),
         ],
         compiler_params=pltpu.CompilerParams(
-            collective_id=0, has_side_effects=True, vmem_limit_bytes=62 << 20
+            collective_id=0, has_side_effects=True, vmem_limit_bytes=44 << 20
         ),
         name="substep",
-    )(velocity, ints, delta_weights, marker_offset, sphere_motion, contact_sphere, contact_partner)
+    )(
+        velocity,
+        owner_block.reshape(1, markers),
+        base_x.reshape(1, markers),
+        base_y.reshape(1, markers),
+        base_z.reshape(1, markers),
+        delta_weights,
+        marker_offset,
+        sphere_motion.T,
+        contact_sphere,
+        contact_partner,
+    )
+    relaxed = pl.pallas_call(
+        functools.partial(relax_kernel, n_gy),
+        out_shape=jax.ShapeDtypeStruct(velocity.shape, F32),
+        in_specs=[vmem],
+        out_specs=pl.BlockSpec(memory_space=pl.ANY),
+        scratch_shapes=[
+            pltpu.VMEM((planes + 4, 3, ROWS, extent_z), F32),
+            pltpu.VMEM((planes + 4, 3, ROWS, extent_z), F32),
+            pltpu.VMEM(velocity.shape, F32),
+            dma((span_x // 2,)),
+        ],
+        compiler_params=pltpu.CompilerParams(vmem_limit_bytes=20 << 20),
+        name="relax",
+    )(rhs)
+    return relaxed, new_motion.T
 
 
 def solution(mesh):

time: 96.1 us -> 86.1 us (0.90)
  Pallas kernels: 88 us -> 75.9 us
  local copies, waits for them, and re-layouts: 5.39 us -> 8.4 us
  other arithmetic: 1.39 us -> 0 us
    pallas_call x1, Pallas kernels: 88 us -> 66.5 us  [on_device(): pl.pallas_call(functools.partial(kernel, n_gx, n_gy), out_shape=(jax.Shap...]
    pallas_call x0 -> x1, Pallas kernels: none -> 9.46 us  [on_device(): pl.pallas_call(functools.partial(relax_kernel, n_gy), out_shape=jax.Shape...]
    unnamed x2 -> x21, local copies, waits for them, and re-layouts: 4.08 us -> 8.4 us
    another operation x1 -> x0, other arithmetic: 1.39 us -> none  [on_device(): ints = jnp.stack([owner_block[:, 0], base_x, base_y, base_z])]
    pallas_call x1 -> x0, local copies, waits for them, and re-layouts: 1.31 us -> none  [on_device(): pl.pallas_call(functools.partial(kernel, n_gx, n_gy), out_shape=(jax.Shap...]
where the time goes in v2:
time: 86.1 us; the launch traced here: 85 us
  Pallas kernels  75.9 us (88%)
  local copies, waits for them, and re-layouts  8.4 us (10%)
    pallas_call x1, Pallas kernels, on_device(): pl.pallas_call(functools.partial(kernel, n_gx, n_gy), out_shape=(jax.Shap...  66.5 us
    pallas_call x1, Pallas kernels, on_device(): pl.pallas_call(functools.partial(relax_kernel, n_gy), out_shape=jax.Shape...  9.46 us
    unnamed x21, local copies, waits for them, and re-layouts  8.4 us

profile of v2, /device:TPU:1, one launch (start us, length us, event | category | flops | bytes accessed | tf_op | source)
XLA Modules:
  0.0 85.0 jit_solution(15776545640439382147)
XLA Ops:
  0.6 0.0 copy-start
  0.6 1.4 %copy-done = f32[3,16,32,256]{3,2,1,0:T(8,128)S(1)} copy-done((f32[3,16,32,256]{3,2,1,0:T(8,128)S(1)}, f32[3,16,32,256]{3,2,1,0:T(8,128)}, u32[]{:S(2)}) %copy-start) | copy-done | bytes 1572888
  2.0 0.0 copy-start.1
  2.0 0.9 %copy-done.1 = f32[12,2048]{1,0:T(8,128)S(1)} copy-done((f32[12,2048]{1,0:T(8,128)S(1)}, f32[12,2048]{1,0:T(8,128)}, u32[]{:S(2)}) %copy-start.1) | copy-done | bytes 98328
  2.9 0.0 copy-start.2
  2.9 0.8 copy-done.2
  3.7 0.0 copy-start.3
  3.7 0.7 copy-done.3
  4.4 0.0 copy-start.4
  4.4 0.7 copy-done.4
  5.1 0.0 copy-start.5
  5.1 0.7 copy-done.5
  5.8 0.0 copy-start.6
  5.8 0.7 copy-done.6
  6.5 0.0 copy-start.7
  6.5 0.7 copy-done.7
  7.2 0.0 copy-start.8
  7.2 0.7 copy-done.8
  7.8 0.0 copy-start.9
  7.8 0.7 copy-done.9
  8.5 66.5 %substep.1 = (f32[24,3,40,256]{3,2,1,0:T(8,128)S(1)}, f32[2,6]{1,0:T(2,128)S(1)}) custom-call(f32[3,16,32,256]{3,2,1,0:T(8,128)S(1)} %copy-done, s32[1,2048]{1,0:T(1,128)S(1)} %bitcast.6, s32[1,2048]{1,0:T(1,128)S(1)} %bitcast.7, s32[1,2048]{1,0:T(1,128)S(1)} %bitcast.8, s32[1,2048]{1,0:T(1,128)S(1)} %bitcast.9, f32[12,2048]{1,0:T(8,128)S(1)} %copy-done.1, ...), custom_call_target="tpu_custom_call" | custom-call | tf_op jit(solution)/shard_map/substep/pallas_call | solution.py:604
  75.0 9.5 %relax.1 = f32[3,16,32,256]{3,2,1,0:T(8,128)} custom-call(f32[24,3,40,256]{3,2,1,0:T(8,128)S(1)} %get-tuple-element.4.rhs), custom_call_target="tpu_custom_call" | custom-call | tf_op jit(solution)/shard_map/relax/pallas_call | solution.py:666
  84.4 0.6 copy.13
Async XLA Ops:
  0.6 1.4 %copy-start = (f32[3,16,32,256]{3,2,1,0:T(8,128)S(1)}, f32[3,16,32,256]{3,2,1,0:T(8,128)}, u32[]{:S(2)}) copy-start(f32[3,16,32,256]{3,2,1,0:T(8,128)} %v_ref.1) | copy-start | bytes 4718596
  2.0 0.9 %copy-start.1 = (f32[12,2048]{1,0:T(8,128)S(1)}, f32[12,2048]{1,0:T(8,128)}, u32[]{:S(2)}) copy-start(f32[12,2048]{1,0:T(8,128)} %dw_ref.1) | copy-start | bytes 294916
  2.9 0.8 copy-start.2
  3.7 0.7 copy-start.3
  4.4 0.7 copy-start.4
  5.1 0.7 copy-start.5
  5.8 0.7 copy-start.6
  6.5 0.7 copy-start.7
  7.2 0.7 copy-start.8
  7.8 0.7 copy-start.9

commit v3 on v2

v3 whole, which is shorter than its diff:
```python
import functools

import jax
import jax.numpy as jnp
from jax import lax
from jax.experimental import pallas as pl
from jax.experimental.pallas import tpu as pltpu
from jax.sharding import PartitionSpec as P

F32 = jnp.float32
BF16 = jnp.bfloat16
I32 = jnp.int32
MESH = pl.DeviceIdType.MESH

ITERS = 4
DIFFUSION = 1.0
RESPONSE = 0.5
DASHPOT = 0.1

TILE = 256
BINS = 32
WINDOW = 6
ROWS = 40
HALO = 4
LANES = [(dx, dy) for dx in (-1, 0, 1) for dy in (-1, 0, 1) if (dx, dy) != (0, 0)]
RUNS = [((0, 3), (17, 3)), ((3, 3), (14, 3)), ((6, 8),)]


def split(values):
    high = values.astype(BF16)
    low = (values - high.astype(F32)).astype(BF16)
    return high, low


def pick(distance, weights):
    result = jnp.where(distance == 3, weights[3], 0.0)
    for k in (2, 1, 0):
        result = jnp.where(distance == k, weights[k], result)
    return result


def cross(a, b):
    return (
        a[1] * b[2] - a[2] * b[1],
        a[2] * b[0] - a[0] * b[2],
        a[0] * b[1] - a[1] * b[0],
    )


def remote(src, dst, send, recv, peer):
    return pltpu.make_async_remote_copy(
        src_ref=src,
        dst_ref=dst,
        send_sem=send,
        recv_sem=recv,
        device_id=peer,
        device_id_type=MESH,
    )


def greet(peers):
    barrier = pltpu.get_barrier_semaphore()
    for peer in peers:
        pl.semaphore_signal(barrier, inc=1, device_id=peer, device_id_type=MESH)
    return barrier


def neighbours(n_gx, n_gy):
    gx = lax.axis_index("gx")
    gy = lax.axis_index("gy")

    def at(dx, dy):
        return (lax.rem(gx + (dx + n_gx), n_gx), lax.rem(gy + (dy + n_gy), n_gy))

    return gx, gy, at


def terms(values):
    parts = []
    rest = values
    for _ in range(3):
        part = rest.astype(BF16)
        parts.append(part)
        rest = rest - part.astype(F32)
    return jnp.concatenate(parts, axis=0)


def chosen_columns(parts, slots, first):
    wanted = lax.broadcasted_iota(I32, (TILE, TILE), 0).astype(F32) + first
    hit = jnp.where(wanted == slots, 1.0, 0.0).astype(BF16)
    return lax.dot_general(parts, hit, (((1,), (1,)), ((), ())), preferred_element_type=F32)


def ranks(hits, above):
    return jnp.dot(hits.astype(BF16), above, preferred_element_type=F32)


def strictly_above(size):
    return (
        lax.broadcasted_iota(I32, (size, size), 0) < lax.broadcasted_iota(I32, (size, size), 1)
    ).astype(BF16)


def request_kernel(
    n_gx,
    n_gy,
    v_hbm,
    own_hbm,
    bx_hbm,
    by_hbm,
    bz_hbm,
    dw_hbm,
    off_hbm,
    mot_hbm,
    fhl,
    rhs,
    home,
    arrived,
    v_ref,
    own_ref,
    bx_ref,
    by_ref,
    bz_ref,
    dw_ref,
    off_ref,
    mot_ref,
    hx,
    hy,
    hc,
    pay,
    pay3,
    slot_s,
    snd,
    inbox,
    frame,
    in_sem,
    halo_send,
    halo_recv,
    pay_send,
    pay_recv,
):
    gx, gy, at = neighbours(n_gx, n_gy)
    here = gx * n_gy + gy
    barrier = greet([at(dx, dy) for dx, dy in LANES])
    loads = [
        pltpu.make_async_copy(src, dst, in_sem.at[i])
        for i, (src, dst) in enumerate(
            (
                (v_hbm, v_ref),
                (own_hbm, own_ref),
                (bx_hbm, bx_ref),
                (by_hbm, by_ref),
                (bz_hbm, bz_ref),
                (dw_hbm, dw_ref),
                (off_hbm, off_ref),
                (mot_hbm, mot_ref),
            )
        )
    ]
    for copy in loads:
        copy.start()
    markers = dw_ref.shape[1]
    chunks = markers // TILE
    span_x = v_ref.shape[1]
    span_y = v_ref.shape[2]
    extent_z = v_ref.shape[3]
    planes = span_x + 4
    for copy in loads:
        copy.wait()

    pl.semaphore_wait(barrier, len(LANES))
    last = span_x - 2
    top = span_y - 8
    halo = []
    halo.append(remote(v_ref.at[:, 0:2], hx.at[1], halo_send.at[0], halo_recv.at[0], at(-1, 0)))
    halo.append(
        remote(v_ref.at[:, last:span_x], hx.at[0], halo_send.at[1], halo_recv.at[1], at(1, 0))
    )
    halo.append(
        remote(v_ref.at[:, :, 0:8], hy.at[1], halo_send.at[2], halo_recv.at[2], at(0, -1))
    )
    halo.append(
        remote(v_ref.at[:, :, top:span_y], hy.at[0], halo_send.at[3], halo_recv.at[3], at(0, 1))
    )
    k = 4
    for dx in (-1, 1):
        for dy in (-1, 1):
            x0 = 0 if dx < 0 else last
            y0 = 0 if dy < 0 else top
            slot = (1 if dx < 0 else 0) * 2 + (1 if dy < 0 else 0)
            halo.append(
                remote(
                    v_ref.at[:, x0 : x0 + 2, y0 : y0 + 8],
                    hc.at[slot],
                    halo_send.at[k],
                    halo_recv.at[k],
                    at(dx, dy),
                )
            )
            k += 1
    for copy in halo:
        copy.start()

    pay[0:12, :] = dw_ref[...]
    pay[12:13, :] = bx_ref[...].astype(F32)
    pay[13:14, :] = by_ref[...].astype(F32)
    pay[14:15, :] = bz_ref[...].astype(F32)
    per_sphere = markers // 2
    second = (lax.broadcasted_iota(I32, (1, markers), 1) >= per_sphere).astype(F32)
    pay[15:16, :] = second
    motion = [mot_ref[0, c] * (1.0 - second) + mot_ref[1, c] * second for c in range(6)]
    offset = [off_ref[c : c + 1, :] for c in range(3)]
    swing = cross(motion[3:6], offset)
    for c in range(3):
        pay[16 + c : 17 + c, :] = motion[c] + swing[c]
        pay[19 + c : 20 + c, :] = offset[c]
    pay[22:23, :] = jnp.ones((1, markers), F32)
    pay[23:32, :] = jnp.zeros((9, markers), F32)
    whole = pay[...]
    pay3[...] = terms(whole)
    home[...] = whole
    home[22:23, :] = (own_ref[...] == here).astype(F32)

    above = strictly_above(TILE)
    bins = lax.broadcasted_iota(I32, (8, TILE), 0)
    carry = jnp.zeros((8, 1), F32)
    for q in range(chunks):
        owner = own_ref[:, q * TILE : (q + 1) * TILE]
        owner_x = lax.shift_right_logical(owner, n_gy.bit_length() - 1)
        owner_y = owner & (n_gy - 1)
        step_x = (owner_x - gx + 1) & (n_gx - 1)
        lane = step_x * 3 + (owner_y - gy + 1)
        lane = jnp.where(owner == here, -1, jnp.where(lane > 4, lane - 1, lane))
        hits = jnp.where(bins == lane, 1.0, 0.0)
        ranked = ranks(hits, above) + carry + bins.astype(F32) * TILE
        carry = carry + jnp.sum(hits, axis=1, keepdims=True)
        slot = jnp.sum(hits * ranked, axis=0, keepdims=True)
        slot_s[q : q + 1, :] = jnp.where(lane < 0, -1.0, slot)

    def compact(n, _):
        first = (n * TILE).astype(F32)
        moved = None
        for q in range(chunks):
            part = chosen_columns(
                pay3[:, q * TILE : (q + 1) * TILE], slot_s[q : q + 1, :], first
            )
            moved = part if moved is None else moved + part
        snd[n] = moved[0:24] + moved[32:56] + moved[64:88]
        return 0

    lax.fori_loop(0, 8, compact, 0)

    requests = [
        remote(snd.at[n], inbox.at[n], pay_send.at[n], pay_recv.at[n], at(dx, dy))
        for n, (dx, dy) in enumerate(LANES)
    ]
    for copy in requests:
        copy.start()

    inner_low = jnp.where(gy > 0, 1.0, 0.0).astype(F32)
    inner_high = jnp.where(gy < n_gy - 1, 1.0, 0.0).astype(F32)

    def clear(p, _):
        rhs[p] = jnp.zeros((3, ROWS, extent_z), F32)
        return 0

    lax.fori_loop(0, rhs.shape[0], clear, 0)

    def clear_frame(p, _):
        frame[p] = jnp.zeros((3, ROWS, extent_z), F32)
        return 0

    lax.fori_loop(0, planes, clear_frame, 0)

    def clear_beyond(p, _):
        fhl[p] = jnp.zeros((3 * ROWS, 2 * extent_z), BF16)
        return 0

    lax.fori_loop(planes, fhl.shape[0], clear_beyond, 0)

    def place(x, _):
        for c in range(3):
            plane = v_ref[c, x]
            frame[x + 2, c, 4 : 4 + span_y, :] = plane
            rhs[x + 4, c, 4 : 4 + span_y, :] = plane
        return 0

    lax.fori_loop(0, span_x, place, 0)
    for copy in halo:
        copy.wait()

    def rims(x, _):
        for c in range(3):
            frame[x + 2, c, 2:4, :] = hy[0, c, x, 6:8, :] * inner_low
            frame[x + 2, c, 36:38, :] = hy[1, c, x, 0:2, :] * inner_high
        return 0

    lax.fori_loop(0, span_x, rims, 0)
    for side in range(2):
        for i in range(2):
            p = (0 if side == 0 else planes - 2) + i
            for c in range(3):
                frame[p, c, 4 : 4 + span_y, :] = hx[side, c, i]
                frame[p, c, 2:4, :] = hc[side * 2, c, i, 6:8, :] * inner_low
                frame[p, c, 36:38, :] = hc[side * 2 + 1, c, i, 0:2, :] * inner_high

    def halve(p, _):
        high, low = split(frame[p].reshape(3 * ROWS, extent_z))
        fhl[p, :, 0:extent_z] = high
        fhl[p, :, extent_z : 2 * extent_z] = low
        return 0

    lax.fori_loop(0, planes, halve, 0)
    for copy in requests:
        copy.wait()
    arrived[...] = inbox[...]


def marker_kernel(
    fhl, rhs_in, home, arrived, rhs, acted, pay3, hit_s, rank_s, slot_s, tz
):
    chunks = home.shape[1] // TILE
    every = chunks + 8
    extent_z = rhs.shape[3]
    bins = lax.broadcasted_iota(I32, (BINS, TILE), 0).astype(F32)

    def chunk(q):
        return home[0:24, q * TILE : (q + 1) * TILE] if q < chunks else arrived[q - chunks]

    totals = []
    for q in range(every):
        m = chunk(q)
        if q < chunks:
            source = jnp.zeros((1, TILE), F32)
        else:
            source = jnp.full((1, TILE), float(q - chunks + 1), F32)
        filled = jnp.concatenate([m[0:23], source, jnp.zeros((8, TILE), F32)], axis=0)
        pay3[q] = terms(filled)
        hits = jnp.where((bins == m[12:13]) & (m[22:23] > 0.5), 1.0, 0.0)
        hit_s[q * BINS : (q + 1) * BINS, :] = hits
        totals.append(jnp.sum(hits, axis=1, keepdims=True))
    rank_s[...] = ranks(hit_s[...], strictly_above(TILE))
    carries = []
    count = jnp.zeros((BINS, 1), F32)
    for q in range(every):
        carries.append(count)
        count = count + totals[q]
    high, low = split(jnp.broadcast_to(count, (BINS, 128)))
    below = (
        lax.broadcasted_iota(I32, (BINS, BINS), 0) > lax.broadcasted_iota(I32, (BINS, BINS), 1)
    ).astype(BF16)
    start = jnp.dot(below, high, preferred_element_type=F32)
    start = (start + jnp.dot(below, low, preferred_element_type=F32))[:, 0:1]
    for q in range(every):
        hits = hit_s[q * BINS : (q + 1) * BINS, :]
        ranked = rank_s[q * BINS : (q + 1) * BINS, :] + (carries[q] + start)
        slot = jnp.sum(hits * ranked, axis=0, keepdims=True)
        there = jnp.sum(hits, axis=0, keepdims=True)
        slot_s[q : q + 1, :] = jnp.where(there > 0.5, slot, -1.0)
    present = jnp.sum(count).astype(I32)
    tiles = lax.shift_right_logical(present + (TILE - 1), TILE.bit_length() - 1)
    acted[...] = jnp.zeros_like(acted)

    def start_from(p, _):
        rhs[p] = rhs_in[p]
        return 0

    lax.fori_loop(0, rhs.shape[0], start_from, 0)

    def work(n, _):
        first = (n * TILE).astype(F32)
        moved = None
        for q in range(every):
            part = chosen_columns(pay3[q], slot_s[q : q + 1, :], first)
            moved = part if moved is None else moved + part
        m = moved[0:32] + moved[32:64] + moved[64:96]
        cell_x = m[12:13]
        there = m[22:23] > 0.5
        low_plane = jnp.min(jnp.where(there, cell_x, 16.0)).astype(I32)
        high_plane = jnp.max(jnp.where(there, cell_x, 0.0)).astype(I32) + 3
        spans = (high_plane - low_plane + WINDOW) // WINDOW
        cell_x = cell_x.astype(I32)
        cell_y = m[13:14].astype(I32)
        cell_z = m[14:15].astype(I32)
        z = lax.broadcasted_iota(I32, (extent_z, TILE), 0)
        table = pick((z - cell_z) & (extent_z - 1), [m[8 + i : 9 + i] for i in range(4)])
        high, low = split(table)
        tz[0] = high
        tz[1] = low
        y = lax.broadcasted_iota(I32, (ROWS, TILE), 0) - 2
        table_y = pick(y - cell_y, [m[4 + i : 5 + i] for i in range(4)])
        folded_y = table_y.reshape(ROWS // 8, 8, TILE)
        x = lax.broadcasted_iota(I32, (WINDOW, TILE), 0)
        x_weights = [m[i : i + 1] for i in range(4)]

        def sample(j, totals):
            plane = low_plane + j * WINDOW
            table_x = pick(x + plane - cell_x, x_weights)
            both = fhl[pl.ds(plane, WINDOW)].reshape(WINDOW * 3 * ROWS, 2 * extent_z)
            left = jnp.concatenate([both, both[:, 0:extent_z]], axis=1)
            right = jnp.concatenate([tz[0], tz[0], tz[1]], axis=0)
            part = jnp.dot(left, right, preferred_element_type=F32)
            part = part.reshape(WINDOW, 3, ROWS // 8, 8, TILE)
            result = []
            for c in range(3):
                total = totals[c]
                for p in range(WINDOW):
                    total = total + jnp.sum(part[p, c] * folded_y, axis=0) * table_x[p : p + 1]
                result.append(total)
            return tuple(result)

        totals = lax.fori_loop(0, spans, sample, (jnp.zeros((8, TILE), F32),) * 3)
        totals = [jnp.sum(total, axis=0, keepdims=True) for total in totals]
        force = [m[16 + c : 17 + c] - totals[c] for c in range(3)]
        torque = cross([m[19 + c : 20 + c] for c in range(3)], force)
        acting = jnp.concatenate(force + list(torque) + [jnp.zeros((2, TILE), F32)], axis=0)
        group = m[23:24] * 2.0 + m[15:16]
        member = (
            (lax.broadcasted_iota(I32, (128, TILE), 0).astype(F32) == group) & there
        ).astype(F32)
        summed = lax.dot_general(
            terms(acting),
            member.astype(BF16),
            (((1,), (1,)), ((), ())),
            preferred_element_type=F32,
        )
        acted[...] += summed[0:8] + summed[8:16] + summed[16:24]

        def deposit(j, _):
            plane = low_plane + j * WINDOW
            table_x = pick(x + plane - cell_x, x_weights)
            rows = []
            for p in range(WINDOW):
                for c in range(3):
                    rows.append((force[c] * table_x[p : p + 1]) * table_y)
            high, low = split(jnp.concatenate(rows, axis=0))
            left = jnp.concatenate([high, low, high], axis=1)
            right = jnp.concatenate([tz[0], tz[0], tz[1]], axis=1)
            added = lax.dot_general(
                left, right, (((1,), (1,)), ((), ())), preferred_element_type=F32
            )
            rhs[pl.ds(plane + 2, WINDOW)] += added.reshape(WINDOW, 3, ROWS, extent_z)
            return 0

        lax.fori_loop(0, spans, deposit, 0)
        return 0

    lax.fori_loop(0, tiles, work, 0)


def strip_kernel(
    n_gx,
    n_gy,
    per_sphere,
    rhs,
    acted,
    mot_ref,
    cs_ref,
    cp_ref,
    nm_ref,
    ybuf,
    xbuf,
    sums,
    ret,
    agx,
    agy,
    ag1,
    moved_s,
    staged,
    ret_send,
    ret_recv,
    agx_send,
    agx_recv,
    agy_send,
    agy_recv,
    y_send,
    y_recv,
    x_send,
    x_recv,
):
    gx, gy, at = neighbours(n_gx, n_gy)
    here = gx * n_gy + gy
    planes = ybuf.shape[1]
    peers = (
        [at(k, 0) for k in range(1, n_gx)]
        + [at(0, k) for k in range(1, n_gy)]
        + [at(dx, dy) for dx in (-1, 1) for dy in (-1, 1)]
    )
    barrier = greet(peers)
    inner_low = jnp.where(gy > 0, 1.0, 0.0).astype(F32)
    inner_high = jnp.where(gy < n_gy - 1, 1.0, 0.0).astype(F32)
    for n in range(8):
        sums[n] = pltpu.roll(acted[...], 128 - 2 * (n + 1), 1)
    replies = [
        remote(sums.at[n], ret.at[n], ret_send.at[n], ret_recv.at[n], at(-dx, -dy))
        for n, (dx, dy) in enumerate(LANES)
    ]
    lanes = lax.broadcasted_iota(I32, (8, 128), 1)
    row_id = lax.broadcasted_iota(I32, (8, 128), 0)
    pl.semaphore_wait(barrier, len(peers))

    def along_x(k):
        return remote(ag1.at[0], agx.at[k], agx_send.at[k], agx_recv.at[k], at(k, 0))

    def along_y(k):
        return remote(ag1.at[1], agy.at[k], agy_send.at[k], agy_recv.at[k], at(0, k))

    def sphere_step_one():
        for copy in replies:
            copy.wait()
        total = acted[...]
        for n in range(8):
            total = total + ret[n]
        start = jnp.zeros((8, 128), F32)
        for c in range(6):
            for s in range(2):
                start = jnp.where((row_id == c) & (lanes == s), mot_ref[s, c], start)
        moved = start - total * (RESPONSE / per_sphere)
        moved_s[...] = moved
        first = jnp.broadcast_to(moved[:, 0:1], (8, 128))
        other = pltpu.roll(jnp.broadcast_to(moved[:, 1:2], (8, 128)), 3, 0)
        ag1[0] = jnp.where(lanes == here, jnp.where(row_id < 3, first, other), 0.0)
        for k in range(1, n_gx):
            along_x(k).start()

    def sphere_step_two():
        for k in range(1, n_gx):
            along_x(k).wait()
        total = ag1[0]
        for k in range(1, n_gx):
            total = total + agx[k]
        ag1[1] = total
        for k in range(1, n_gy):
            along_y(k).start()

    def sphere_step_three():
        for k in range(1, n_gy):
            along_y(k).wait()
        total = ag1[1]
        for k in range(1, n_gy):
            total = total + agy[k]
        moved = moved_s[...]
        pull = jnp.zeros((8, 128), F32)
        for k in range(cs_ref.shape[0]):
            partner = cp_ref[k]
            own = cs_ref[k] - 2 * here
            chosen = jnp.sum(
                jnp.where(lanes == lax.shift_right_logical(partner, 1), total, 0.0),
                axis=1,
                keepdims=True,
            )
            chosen = jnp.broadcast_to(chosen, (8, 128))
            odd = jnp.broadcast_to(partner & 1, (8, 128)) == 1
            chosen = jnp.where(odd, pltpu.roll(chosen, 5, 0), chosen)
            pull = pull + jnp.where((lanes == own) & (row_id < 3), chosen - moved, 0.0)
        settled = jnp.concatenate(
            [moved + DASHPOT * pull, jnp.zeros((120, 128), F32)], axis=0
        )
        nm_ref[...] = settled.T[0:2, 0:6]

    def y_copies(g):
        copies = []
        for r, (first, count) in enumerate(RUNS[g]):
            lo = first + 2
            base = 4 * g + 2 * r
            copies.append(
                remote(
                    rhs.at[pl.ds(lo, count), :, pl.ds(0, 8)],
                    ybuf.at[1, pl.ds(first, count)],
                    y_send.at[base],
                    y_recv.at[base],
                    at(0, -1),
                )
            )
            copies.append(
                remote(
                    rhs.at[pl.ds(lo, count), :, pl.ds(ROWS - 8, 8)],
                    ybuf.at[0, pl.ds(first, count)],
                    y_send.at[base + 1],
                    y_recv.at[base + 1],
                    at(0, 1),
                )
            )
        return copies

    def x_copies(g):
        low = 3 * g
        return [
            remote(
                staged.at[1, pl.ds(low, 3)],
                xbuf.at[1, pl.ds(low, 3)],
                x_send.at[2 * g],
                x_recv.at[2 * g],
                at(-1, 0),
            ),
            remote(
                staged.at[0, pl.ds(3 - low, 3)],
                xbuf.at[0, pl.ds(3 - low, 3)],
                x_send.at[2 * g + 1],
                x_recv.at[2 * g + 1],
                at(1, 0),
            ),
        ]

    def stage(g):
        for side, first, base in ((1, RUNS[g][0][0], 0), (0, RUNS[g][1][0], planes - 6)):
            for i in range(3):
                p = first + i
                whole = rhs[p + 2]
                staged[side, p - base, :, 0:8, :] = whole[:, 0:8] + ybuf[0, p] * inner_low
                staged[side, p - base, :, 8 : ROWS - 8, :] = whole[:, 8 : ROWS - 8]
                staged[side, p - base, :, ROWS - 8 : ROWS, :] = (
                    whole[:, ROWS - 8 : ROWS] + ybuf[1, p] * inner_high
                )

    for g in range(2):
        for copy in y_copies(g):
            copy.start()
    for copy in replies:
        copy.start()
    for copy in y_copies(2):
        copy.start()
    for copy in y_copies(0):
        copy.wait()
    stage(0)
    for copy in x_copies(0):
        copy.start()
    sphere_step_one()
    for copy in y_copies(1):
        copy.wait()
    stage(1)
    for copy in x_copies(1):
        copy.start()
    sphere_step_two()
    sphere_step_three()
    for copy in y_copies(2):
        copy.wait()
    for g in range(2):
        for copy in x_copies(g):
            copy.wait()


def relax_kernel(n_gy, rhs_in, ybuf, xbuf, out_ref, rhs, state_a, state_b, staged, sems):
    gy = lax.axis_index("gy")
    extent_z = rhs.shape[3]
    planes = ybuf.shape[1]
    span_x = planes - 4
    span_y = out_ref.shape[2]
    y = lax.broadcasted_iota(I32, (ROWS, extent_z), 0)
    low_edge = jnp.where(gy > 0, 0, HALO)
    high_edge = jnp.where(gy < n_gy - 1, ROWS, HALO + span_y)
    inside = jnp.where((y >= low_edge) & (y < high_edge), 1.0, 0.0).astype(F32)
    inside = jnp.concatenate([inside] * 3, axis=0)
    scale = inside * (1.0 / (1.0 + 6.0 * DIFFUSION))
    flat = (3 * ROWS, extent_z)

    inner_low = jnp.where(gy > 0, 1.0, 0.0).astype(F32)
    inner_high = jnp.where(gy < n_gy - 1, 1.0, 0.0).astype(F32)

    def begin(x, beside):
        whole = rhs_in[x]
        if beside is None:
            whole = whole + xbuf[0 if x < planes // 2 else 1, x % (planes - 2)]
        if not isinstance(x, int) or 2 <= x < planes + 2:
            low = ybuf[0, x - 2] * inner_low
            high = ybuf[1, x - 2] * inner_high
            middle = jnp.zeros((3, ROWS - 16, extent_z), F32)
            whole = whole + jnp.concatenate([low, middle, high], axis=1)
        rhs[x] = whole
        state_a[x] = (whole.reshape(flat) * inside).reshape(3, ROWS, extent_z)
        return 0

    for x in list(range(6)) + list(range(planes - 2, planes + 4)):
        begin(x, None)
    lax.fori_loop(6, planes - 2, begin, 0)

    def sweep(source, x):
        centre = source[x].reshape(flat)
        total = rhs[x].reshape(flat) + source[x - 1].reshape(flat) + source[x + 1].reshape(flat)
        total = total + pltpu.roll(centre, 1, 0) + pltpu.roll(centre, 3 * ROWS - 1, 0)
        total = total + pltpu.roll(centre, 1, 1) + pltpu.roll(centre, extent_z - 1, 1)
        return total * scale

    buffers = (state_a, state_b)
    for k in range(ITERS - 1):
        source, target = buffers[k % 2], buffers[(k + 1) % 2]

        def step(s, _, source=source, target=target, first=k + 1):
            for u in range(2):
                x = first + 2 * s + u
                target[x] = sweep(source, x).reshape(3, ROWS, extent_z)
            return 0

        lax.fori_loop(0, (planes + 2 - 2 * k) // 2, step, 0)
    source = buffers[(ITERS - 1) % 2]

    def store(s):
        return pltpu.make_async_copy(
            staged.at[:, pl.ds(2 * s, 2)], out_ref.at[:, pl.ds(2 * s, 2)], sems.at[s]
        )

    def final(s, _):
        for u in range(2):
            x = 2 * s + u
            result = sweep(source, x + HALO).reshape(3, ROWS, extent_z)
            for c in range(3):
                staged[c, x] = result[c, HALO : HALO + span_y, :]
        store(s).start()
        return 0

    lax.fori_loop(0, span_x // 2, final, 0)
    for s in range(span_x // 2):
        store(s).wait()


def on_device(
    n_gx,
    n_gy,
    velocity,
    owner_block,
    base_x,
    base_y,
    base_z,
    delta_weights,
    marker_offset,
    sphere_motion,
    contact_sphere,
    contact_partner,
):
    span_x, span_y, extent_z = velocity.shape[1:]
    markers = base_x.shape[0]
    planes = span_x + 4
    every = markers // TILE + 8
    padded = planes + WINDOW - 1
    grown = (padded + 2, 3, ROWS, extent_z)
    vmem = pl.BlockSpec(memory_space=pltpu.VMEM)
    smem = pl.BlockSpec(memory_space=pltpu.SMEM)
    hbm = pl.BlockSpec(memory_space=pltpu.HBM)
    dma = pltpu.SemaphoreType.DMA
    motion = sphere_motion.T
    fhl, started, home, arrived = pl.pallas_call(
        functools.partial(request_kernel, n_gx, n_gy),
        out_shape=(
            jax.ShapeDtypeStruct((padded, 3 * ROWS, 2 * extent_z), BF16),
            jax.ShapeDtypeStruct(grown, F32),
            jax.ShapeDtypeStruct((32, markers), F32),
            jax.ShapeDtypeStruct((8, 24, TILE), F32),
        ),
        in_specs=[hbm] * 8,
        out_specs=(vmem,) * 4,
        scratch_shapes=[
            pltpu.VMEM(velocity.shape, F32),
            pltpu.VMEM((1, markers), I32),
            pltpu.VMEM((1, markers), I32),
            pltpu.VMEM((1, markers), I32),
            pltpu.VMEM((1, markers), I32),
            pltpu.VMEM((12, markers), F32),
            pltpu.VMEM((3, markers), F32),
            pltpu.SMEM((2, 6), F32),
            pltpu.VMEM((2, 3, 2, span_y, extent_z), F32),
            pltpu.VMEM((2, 3, span_x, 8, extent_z), F32),
            pltpu.VMEM((4, 3, 2, 8, extent_z), F32),
            pltpu.VMEM((32, markers), F32),
            pltpu.VMEM((96, markers), BF16),
            pltpu.VMEM((8, TILE), F32),
            pltpu.VMEM((8, 24, TILE), F32),
            pltpu.VMEM((8, 24, TILE), F32),
            pltpu.VMEM((planes, 3, ROWS, extent_z), F32),
            dma((8,)),
            dma((8,)),
            dma((8,)),
            dma((8,)),
            dma((8,)),
        ],
        compiler_params=pltpu.CompilerParams(
            collective_id=0, has_side_effects=True, vmem_limit_bytes=24 << 20
        ),
        name="requests",
    )(
        *(
            pltpu.with_memory_space_constraint(array, pltpu.HBM)
            for array in (
                velocity,
                owner_block.reshape(1, markers),
                base_x.reshape(1, markers),
                base_y.reshape(1, markers),
                base_z.reshape(1, markers),
                delta_weights,
                marker_offset,
                motion,
            )
        )
    )
    rhs, acted = pl.pallas_call(
        marker_kernel,
        out_shape=(
            jax.ShapeDtypeStruct(grown, F32),
            jax.ShapeDtypeStruct((8, 128), F32),
        ),
        in_specs=[vmem] * 4,
        out_specs=(vmem,) * 2,
        scratch_shapes=[
            pltpu.VMEM((every, 96, TILE), BF16),
            pltpu.VMEM((every * BINS, TILE), F32),
            pltpu.VMEM((every * BINS, TILE), F32),
            pltpu.VMEM((every, TILE), F32),
            pltpu.VMEM((2, extent_z, TILE), BF16),
        ],
        compiler_params=pltpu.CompilerParams(vmem_limit_bytes=24 << 20),
        name="markers",
    )(fhl, started, home, arrived)
    new_motion, ybuf, xbuf = pl.pallas_call(
        functools.partial(strip_kernel, n_gx, n_gy, markers // 2),
        out_shape=(
            jax.ShapeDtypeStruct(motion.shape, F32),
            jax.ShapeDtypeStruct((2, planes, 3, 8, extent_z), F32),
            jax.ShapeDtypeStruct((2, 6, 3, ROWS, extent_z), F32),
        ),
        in_specs=[vmem] * 2 + [smem] * 3,
        out_specs=(vmem,) * 3,
        scratch_shapes=[
            pltpu.VMEM((8, 8, 128), F32),
            pltpu.VMEM((8, 8, 128), F32),
            pltpu.VMEM((n_gx, 8, 128), F32),
            pltpu.VMEM((n_gy, 8, 128), F32),
            pltpu.VMEM((2, 8, 128), F32),
            pltpu.VMEM((8, 128), F32),
            pltpu.VMEM((2, 6, 3, ROWS, extent_z), F32),
            dma((8,)),
            dma((8,)),
            dma((n_gx,)),
            dma((n_gx,)),
            dma((n_gy,)),
            dma((n_gy,)),
            dma((12,)),
            dma((12,)),
            dma((4,)),
            dma((4,)),
        ],
        compiler_params=pltpu.CompilerParams(
            collective_id=1, has_side_effects=True, vmem_limit_bytes=24 << 20
        ),
        name="strips",
    )(rhs, acted, motion, contact_sphere, contact_partner)
    relaxed = pl.pallas_call(
        functools.partial(relax_kernel, n_gy),
        out_shape=jax.ShapeDtypeStruct(velocity.shape, F32),
        in_specs=[vmem] * 3,
        out_specs=pl.BlockSpec(memory_space=pltpu.HBM),
        scratch_shapes=[
            pltpu.VMEM((planes + 4, 3, ROWS, extent_z), F32),
            pltpu.VMEM((planes + 4, 3, ROWS, extent_z), F32),
            pltpu.VMEM((planes + 4, 3, ROWS, extent_z), F32),
            pltpu.VMEM(velocity.shape, F32),
            dma((span_x // 2,)),
        ],
        compiler_params=pltpu.CompilerParams(vmem_limit_bytes=24 << 20),
        name="relax",
    )(rhs, ybuf, xbuf)
    return relaxed, new_motion.T


def solution(mesh):
    placed = (
        P(None, "gx", "gy", None),
        P(("gx", "gy"), None),
        P(("gx", "gy")),
        P(("gx", "gy")),
        P(("gx", "gy")),
        P(None, ("gx", "gy")),
        P(None, ("gx", "gy")),
        P(None, ("gx", "gy")),
        P(("gx", "gy")),
        P(("gx", "gy")),
    )
    return jax.shard_map(
        functools.partial(on_device, mesh.shape["gx"], mesh.shape["gy"]),
        mesh=mesh,
        in_specs=placed,
        out_specs=(P(None, "gx", "gy", None), P(None, ("gx", "gy"))),
        check_vma=False,
    )
```

time: 86.1 us -> 81.6 us (0.948)
  local copies, waits for them, and re-layouts: 8.4 us -> 0.58 us
  Pallas kernels: 75.9 us -> 79.6 us
    unnamed x21 -> x7, local copies, waits for them, and re-layouts: 8.4 us -> 0.58 us
    pallas_call x1 -> x3, Pallas kernels: 66.5 us -> 70.3 us  [the longest x1 31.7 us: on_device(): pl.pallas_call(functools.partial(strip_kernel, n_gx, n_gy, markers // 2),...]
where the time goes in v3:
time: 81.6 us; the launch traced here: 80.9 us
  Pallas kernels  79.6 us (98%)
    pallas_call x1, Pallas kernels, on_device(): pl.pallas_call(functools.partial(strip_kernel, n_gx, n_gy, markers // 2),...  31.7 us
    pallas_call x1, Pallas kernels, on_device(): pl.pallas_call(marker_kernel, out_shape=(jax.ShapeDtypeStruct(grown, F32)...  20 us
    pallas_call x1, Pallas kernels, on_device(): pl.pallas_call(functools.partial(request_kernel, n_gx, n_gy), out_shape=(...  18.6 us
    pallas_call x1, Pallas kernels, on_device(): pl.pallas_call(functools.partial(relax_kernel, n_gy), out_shape=jax.Shape...  9.33 us

profile of v3, /device:TPU:1, one launch (start us, length us, event | category | flops | bytes accessed | tf_op | source)
XLA Modules:
  0.0 80.9 jit_solution(17453256722886009485)
XLA Ops:
  0.6 18.6 %requests.1 = (bf16[25,120,512]{2,1,0:T(8,128)(2,1)S(1)}, f32[27,3,40,256]{3,2,1,0:T(8,128)S(1)}, f32[32,2048]{1,0:T(8,128)S(1)}, f32[8,24,256]{2,1,0:T(8,128)S(1)}) custom-call(f32[3,16,32,256]{3,2,1,0:T(8,128)} %v_hbm.1, s32[1,2048]{1,0:T(1,128)} %bitcast.9, s32[1,2048]{1,0:T(1,128)} %bitcast.10, s32[1,2048]{1,0:T(1,128)} %bitcast.11, s32[1,2048]{1,0:T(1,128)} %bitcast.12, ...), custom_call_target="tpu_custom_call" | custom-call | tf_op jit(solution)/shard_map/requests/pallas_call | solution.py:741
  19.2 0.0 copy-start
  19.2 0.0 copy-start.1
  19.2 0.0 copy-start.2
  19.2 20.0 %markers.1 = (f32[27,3,40,256]{3,2,1,0:T(8,128)S(1)}, f32[8,128]{1,0:T(8,128)S(1)}) custom-call(bf16[25,120,512]{2,1,0:T(8,128)(2,1)S(1)} %get-tuple-element.11.fhl, f32[27,3,40,256]{3,2,1,0:T(8,128)S(1)} %get-tuple-element.12.rhs_in, f32[32,2048]{1,0:T(8,128)S(1)} %get-tuple-element.13.home, f32[8,24,256]{2,1,0:T(8,128)S(1)} %get-tuple-element.14.arrived), custom_call_target="tpu_custom_call" | custom-call | tf_op jit(solution)/shard_map/markers/pallas_call | solution.py:794
  39.3 0.0 copy-done
  39.3 0.0 copy-done.1
  39.3 0.0 copy-done.2
  39.3 31.7 %strips.1 = (f32[2,6]{1,0:T(2,128)S(1)}, f32[2,20,3,8,256]{4,3,2,1,0:T(8,128)S(1)}, f32[2,6,3,40,256]{4,3,2,1,0:T(8,128)S(1)}) custom-call(f32[27,3,40,256]{3,2,1,0:T(8,128)S(1)} %get-tuple-element.15.rhs.rhs_in, f32[8,128]{1,0:T(8,128)S(1)} %get-tuple-element.16.acted, f32[2,6]{1,0:T(2,128)S(1)} %bitcast.7, s32[4]{0:T(128)S(1)} %copy-done.1, s32[4]{0:T(128)S(1)} %copy-done.2), custom_call_target="tpu_custom_call" | custom-call | tf_op jit(solution)/shard_map/strips/pallas_call | solution.py:812
  71.0 9.3 %relax.1 = f32[3,16,32,256]{3,2,1,0:T(8,128)} custom-call(f32[27,3,40,256]{3,2,1,0:T(8,128)S(1)} %get-tuple-element.15.rhs.rhs_in, f32[2,20,3,8,256]{4,3,2,1,0:T(8,128)S(1)} %get-tuple-element.17.ybuf, f32[2,6,3,40,256]{4,3,2,1,0:T(8,128)S(1)} %get-tuple-element.18.xbuf), custom_call_target="tpu_custom_call" | custom-call | tf_op jit(solution)/shard_map/relax/pallas_call | solution.py:845
  80.3 0.6 copy.13
Async XLA Ops:
  19.2 20.1 %copy-start = (f32[6,2]{0,1:T(2,128)S(1)}, f32[6,2]{0,1:T(2,128)}, u32[]{:S(2)}) copy-start(f32[6,2]{0,1:T(2,128)} %param.17) | copy-start | bytes 148
  19.2 20.1 %copy-start.1 = (s32[4]{0:T(128)S(1)}, s32[4]{0:T(128)}, u32[]{:S(2)}) copy-start(s32[4]{0:T(128)} %cs_ref.1) | copy-start | bytes 52
  19.2 20.1 %copy-start.2 = (s32[4]{0:T(128)S(1)}, s32[4]{0:T(128)}, u32[]{:S(2)}) copy-start(s32[4]{0:T(128)} %cp_ref.1) | copy-start | bytes 52

commit v4 on v3

--- a/solution.py
+++ b/solution.py
@@ -23,7 +23,8 @@
 ROWS = 40
 HALO = 4
 LANES = [(dx, dy) for dx in (-1, 0, 1) for dy in (-1, 0, 1) if (dx, dy) != (0, 0)]
-RUNS = [((0, 3), (17, 3)), ((3, 3), (14, 3)), ((6, 8),)]
+DIAGONALS = [(dx, dy) for dx, dy in LANES if dx * dy != 0]
+RUNS = [((0, 1), (19, 1)), ((1, 2), (17, 2)), ((3, 3), (14, 3)), ((6, 8),)]
 
 
 def split(values):
@@ -127,6 +128,7 @@
     hx,
     hy,
     hc,
+    corner,
     pay,
     pay3,
     slot_s,
@@ -168,9 +170,17 @@
     for copy in loads:
         copy.wait()
 
-    pl.semaphore_wait(barrier, len(LANES))
     last = span_x - 2
     top = span_y - 8
+    corner[...] = jnp.zeros_like(corner)
+    for k, (dx, dy) in enumerate(DIAGONALS):
+        x0 = 0 if dx < 0 else last
+        y0 = 0 if dy < 0 else span_y - 2
+        for c in range(3):
+            for i in range(2):
+                row = 4 * c + 2 * i
+                corner[k, row : row + 2, :] = v_ref[c, x0 + i, y0 : y0 + 2, :]
+    pl.semaphore_wait(barrier, len(LANES))
     halo = []
     halo.append(remote(v_ref.at[:, 0:2], hx.at[1], halo_send.at[0], halo_recv.at[0], at(-1, 0)))
     halo.append(
@@ -182,22 +192,13 @@
     halo.append(
         remote(v_ref.at[:, :, top:span_y], hy.at[0], halo_send.at[3], halo_recv.at[3], at(0, 1))
     )
-    k = 4
-    for dx in (-1, 1):
-        for dy in (-1, 1):
-            x0 = 0 if dx < 0 else last
-            y0 = 0 if dy < 0 else top
-            slot = (1 if dx < 0 else 0) * 2 + (1 if dy < 0 else 0)
-            halo.append(
-                remote(
-                    v_ref.at[:, x0 : x0 + 2, y0 : y0 + 8],
-                    hc.at[slot],
-                    halo_send.at[k],
-                    halo_recv.at[k],
-                    at(dx, dy),
-                )
+    for k, (dx, dy) in enumerate(DIAGONALS):
+        slot = (1 if dx < 0 else 0) * 2 + (1 if dy < 0 else 0)
+        halo.append(
+            remote(
+                corner.at[k], hc.at[slot], halo_send.at[4 + k], halo_recv.at[4 + k], at(dx, dy)
             )
-            k += 1
+        )
     for copy in halo:
         copy.start()
 
@@ -301,8 +302,10 @@
             p = (0 if side == 0 else planes - 2) + i
             for c in range(3):
                 frame[p, c, 4 : 4 + span_y, :] = hx[side, c, i]
-                frame[p, c, 2:4, :] = hc[side * 2, c, i, 6:8, :] * inner_low
-                frame[p, c, 36:38, :] = hc[side * 2 + 1, c, i, 0:2, :] * inner_high
+                frame[p, c, 2:4, :] = hc[side * 2, 4 * c + 2 * i : 4 * c + 2 * i + 2, :] * inner_low
+                frame[p, c, 36:38, :] = (
+                    hc[side * 2 + 1, 4 * c + 2 * i : 4 * c + 2 * i + 2, :] * inner_high
+                )
 
     def halve(p, _):
         high, low = split(frame[p].reshape(3 * ROWS, extent_z))
@@ -317,7 +320,21 @@
 
 
 def marker_kernel(
-    fhl, rhs_in, home, arrived, rhs, acted, pay3, hit_s, rank_s, slot_s, tz
+    fhl,
+    rhs_in,
+    home,
+    arrived,
+    rhs,
+    acted,
+    pay3,
+    hit_s,
+    rank_s,
+    slot_s,
+    tz,
+    held,
+    edge_v,
+    edge,
+    edge_sem,
 ):
     chunks = home.shape[1] // TILE
     every = chunks + 8
@@ -330,12 +347,6 @@
     totals = []
     for q in range(every):
         m = chunk(q)
-        if q < chunks:
-            source = jnp.zeros((1, TILE), F32)
-        else:
-            source = jnp.full((1, TILE), float(q - chunks + 1), F32)
-        filled = jnp.concatenate([m[0:23], source, jnp.zeros((8, TILE), F32)], axis=0)
-        pay3[q] = terms(filled)
         hits = jnp.where((bins == m[12:13]) & (m[22:23] > 0.5), 1.0, 0.0)
         hit_s[q * BINS : (q + 1) * BINS, :] = hits
         totals.append(jnp.sum(hits, axis=1, keepdims=True))
@@ -345,20 +356,37 @@
     for q in range(every):
         carries.append(count)
         count = count + totals[q]
-    high, low = split(jnp.broadcast_to(count, (BINS, 128)))
+    count = jnp.broadcast_to(count, (BINS, 128))
+    high, low = split(count)
     below = (
         lax.broadcasted_iota(I32, (BINS, BINS), 0) > lax.broadcasted_iota(I32, (BINS, BINS), 1)
     ).astype(BF16)
     start = jnp.dot(below, high, preferred_element_type=F32)
-    start = (start + jnp.dot(below, low, preferred_element_type=F32))[:, 0:1]
+    start = start + jnp.dot(below, low, preferred_element_type=F32)
+    opening = lax.broadcasted_iota(I32, (BINS, 128), 1).astype(F32) * TILE
+    present = jnp.sum(count, axis=0, keepdims=True)
+    closing = jnp.minimum(opening + TILE, present)
+    first_bin = jnp.sum(jnp.where(start + count <= opening, 1.0, 0.0), axis=0, keepdims=True)
+    last_bin = jnp.sum(jnp.where(start < closing, 1.0, 0.0), axis=0, keepdims=True) - 1.0
+    edge_v[...] = jnp.concatenate(
+        [first_bin, last_bin, present, jnp.zeros((5, 128), F32)], axis=0
+    ).astype(I32)
+    to_scalars = pltpu.make_async_copy(edge_v, edge, edge_sem)
+    to_scalars.start()
+    start = start[:, 0:1]
     for q in range(every):
         hits = hit_s[q * BINS : (q + 1) * BINS, :]
         ranked = rank_s[q * BINS : (q + 1) * BINS, :] + (carries[q] + start)
         slot = jnp.sum(hits * ranked, axis=0, keepdims=True)
         there = jnp.sum(hits, axis=0, keepdims=True)
         slot_s[q : q + 1, :] = jnp.where(there > 0.5, slot, -1.0)
-    present = jnp.sum(count).astype(I32)
-    tiles = lax.shift_right_logical(present + (TILE - 1), TILE.bit_length() - 1)
+        m = chunk(q)
+        if q < chunks:
+            source = jnp.zeros((1, TILE), F32)
+        else:
+            source = jnp.full((1, TILE), float(q - chunks + 1), F32)
+        filled = jnp.concatenate([m[0:23], source, jnp.zeros((8, TILE), F32)], axis=0)
+        pay3[q] = terms(filled)
     acted[...] = jnp.zeros_like(acted)
 
     def start_from(p, _):
@@ -366,57 +394,59 @@
         return 0
 
     lax.fori_loop(0, rhs.shape[0], start_from, 0)
-
-    def work(n, _):
-        first = (n * TILE).astype(F32)
+    slot_id = lax.broadcasted_iota(I32, (TILE, TILE), 0).astype(F32)
+
+    def gather(n):
+        wanted = slot_id + (n * TILE).astype(F32)
         moved = None
         for q in range(every):
-            part = chosen_columns(pay3[q], slot_s[q : q + 1, :], first)
+            hit = jnp.where(wanted == slot_s[q : q + 1, :], 1.0, 0.0).astype(BF16)
+            part = lax.dot_general(
+                hit, pay3[q], (((1,), (1,)), ((), ())), preferred_element_type=F32
+            )
             moved = part if moved is None else moved + part
-        m = moved[0:32] + moved[32:64] + moved[64:96]
-        cell_x = m[12:13]
-        there = m[22:23] > 0.5
-        low_plane = jnp.min(jnp.where(there, cell_x, 16.0)).astype(I32)
-        high_plane = jnp.max(jnp.where(there, cell_x, 0.0)).astype(I32) + 3
-        spans = (high_plane - low_plane + WINDOW) // WINDOW
-        cell_x = cell_x.astype(I32)
+        moved = jnp.concatenate([moved, jnp.zeros((TILE, 32), F32)], axis=1).T
+        return moved[0:32] + moved[32:64] + moved[64:96]
+
+    def prepare(m):
         cell_y = m[13:14].astype(I32)
         cell_z = m[14:15].astype(I32)
         z = lax.broadcasted_iota(I32, (extent_z, TILE), 0)
         table = pick((z - cell_z) & (extent_z - 1), [m[8 + i : 9 + i] for i in range(4)])
         high, low = split(table)
-        tz[0] = high
-        tz[1] = low
         y = lax.broadcasted_iota(I32, (ROWS, TILE), 0) - 2
         table_y = pick(y - cell_y, [m[4 + i : 5 + i] for i in range(4)])
+        return high, low, table_y
+
+    def x_table(m, plane):
+        x = lax.broadcasted_iota(I32, (8, TILE), 0)
+        return pick(x + plane - m[12:13].astype(I32), [m[i : i + 1] for i in range(4)])
+
+    def sample(m, plane, high, low, table_y, totals):
+        table_x = x_table(m, plane)
         folded_y = table_y.reshape(ROWS // 8, 8, TILE)
-        x = lax.broadcasted_iota(I32, (WINDOW, TILE), 0)
-        x_weights = [m[i : i + 1] for i in range(4)]
-
-        def sample(j, totals):
-            plane = low_plane + j * WINDOW
-            table_x = pick(x + plane - cell_x, x_weights)
-            both = fhl[pl.ds(plane, WINDOW)].reshape(WINDOW * 3 * ROWS, 2 * extent_z)
-            left = jnp.concatenate([both, both[:, 0:extent_z]], axis=1)
-            right = jnp.concatenate([tz[0], tz[0], tz[1]], axis=0)
-            part = jnp.dot(left, right, preferred_element_type=F32)
-            part = part.reshape(WINDOW, 3, ROWS // 8, 8, TILE)
-            result = []
-            for c in range(3):
-                total = totals[c]
-                for p in range(WINDOW):
-                    total = total + jnp.sum(part[p, c] * folded_y, axis=0) * table_x[p : p + 1]
-                result.append(total)
-            return tuple(result)
-
-        totals = lax.fori_loop(0, spans, sample, (jnp.zeros((8, TILE), F32),) * 3)
+        both = fhl[pl.ds(plane, WINDOW)].reshape(WINDOW * 3 * ROWS, 2 * extent_z)
+        left = jnp.concatenate([both, both[:, 0:extent_z]], axis=1)
+        right = jnp.concatenate([high, high, low], axis=0)
+        part = jnp.dot(left, right, preferred_element_type=F32)
+        part = part.reshape(WINDOW, 3, ROWS // 8, 8, TILE)
+        result = []
+        for c in range(3):
+            total = totals[c]
+            for p in range(WINDOW):
+                total = total + jnp.sum(part[p, c] * folded_y, axis=0) * table_x[p : p + 1]
+            result.append(total)
+        return tuple(result)
+
+    def act(m, totals):
         totals = [jnp.sum(total, axis=0, keepdims=True) for total in totals]
         force = [m[16 + c : 17 + c] - totals[c] for c in range(3)]
         torque = cross([m[19 + c : 20 + c] for c in range(3)], force)
         acting = jnp.concatenate(force + list(torque) + [jnp.zeros((2, TILE), F32)], axis=0)
         group = m[23:24] * 2.0 + m[15:16]
         member = (
-            (lax.broadcasted_iota(I32, (128, TILE), 0).astype(F32) == group) & there
+            (lax.broadcasted_iota(I32, (128, TILE), 0).astype(F32) == group)
+            & (m[22:23] > 0.5)
         ).astype(F32)
         summed = lax.dot_general(
             terms(acting),
@@ -425,27 +455,85 @@
             preferred_element_type=F32,
         )
         acted[...] += summed[0:8] + summed[8:16] + summed[16:24]
-
-        def deposit(j, _):
-            plane = low_plane + j * WINDOW
-            table_x = pick(x + plane - cell_x, x_weights)
-            rows = []
-            for p in range(WINDOW):
-                for c in range(3):
-                    rows.append((force[c] * table_x[p : p + 1]) * table_y)
-            high, low = split(jnp.concatenate(rows, axis=0))
-            left = jnp.concatenate([high, low, high], axis=1)
-            right = jnp.concatenate([tz[0], tz[0], tz[1]], axis=1)
-            added = lax.dot_general(
-                left, right, (((1,), (1,)), ((), ())), preferred_element_type=F32
-            )
-            rhs[pl.ds(plane + 2, WINDOW)] += added.reshape(WINDOW, 3, ROWS, extent_z)
-            return 0
-
-        lax.fori_loop(0, spans, deposit, 0)
+        return force
+
+    def deposit(m, plane, force, z_high, z_low, table_y):
+        table_x = x_table(m, plane)
+        rows = []
+        for p in range(WINDOW):
+            for c in range(3):
+                rows.append((force[c] * table_x[p : p + 1]) * table_y)
+        high, low = split(jnp.concatenate(rows, axis=0))
+        left = jnp.concatenate([high, low, high], axis=1)
+        right = jnp.concatenate([z_high, z_high, z_low], axis=1)
+        added = lax.dot_general(
+            left, right, (((1,), (1,)), ((), ())), preferred_element_type=F32
+        )
+        rhs[pl.ds(plane + 2, WINDOW)] += added.reshape(WINDOW, 3, ROWS, extent_z)
+
+    held[0] = gather(jnp.int32(0))
+    to_scalars.wait()
+    tiles = lax.shift_right_logical(edge[2, 0] + (TILE - 1), TILE.bit_length() - 1)
+    nothing = (jnp.zeros((8, TILE), F32),) * 3
+
+    def work(n, _):
+        low_plane = edge[0, n]
+        spans = (edge[1, n] + 3 - low_plane + WINDOW) // WINDOW
+        slot = n & 1
+
+        @pl.when(spans <= 1)
+        def _narrow():
+            m = held[slot]
+            high, low, table_y = prepare(m)
+            totals = sample(m, low_plane, high, low, table_y, nothing)
+            following = gather(n + 1)
+            force = act(m, totals)
+            deposit(m, low_plane, force, high, low, table_y)
+            held[1 - slot] = following
+
+        @pl.when(spans > 1)
+        def _wide():
+            m = held[slot]
+            high, low, table_y = prepare(m)
+            tz[0] = high
+            tz[1] = low
+
+            def sample_span(j, totals):
+                plane = low_plane + j * WINDOW
+                return sample(held[slot], plane, tz[0], tz[1], table_y, totals)
+
+            force = act(m, lax.fori_loop(0, spans, sample_span, nothing))
+
+            def deposit_span(j, _):
+                plane = low_plane + j * WINDOW
+                deposit(held[slot], plane, force, tz[0], tz[1], table_y)
+                return 0
+
+            lax.fori_loop(0, spans, deposit_span, 0)
+            held[1 - slot] = gather(n + 1)
+
         return 0
 
     lax.fori_loop(0, tiles, work, 0)
+
+
+def wall_masks(gy, n_gy, span_y, extent_z):
+    y = lax.broadcasted_iota(I32, (ROWS, extent_z), 0)
+    low_edge = jnp.where(gy > 0, 0, HALO)
+    high_edge = jnp.where(gy < n_gy - 1, ROWS, HALO + span_y)
+    inside = jnp.where((y >= low_edge) & (y < high_edge), 1.0, 0.0).astype(F32)
+    inside = jnp.concatenate([inside] * 3, axis=0)
+    return inside, inside * (1.0 / (1.0 + 6.0 * DIFFUSION))
+
+
+def relaxed(rhs, before, centre, after, scale):
+    shape = rhs.shape
+    flat = scale.shape
+    centre = centre.reshape(flat)
+    total = rhs.reshape(flat) + before.reshape(flat) + after.reshape(flat)
+    total = total + pltpu.roll(centre, 1, 0) + pltpu.roll(centre, flat[0] - 1, 0)
+    total = total + pltpu.roll(centre, 1, 1) + pltpu.roll(centre, flat[1] - 1, 1)
+    return (total * scale).reshape(shape)
 
 
 def strip_kernel(
@@ -460,6 +548,11 @@
     nm_ref,
     ybuf,
     xbuf,
+    mid_0,
+    mid_1,
+    mid_2,
+    mid_3,
+    done,
     sums,
     ret,
     agx,
@@ -481,6 +574,7 @@
     gx, gy, at = neighbours(n_gx, n_gy)
     here = gx * n_gy + gy
     planes = ybuf.shape[1]
+    span_y = done.shape[2]
     peers = (
         [at(k, 0) for k in range(1, n_gx)]
         + [at(0, k) for k in range(1, n_gy)]
@@ -584,133 +678,176 @@
         return copies
 
     def x_copies(g):
-        low = 3 * g
+        (low, count), (high, _) = RUNS[g]
+        high = high - (planes - 6)
         return [
             remote(
-                staged.at[1, pl.ds(low, 3)],
-                xbuf.at[1, pl.ds(low, 3)],
+                staged.at[1, pl.ds(low, count)],
+                xbuf.at[1, pl.ds(low, count)],
                 x_send.at[2 * g],
                 x_recv.at[2 * g],
                 at(-1, 0),
             ),
             remote(
-                staged.at[0, pl.ds(3 - low, 3)],
-                xbuf.at[0, pl.ds(3 - low, 3)],
+                staged.at[0, pl.ds(high, count)],
+                xbuf.at[0, pl.ds(high, count)],
                 x_send.at[2 * g + 1],
                 x_recv.at[2 * g + 1],
                 at(1, 0),
             ),
         ]
 
+    def with_strips(p):
+        whole = rhs[p + 2]
+        low = whole[:, 0:8] + ybuf[0, p] * inner_low
+        high = whole[:, ROWS - 8 : ROWS] + ybuf[1, p] * inner_high
+        return jnp.concatenate([low, whole[:, 8 : ROWS - 8], high], axis=1)
+
     def stage(g):
-        for side, first, base in ((1, RUNS[g][0][0], 0), (0, RUNS[g][1][0], planes - 6)):
-            for i in range(3):
-                p = first + i
-                whole = rhs[p + 2]
-                staged[side, p - base, :, 0:8, :] = whole[:, 0:8] + ybuf[0, p] * inner_low
-                staged[side, p - base, :, 8 : ROWS - 8, :] = whole[:, 8 : ROWS - 8]
-                staged[side, p - base, :, ROWS - 8 : ROWS, :] = (
-                    whole[:, ROWS - 8 : ROWS] + ybuf[1, p] * inner_high
-                )
+        for side, base in ((1, 0), (0, planes - 6)):
+            first, count = RUNS[g][1 - side]
+            for p in range(first, first + count):
+                staged[side, p - base] = with_strips(p)
 
     for g in range(2):
         for copy in y_copies(g):
             copy.start()
     for copy in replies:
         copy.start()
-    for copy in y_copies(2):
-        copy.start()
-    for copy in y_copies(0):
-        copy.wait()
-    stage(0)
-    for copy in x_copies(0):
-        copy.start()
+    for g in range(2, 4):
+        for copy in y_copies(g):
+            copy.start()
+    for g in range(2):
+        for copy in y_copies(g):
+            copy.wait()
+        stage(g)
+        for copy in x_copies(g):
+            copy.start()
     sphere_step_one()
-    for copy in y_copies(1):
-        copy.wait()
-    stage(1)
-    for copy in x_copies(1):
-        copy.start()
-    sphere_step_two()
-    sphere_step_three()
     for copy in y_copies(2):
         copy.wait()
-    for g in range(2):
+    stage(2)
+    for copy in x_copies(2):
+        copy.start()
+    for copy in y_copies(3):
+        copy.wait()
+    inside, scale = wall_masks(gy, n_gy, span_y, rhs.shape[3])
+    span_mid = mid_0.shape[0]
+
+    def begin(i, _):
+        mid_0[i] = (with_strips(i + 4).reshape(inside.shape) * inside).reshape(mid_0.shape[1:])
+        return 0
+
+    lax.fori_loop(0, span_mid, begin, 0)
+    sphere_step_two()
+    stages = (mid_0, mid_1, mid_2, mid_3)
+    for k in range(1, ITERS):
+        source, target = stages[k - 1], stages[k]
+
+        def step(s, _, source=source, target=target, k=k):
+            for u in range(2):
+                i = 2 * s + u
+                target[i] = relaxed(
+                    mid_0[i + k], source[i], source[i + 1], source[i + 2], scale
+                )
+            return 0
+
+        lax.fori_loop(0, (span_mid - 2 * k) // 2, step, 0)
+    for i in range(span_mid - 2 * ITERS):
+        result = relaxed(mid_0[i + ITERS], mid_3[i], mid_3[i + 1], mid_3[i + 2], scale)
+        for c in range(3):
+            done[c, i] = result[c, HALO : HALO + span_y, :]
+    sphere_step_three()
+    for g in range(3):
         for copy in x_copies(g):
             copy.wait()
 
 
-def relax_kernel(n_gy, rhs_in, ybuf, xbuf, out_ref, rhs, state_a, state_b, staged, sems):
+def relax_kernel(
+    n_gy,
+    rhs_in,
+    ybuf,
+    xbuf,
+    mid_0,
+    mid_1,
+    mid_2,
+    mid_3,
+    done,
+    out_ref,
+    rhs,
+    one,
+    two,
+    three,
+    staged,
+    sems,
+    done_sem,
+):
     gy = lax.axis_index("gy")
-    extent_z = rhs.shape[3]
     planes = ybuf.shape[1]
     span_x = planes - 4
     span_y = out_ref.shape[2]
-    y = lax.broadcasted_iota(I32, (ROWS, extent_z), 0)
-    low_edge = jnp.where(gy > 0, 0, HALO)
-    high_edge = jnp.where(gy < n_gy - 1, ROWS, HALO + span_y)
-    inside = jnp.where((y >= low_edge) & (y < high_edge), 1.0, 0.0).astype(F32)
-    inside = jnp.concatenate([inside] * 3, axis=0)
-    scale = inside * (1.0 / (1.0 + 6.0 * DIFFUSION))
-    flat = (3 * ROWS, extent_z)
-
+    whole_span = planes + 4
+    middle = pltpu.make_async_copy(done, out_ref.at[:, 6 : span_x - 6], done_sem)
+    middle.start()
+    inside, scale = wall_masks(gy, n_gy, span_y, rhs.shape[3])
     inner_low = jnp.where(gy > 0, 1.0, 0.0).astype(F32)
     inner_high = jnp.where(gy < n_gy - 1, 1.0, 0.0).astype(F32)
-
-    def begin(x, beside):
-        whole = rhs_in[x]
-        if beside is None:
-            whole = whole + xbuf[0 if x < planes // 2 else 1, x % (planes - 2)]
-        if not isinstance(x, int) or 2 <= x < planes + 2:
-            low = ybuf[0, x - 2] * inner_low
-            high = ybuf[1, x - 2] * inner_high
-            middle = jnp.zeros((3, ROWS - 16, extent_z), F32)
-            whole = whole + jnp.concatenate([low, middle, high], axis=1)
-        rhs[x] = whole
-        state_a[x] = (whole.reshape(flat) * inside).reshape(3, ROWS, extent_z)
-        return 0
-
-    for x in list(range(6)) + list(range(planes - 2, planes + 4)):
-        begin(x, None)
-    lax.fori_loop(6, planes - 2, begin, 0)
-
-    def sweep(source, x):
-        centre = source[x].reshape(flat)
-        total = rhs[x].reshape(flat) + source[x - 1].reshape(flat) + source[x + 1].reshape(flat)
-        total = total + pltpu.roll(centre, 1, 0) + pltpu.roll(centre, 3 * ROWS - 1, 0)
-        total = total + pltpu.roll(centre, 1, 1) + pltpu.roll(centre, extent_z - 1, 1)
-        return total * scale
-
-    buffers = (state_a, state_b)
-    for k in range(ITERS - 1):
-        source, target = buffers[k % 2], buffers[(k + 1) % 2]
-
-        def step(s, _, source=source, target=target, first=k + 1):
+    for i in range(6):
+        for x, beside in ((i, xbuf[0, i]), (planes - 2 + i, xbuf[1, i])):
+            whole = rhs_in[x] + beside
+            if 2 <= x < planes + 2:
+                low = whole[:, 0:8] + ybuf[0, x - 2] * inner_low
+                high = whole[:, ROWS - 8 : ROWS] + ybuf[1, x - 2] * inner_high
+                whole = jnp.concatenate([low, whole[:, 8 : ROWS - 8], high], axis=1)
+            rhs[x] = (whole.reshape(inside.shape) * inside).reshape(whole.shape)
+    stages = (rhs, one, two, three)
+    for k, (mid, count) in enumerate(((mid_0, 4), (mid_1, 2), (mid_2, 2), (mid_3, 2))):
+        for i in range(count):
+            stages[k][6 + k + i] = mid[i]
+            stages[k][whole_span - 7 - k - i] = mid[mid.shape[0] - 1 - i]
+
+    def swept(k, x):
+        source = stages[k - 1]
+        return relaxed(rhs[x], source[x - 1], source[x], source[x + 1], scale)
+
+    for k in range(1, ITERS):
+
+        def step(s, _, k=k):
             for u in range(2):
-                x = first + 2 * s + u
-                target[x] = sweep(source, x).reshape(3, ROWS, extent_z)
+                low = k + 2 * s + u
+                high = whole_span - 6 - k + 2 * s + u
+                stages[k][low] = swept(k, low)
+                stages[k][high] = swept(k, high)
             return 0
 
-        lax.fori_loop(0, (planes + 2 - 2 * k) // 2, step, 0)
-    source = buffers[(ITERS - 1) % 2]
-
-    def store(s):
-        return pltpu.make_async_copy(
-            staged.at[:, pl.ds(2 * s, 2)], out_ref.at[:, pl.ds(2 * s, 2)], sems.at[s]
-        )
+        lax.fori_loop(0, 3, step, 0)
+
+    def stores(s):
+        return [
+            pltpu.make_async_copy(
+                staged.at[:, pl.ds(first + 2 * s, 2)],
+                out_ref.at[:, pl.ds(first + 2 * s, 2)],
+                sems.at[2 * s + side],
+            )
+            for side, first in enumerate((0, span_x - 6))
+        ]
 
     def final(s, _):
         for u in range(2):
-            x = 2 * s + u
-            result = sweep(source, x + HALO).reshape(3, ROWS, extent_z)
-            for c in range(3):
-                staged[c, x] = result[c, HALO : HALO + span_y, :]
-        store(s).start()
+            for first in (0, span_x - 6):
+                x = first + 2 * s + u
+                result = swept(ITERS, x + HALO)
+                for c in range(3):
+                    staged[c, x] = result[c, HALO : HALO + span_y, :]
+        for copy in stores(s):
+            copy.start()
         return 0
 
-    lax.fori_loop(0, span_x // 2, final, 0)
-    for s in range(span_x // 2):
-        store(s).wait()
+    lax.fori_loop(0, 3, final, 0)
+    for s in range(3):
+        for copy in stores(s):
+            copy.wait()
+    middle.wait()
 
 
 def on_device(
@@ -759,7 +896,8 @@
             pltpu.SMEM((2, 6), F32),
             pltpu.VMEM((2, 3, 2, span_y, extent_z), F32),
             pltpu.VMEM((2, 3, span_x, 8, extent_z), F32),
-            pltpu.VMEM((4, 3, 2, 8, extent_z), F32),
+            pltpu.VMEM((4, 16, extent_z), F32),
+            pltpu.VMEM((4, 16, extent_z), F32),
             pltpu.VMEM((32, markers), F32),
             pltpu.VMEM((96, markers), BF16),
             pltpu.VMEM((8, TILE), F32),
@@ -805,19 +943,30 @@
             pltpu.VMEM((every * BINS, TILE), F32),
             pltpu.VMEM((every, TILE), F32),
             pltpu.VMEM((2, extent_z, TILE), BF16),
+            pltpu.VMEM((2, 32, TILE), F32),
+            pltpu.VMEM((8, 128), I32),
+            pltpu.SMEM((8, 128), I32),
+            dma,
         ],
         compiler_params=pltpu.CompilerParams(vmem_limit_bytes=24 << 20),
         name="markers",
     )(fhl, started, home, arrived)
-    new_motion, ybuf, xbuf = pl.pallas_call(
+    plane = (3, ROWS, extent_z)
+    middle = planes - 8
+    new_motion, *strips = pl.pallas_call(
         functools.partial(strip_kernel, n_gx, n_gy, markers // 2),
         out_shape=(
             jax.ShapeDtypeStruct(motion.shape, F32),
             jax.ShapeDtypeStruct((2, planes, 3, 8, extent_z), F32),
             jax.ShapeDtypeStruct((2, 6, 3, ROWS, extent_z), F32),
+            jax.ShapeDtypeStruct((middle,) + plane, F32),
+            jax.ShapeDtypeStruct((middle - 2,) + plane, F32),
+            jax.ShapeDtypeStruct((middle - 4,) + plane, F32),
+            jax.ShapeDtypeStruct((middle - 6,) + plane, F32),
+            jax.ShapeDtypeStruct((3, middle - 8, span_y, extent_z), F32),
         ),
         in_specs=[vmem] * 2 + [smem] * 3,
-        out_specs=(vmem,) * 3,
+        out_specs=(vmem,) * 8,
         scratch_shapes=[
             pltpu.VMEM((8, 8, 128), F32),
             pltpu.VMEM((8, 8, 128), F32),
@@ -832,32 +981,31 @@
             dma((n_gx,)),
             dma((n_gy,)),
             dma((n_gy,)),
-            dma((12,)),
-            dma((12,)),
-            dma((4,)),
-            dma((4,)),
+            dma((16,)),
+            dma((16,)),
+            dma((6,)),
+            dma((6,)),
         ],
         compiler_params=pltpu.CompilerParams(
             collective_id=1, has_side_effects=True, vmem_limit_bytes=24 << 20
         ),
         name="strips",
     )(rhs, acted, motion, contact_sphere, contact_partner)
-    relaxed = pl.pallas_call(
+    velocity_star = pl.pallas_call(
         functools.partial(relax_kernel, n_gy),
         out_shape=jax.ShapeDtypeStruct(velocity.shape, F32),
-        in_specs=[vmem] * 3,
+        in_specs=[vmem] * 8,
         out_specs=pl.BlockSpec(memory_space=pltpu.HBM),
-        scratch_shapes=[
-            pltpu.VMEM((planes + 4, 3, ROWS, extent_z), F32),
-            pltpu.VMEM((planes + 4, 3, ROWS, extent_z), F32),
-            pltpu.VMEM((planes + 4, 3, ROWS, extent_z), F32),
+        scratch_shapes=[pltpu.VMEM((planes + 4,) + plane, F32)] * 4
+        + [
             pltpu.VMEM(velocity.shape, F32),
-            dma((span_x // 2,)),
+            dma((6,)),
+            dma,
         ],
         compiler_params=pltpu.CompilerParams(vmem_limit_bytes=24 << 20),
         name="relax",
-    )(rhs, ybuf, xbuf)
-    return relaxed, new_motion.T
+    )(rhs, *strips)
+    return velocity_star, new_motion.T
 
 
 def solution(mesh):

time: 81.6 us -> 69.9 us (0.86)
  Pallas kernels: 79.6 us -> 68.3 us
    pallas_call x1, Pallas kernels: 20 us -> 15.1 us  [on_device(): pl.pallas_call(marker_kernel, out_shape=(jax.ShapeDtypeStruct(grown, F32)...]
    pallas_call x1, Pallas kernels: 9.33 us -> 5.49 us  [on_device(): pl.pallas_call(functools.partial(relax_kernel, n_gy), out_shape=jax.Shape...]
    pallas_call x1, Pallas kernels: 18.6 us -> 17.1 us  [on_device(): pl.pallas_call(functools.partial(request_kernel, n_gx, n_gy), out_shape=(...]
    pallas_call x1, Pallas kernels: 31.7 us -> 30.6 us  [on_device(): pl.pallas_call(functools.partial(strip_kernel, n_gx, n_gy, markers // 2),...]
where the time goes in v4:
time: 69.9 us; the launch traced here: 69.6 us
  Pallas kernels  68.3 us (98%)
  between operations  0.71 us (1%)
    pallas_call x1, Pallas kernels, on_device(): pl.pallas_call(functools.partial(strip_kernel, n_gx, n_gy, markers // 2),...  30.6 us
    pallas_call x1, Pallas kernels, on_device(): pl.pallas_call(functools.partial(request_kernel, n_gx, n_gy), out_shape=(...  17.1 us
    pallas_call x1, Pallas kernels, on_device(): pl.pallas_call(marker_kernel, out_shape=(jax.ShapeDtypeStruct(grown, F32)...  15.1 us
    pallas_call x1, Pallas kernels, on_device(): pl.pallas_call(functools.partial(relax_kernel, n_gy), out_shape=jax.Shape...  5.49 us

profile of v4, /device:TPU:1, one launch (start us, length us, event | category | flops | bytes accessed | tf_op | source)
XLA Modules:
  0.0 69.6 jit_solution(11100578155702418685)
XLA Ops:
  0.6 17.1 %requests.1 = (bf16[25,120,512]{2,1,0:T(8,128)(2,1)S(1)}, f32[27,3,40,256]{3,2,1,0:T(8,128)S(1)}, f32[32,2048]{1,0:T(8,128)S(1)}, f32[8,24,256]{2,1,0:T(8,128)S(1)}) custom-call(f32[3,16,32,256]{3,2,1,0:T(8,128)} %v_hbm.1, s32[1,2048]{1,0:T(1,128)} %bitcast.9, s32[1,2048]{1,0:T(1,128)} %bitcast.10, s32[1,2048]{1,0:T(1,128)} %bitcast.11, s32[1,2048]{1,0:T(1,128)} %bitcast.12, ...), custom_call_target="tpu_custom_call" | custom-call | tf_op jit(solution)/shard_map/requests/pallas_call | solution.py:878
  17.7 0.0 copy-start
  17.7 0.0 copy-start.1
  17.8 0.0 copy-start.2
  17.8 15.1 %markers.1 = (f32[27,3,40,256]{3,2,1,0:T(8,128)S(1)}, f32[8,128]{1,0:T(8,128)S(1)}) custom-call(bf16[25,120,512]{2,1,0:T(8,128)(2,1)S(1)} %get-tuple-element.16.fhl, f32[27,3,40,256]{3,2,1,0:T(8,128)S(1)} %get-tuple-element.17.rhs_in, f32[32,2048]{1,0:T(8,128)S(1)} %get-tuple-element.18.home, f32[8,24,256]{2,1,0:T(8,128)S(1)} %get-tuple-element.19.arrived), custom_call_target="tpu_custom_call" | custom-call | tf_op jit(solution)/shard_map/markers/pallas_call | solution.py:932
  32.9 0.0 copy-done
  32.9 0.0 copy-done.1
  32.9 0.0 copy-done.2
  32.9 30.6 %strips.1 = (f32[2,6]{1,0:T(2,128)S(1)}, f32[2,20,3,8,256]{4,3,2,1,0:T(8,128)S(1)}, f32[2,6,3,40,256]{4,3,2,1,0:T(8,128)S(1)}, f32[12,3,40,256]{3,2,1,0:T(8,128)...) custom-call(f32[27,3,40,256]{3,2,1,0:T(8,128)S(1)} %get-tuple-elemen, ...), custom_call_target="tpu_custom_call" | custom-call | tf_op jit(solution)/shard_map/strips/pallas_call | solution.py:956
  63.5 5.5 %relax.1 = f32[3,16,32,256]{3,2,1,0:T(8,128)} custom-call(f32[27,3,40,256]{3,2,1,0:T(8,128)S(1)} %get-tuple-element.20.rhs.rhs_in, f32[2,20,3,8,256]{4,3,2,1,0:T(8,128)S(1)} %get-tuple-element.22.ybuf, f32[2,6,3,40,256]{4,3,2,1,0:T(8,128)S(1)} %get-tuple-element.23.xbuf, f32[12,3,40,256]{3,2,1,0:T(8,128)S(1)} %get-tuple-element.24.mid_0, ...), custom_call_target="tpu_custom_call" | custom-call | tf_op jit(solution)/shard_map/relax/pallas_call | solution.py:994
  69.0 0.6 copy.13
Async XLA Ops:
  17.7 15.2 %copy-start = (f32[6,2]{0,1:T(2,128)S(1)}, f32[6,2]{0,1:T(2,128)}, u32[]{:S(2)}) copy-start(f32[6,2]{0,1:T(2,128)} %param.17) | copy-start | bytes 148
  17.7 15.2 %copy-start.1 = (s32[4]{0:T(128)S(1)}, s32[4]{0:T(128)}, u32[]{:S(2)}) copy-start(s32[4]{0:T(128)} %cs_ref.1) | copy-start | bytes 52
  17.8 15.2 %copy-start.2 = (s32[4]{0:T(128)S(1)}, s32[4]{0:T(128)}, u32[]{:S(2)}) copy-start(s32[4]{0:T(128)} %cp_ref.1) | copy-start | bytes 52

commit v5 on v4

--- a/solution.py
+++ b/solution.py
@@ -129,6 +129,7 @@
     hy,
     hc,
     corner,
+    edges,
     pay,
     pay3,
     slot_s,
@@ -171,7 +172,23 @@
         copy.wait()
 
     last = span_x - 2
-    top = span_y - 8
+    pl.semaphore_wait(barrier, len(LANES))
+    halo = []
+    halo.append(remote(v_ref.at[:, 0:2], hx.at[1], halo_send.at[0], halo_recv.at[0], at(-1, 0)))
+    halo.append(
+        remote(v_ref.at[:, last:span_x], hx.at[0], halo_send.at[1], halo_recv.at[1], at(1, 0))
+    )
+    halo.append(remote(edges.at[0], hy.at[1], halo_send.at[2], halo_recv.at[2], at(0, -1)))
+    halo.append(remote(edges.at[1], hy.at[0], halo_send.at[3], halo_recv.at[3], at(0, 1)))
+    for k, (dx, dy) in enumerate(DIAGONALS):
+        slot = (1 if dx < 0 else 0) * 2 + (1 if dy < 0 else 0)
+        halo.append(
+            remote(
+                corner.at[k], hc.at[slot], halo_send.at[4 + k], halo_recv.at[4 + k], at(dx, dy)
+            )
+        )
+    for copy in halo[0:2]:
+        copy.start()
     corner[...] = jnp.zeros_like(corner)
     for k, (dx, dy) in enumerate(DIAGONALS):
         x0 = 0 if dx < 0 else last
@@ -180,26 +197,11 @@
             for i in range(2):
                 row = 4 * c + 2 * i
                 corner[k, row : row + 2, :] = v_ref[c, x0 + i, y0 : y0 + 2, :]
-    pl.semaphore_wait(barrier, len(LANES))
-    halo = []
-    halo.append(remote(v_ref.at[:, 0:2], hx.at[1], halo_send.at[0], halo_recv.at[0], at(-1, 0)))
-    halo.append(
-        remote(v_ref.at[:, last:span_x], hx.at[0], halo_send.at[1], halo_recv.at[1], at(1, 0))
-    )
-    halo.append(
-        remote(v_ref.at[:, :, 0:8], hy.at[1], halo_send.at[2], halo_recv.at[2], at(0, -1))
-    )
-    halo.append(
-        remote(v_ref.at[:, :, top:span_y], hy.at[0], halo_send.at[3], halo_recv.at[3], at(0, 1))
-    )
-    for k, (dx, dy) in enumerate(DIAGONALS):
-        slot = (1 if dx < 0 else 0) * 2 + (1 if dy < 0 else 0)
-        halo.append(
-            remote(
-                corner.at[k], hc.at[slot], halo_send.at[4 + k], halo_recv.at[4 + k], at(dx, dy)
-            )
-        )
-    for copy in halo:
+    for side, y0 in enumerate((0, span_y - 2)):
+        for c in range(3):
+            for x in range(span_x):
+                edges[side, c, 2 * x : 2 * x + 2, :] = v_ref[c, x, y0 : y0 + 2, :]
+    for copy in halo[2:]:
         copy.start()
 
     pay[0:12, :] = dw_ref[...]
@@ -290,13 +292,10 @@
     for copy in halo:
         copy.wait()
 
-    def rims(x, _):
+    for x in range(span_x):
         for c in range(3):
-            frame[x + 2, c, 2:4, :] = hy[0, c, x, 6:8, :] * inner_low
-            frame[x + 2, c, 36:38, :] = hy[1, c, x, 0:2, :] * inner_high
-        return 0
-
-    lax.fori_loop(0, span_x, rims, 0)
+            frame[x + 2, c, 2:4, :] = hy[0, c, 2 * x : 2 * x + 2, :] * inner_low
+            frame[x + 2, c, 36:38, :] = hy[1, c, 2 * x : 2 * x + 2, :] * inner_high
     for side in range(2):
         for i in range(2):
             p = (0 if side == 0 else planes - 2) + i
@@ -773,14 +772,18 @@
     mid_2,
     mid_3,
     done,
+    nm_in,
     out_ref,
+    nm_ref,
     rhs,
     one,
     two,
     three,
     staged,
+    ring,
     sems,
     done_sem,
+    nm_sem,
 ):
     gy = lax.axis_index("gy")
     planes = ybuf.shape[1]
@@ -789,6 +792,8 @@
     whole_span = planes + 4
     middle = pltpu.make_async_copy(done, out_ref.at[:, 6 : span_x - 6], done_sem)
     middle.start()
+    motion = pltpu.make_async_copy(nm_in, nm_ref, nm_sem)
+    motion.start()
     inside, scale = wall_masks(gy, n_gy, span_y, rhs.shape[3])
     inner_low = jnp.where(gy > 0, 1.0, 0.0).astype(F32)
     inner_high = jnp.where(gy < n_gy - 1, 1.0, 0.0).astype(F32)
@@ -806,18 +811,38 @@
             stages[k][6 + k + i] = mid[i]
             stages[k][whole_span - 7 - k - i] = mid[mid.shape[0] - 1 - i]
 
-    def swept(k, x):
+    extent_z = rhs.shape[3]
+    apart = lax.broadcasted_iota(I32, (2 * extent_z, extent_z), 0) - lax.broadcasted_iota(
+        I32, (2 * extent_z, extent_z), 1
+    )
+    apart = apart & (extent_z - 1)
+    ring[...] = jnp.where((apart == 1) | (apart == extent_z - 1), 1.0, 0.0).astype(BF16)
+
+    def swept(k, places):
         source = stages[k - 1]
-        return relaxed(rhs[x], source[x - 1], source[x], source[x + 1], scale)
+        flat = scale.shape
+        high, low = split(jnp.concatenate([source[x].reshape(flat) for x in places], axis=0))
+        along_z = jnp.dot(
+            jnp.concatenate([high, low], axis=1), ring[...], preferred_element_type=F32
+        )
+        results = []
+        for i, x in enumerate(places):
+            centre = source[x].reshape(flat)
+            total = rhs[x].reshape(flat) + source[x - 1].reshape(flat)
+            total = total + source[x + 1].reshape(flat)
+            total = total + pltpu.roll(centre, 1, 0) + pltpu.roll(centre, flat[0] - 1, 0)
+            total = total + along_z[i * flat[0] : (i + 1) * flat[0]]
+            results.append((total * scale).reshape(rhs.shape[1:]))
+        return results
 
     for k in range(1, ITERS):
 
         def step(s, _, k=k):
-            for u in range(2):
-                low = k + 2 * s + u
-                high = whole_span - 6 - k + 2 * s + u
-                stages[k][low] = swept(k, low)
-                stages[k][high] = swept(k, high)
+            places = [
+                first + 2 * s + u for first in (k, whole_span - 6 - k) for u in range(2)
+            ]
+            for x, result in zip(places, swept(k, places)):
+                stages[k][x] = result
             return 0
 
         lax.fori_loop(0, 3, step, 0)
@@ -833,12 +858,10 @@
         ]
 
     def final(s, _):
-        for u in range(2):
-            for first in (0, span_x - 6):
-                x = first + 2 * s + u
-                result = swept(ITERS, x + HALO)
-                for c in range(3):
-                    staged[c, x] = result[c, HALO : HALO + span_y, :]
+        places = [first + 2 * s + u for first in (0, span_x - 6) for u in range(2)]
+        for x, result in zip(places, swept(ITERS, [x + HALO for x in places])):
+            for c in range(3):
+                staged[c, x] = result[c, HALO : HALO + span_y, :]
         for copy in stores(s):
             copy.start()
         return 0
@@ -848,6 +871,7 @@
         for copy in stores(s):
             copy.wait()
     middle.wait()
+    motion.wait()
 
 
 def on_device(
@@ -895,9 +919,10 @@
             pltpu.VMEM((3, markers), F32),
             pltpu.SMEM((2, 6), F32),
             pltpu.VMEM((2, 3, 2, span_y, extent_z), F32),
-            pltpu.VMEM((2, 3, span_x, 8, extent_z), F32),
+            pltpu.VMEM((2, 3, 2 * span_x, extent_z), F32),
             pltpu.VMEM((4, 16, extent_z), F32),
             pltpu.VMEM((4, 16, extent_z), F32),
+            pltpu.VMEM((2, 3, 2 * span_x, extent_z), F32),
             pltpu.VMEM((32, markers), F32),
             pltpu.VMEM((96, markers), BF16),
             pltpu.VMEM((8, TILE), F32),
@@ -991,20 +1016,25 @@
         ),
         name="strips",
     )(rhs, acted, motion, contact_sphere, contact_partner)
-    velocity_star = pl.pallas_call(
+    velocity_star, new_motion = pl.pallas_call(
         functools.partial(relax_kernel, n_gy),
-        out_shape=jax.ShapeDtypeStruct(velocity.shape, F32),
-        in_specs=[vmem] * 8,
-        out_specs=pl.BlockSpec(memory_space=pltpu.HBM),
+        out_shape=(
+            jax.ShapeDtypeStruct(velocity.shape, F32),
+            jax.ShapeDtypeStruct(motion.shape, F32),
+        ),
+        in_specs=[vmem] * 9,
+        out_specs=(hbm, hbm),
         scratch_shapes=[pltpu.VMEM((planes + 4,) + plane, F32)] * 4
         + [
             pltpu.VMEM(velocity.shape, F32),
+            pltpu.VMEM((2 * extent_z, extent_z), BF16),
             dma((6,)),
+            dma,
             dma,
         ],
         compiler_params=pltpu.CompilerParams(vmem_limit_bytes=24 << 20),
         name="relax",
-    )(rhs, *strips)
+    )(rhs, *strips, new_motion)
     return velocity_star, new_motion.T
 
 

time: 69.9 us -> 69 us (0.987)
    pallas_call x1, Pallas kernels: 15.1 us -> 16.7 us  [on_device(): pl.pallas_call(marker_kernel, out_shape=(jax.ShapeDtypeStruct(grown, F32)...]
    pallas_call x1, Pallas kernels: 30.6 us -> 29.5 us  [on_device(): pl.pallas_call(functools.partial(strip_kernel, n_gx, n_gy, markers // 2),...]
where the time goes in v5:
time: 69 us; the launch traced here: 69.1 us
  Pallas kernels  68.4 us (99%)
  between operations  0.7 us (1%)
    pallas_call x1, Pallas kernels, on_device(): pl.pallas_call(functools.partial(strip_kernel, n_gx, n_gy, markers // 2),...  29.5 us
    pallas_call x1, Pallas kernels, on_device(): pl.pallas_call(functools.partial(request_kernel, n_gx, n_gy), out_shape=(...  17 us
    pallas_call x1, Pallas kernels, on_device(): pl.pallas_call(marker_kernel, out_shape=(jax.ShapeDtypeStruct(grown, F32)...  16.7 us
    pallas_call x1, Pallas kernels, on_device(): pl.pallas_call(functools.partial(relax_kernel, n_gy), out_shape=(jax.Shap...  5.15 us

profile of v5, /device:TPU:1, one launch (start us, length us, event | category | flops | bytes accessed | tf_op | source)
XLA Modules:
  0.0 69.1 jit_solution(3341203289970896778)
XLA Ops:
  0.6 17.0 %requests.1 = (bf16[25,120,512]{2,1,0:T(8,128)(2,1)S(1)}, f32[27,3,40,256]{3,2,1,0:T(8,128)S(1)}, f32[32,2048]{1,0:T(8,128)S(1)}, f32[8,24,256]{2,1,0:T(8,128)S(1)}) custom-call(f32[3,16,32,256]{3,2,1,0:T(8,128)} %v_hbm.1, s32[1,2048]{1,0:T(1,128)} %bitcast.8, s32[1,2048]{1,0:T(1,128)} %bitcast.9, s32[1,2048]{1,0:T(1,128)} %bitcast.10, s32[1,2048]{1,0:T(1,128)} %bitcast.11, ...), custom_call_target="tpu_custom_call" | custom-call | tf_op jit(solution)/shard_map/requests/pallas_call | solution.py:902
  17.7 0.0 copy-start
  17.7 0.0 copy-start.1
  17.7 0.0 copy-start.2
  17.7 16.7 %markers.1 = (f32[27,3,40,256]{3,2,1,0:T(8,128)S(1)}, f32[8,128]{1,0:T(8,128)S(1)}) custom-call(bf16[25,120,512]{2,1,0:T(8,128)(2,1)S(1)} %get-tuple-element.18.fhl, f32[27,3,40,256]{3,2,1,0:T(8,128)S(1)} %get-tuple-element.19.rhs_in, f32[32,2048]{1,0:T(8,128)S(1)} %get-tuple-element.20.home, f32[8,24,256]{2,1,0:T(8,128)S(1)} %get-tuple-element.21.arrived), custom_call_target="tpu_custom_call" | custom-call | tf_op jit(solution)/shard_map/markers/pallas_call | solution.py:957
  34.4 0.0 copy-done
  34.4 0.0 copy-done.1
  34.4 0.0 copy-done.2
  34.4 29.5 %strips.1 = (f32[2,6]{1,0:T(2,128)S(1)}, f32[2,20,3,8,256]{4,3,2,1,0:T(8,128)S(1)}, f32[2,6,3,40,256]{4,3,2,1,0:T(8,128)S(1)}, f32[12,3,40,256]{3,2,1,0:T(8,128)...) custom-call(f32[27,3,40,256]{3,2,1,0:T(8,128)S(1)} %get-tuple-elemen, ...), custom_call_target="tpu_custom_call" | custom-call | tf_op jit(solution)/shard_map/strips/pallas_call | solution.py:981
  63.9 5.2 %relax.1 = (f32[3,16,32,256]{3,2,1,0:T(8,128)}, f32[2,6]{1,0:T(2,128)}) custom-call(f32[27,3,40,256]{3,2,1,0:T(8,128)S(1)} %get-tuple-element.22.rhs.rhs_in, f32[2,20,3,8,256]{4,3,2,1,0:T(8,128)S(1)} %get-tuple-element.24.ybuf, f32[2,6,3,40,256]{4,3,2,1,0:T(8,128)S(1)} %get-tuple-element.25.xbuf, f32[12,3,40,256]{3,2,1,0:T(8,128)S(1)} %get-tuple-element.26.mid_0, ...), custom_call_target="tpu_custom_call" | custom-call | tf_op jit(solution)/shard_map/relax/pallas_call | solution.py:1019
Async XLA Ops:
  17.7 16.7 %copy-start = (f32[6,2]{0,1:T(2,128)S(1)}, f32[6,2]{0,1:T(2,128)}, u32[]{:S(2)}) copy-start(f32[6,2]{0,1:T(2,128)} %param.17) | copy-start | bytes 148
  17.7 16.7 %copy-start.1 = (s32[4]{0:T(128)S(1)}, s32[4]{0:T(128)}, u32[]{:S(2)}) copy-start(s32[4]{0:T(128)} %cs_ref.1) | copy-start | bytes 52
  17.7 16.7 %copy-start.2 = (s32[4]{0:T(128)S(1)}, s32[4]{0:T(128)}, u32[]{:S(2)}) copy-start(s32[4]{0:T(128)} %cp_ref.1) | copy-start | bytes 52

commit v6 on v5

--- a/solution.py
+++ b/solution.py
@@ -187,8 +187,6 @@
                 corner.at[k], hc.at[slot], halo_send.at[4 + k], halo_recv.at[4 + k], at(dx, dy)
             )
         )
-    for copy in halo[0:2]:
-        copy.start()
     corner[...] = jnp.zeros_like(corner)
     for k, (dx, dy) in enumerate(DIAGONALS):
         x0 = 0 if dx < 0 else last
@@ -197,11 +195,13 @@
             for i in range(2):
                 row = 4 * c + 2 * i
                 corner[k, row : row + 2, :] = v_ref[c, x0 + i, y0 : y0 + 2, :]
+    for copy in halo[4:] + halo[0:2]:
+        copy.start()
     for side, y0 in enumerate((0, span_y - 2)):
         for c in range(3):
             for x in range(span_x):
                 edges[side, c, 2 * x : 2 * x + 2, :] = v_ref[c, x, y0 : y0 + 2, :]
-    for copy in halo[2:]:
+    for copy in halo[2:4]:
         copy.start()
 
     pay[0:12, :] = dw_ref[...]
@@ -610,9 +610,14 @@
                 start = jnp.where((row_id == c) & (lanes == s), mot_ref[s, c], start)
         moved = start - total * (RESPONSE / per_sphere)
         moved_s[...] = moved
-        first = jnp.broadcast_to(moved[:, 0:1], (8, 128))
-        other = pltpu.roll(jnp.broadcast_to(moved[:, 1:2], (8, 128)), 3, 0)
-        ag1[0] = jnp.where(lanes == here, jnp.where(row_id < 3, first, other), 0.0)
+        lane = lanes[0:1]
+        message = jnp.zeros((1, 128), F32)
+        for sphere in range(2):
+            for c in range(3):
+                message = jnp.where(
+                    lane == 3 * sphere + c, moved[c : c + 1, sphere : sphere + 1], message
+                )
+        ag1[0] = message
         for k in range(1, n_gx):
             along_x(k).start()
 
@@ -621,7 +626,7 @@
             along_x(k).wait()
         total = ag1[0]
         for k in range(1, n_gx):
-            total = total + agx[k]
+            total = total + pltpu.roll(agx[k], 6 * k, 1)
         ag1[1] = total
         for k in range(1, n_gy):
             along_y(k).start()
@@ -629,23 +634,22 @@
     def sphere_step_three():
         for k in range(1, n_gy):
             along_y(k).wait()
-        total = ag1[1]
-        for k in range(1, n_gy):
-            total = total + agy[k]
+        table = jnp.concatenate([ag1[1]] + [agy[k] for k in range(1, n_gy)], axis=0)
         moved = moved_s[...]
         pull = jnp.zeros((8, 128), F32)
         for k in range(cs_ref.shape[0]):
             partner = cp_ref[k]
             own = cs_ref[k] - 2 * here
-            chosen = jnp.sum(
-                jnp.where(lanes == lax.shift_right_logical(partner, 1), total, 0.0),
-                axis=1,
-                keepdims=True,
-            )
-            chosen = jnp.broadcast_to(chosen, (8, 128))
-            odd = jnp.broadcast_to(partner & 1, (8, 128)) == 1
-            chosen = jnp.where(odd, pltpu.roll(chosen, 5, 0), chosen)
-            pull = pull + jnp.where((lanes == own) & (row_id < 3), chosen - moved, 0.0)
+            holder = lax.shift_right_logical(partner, 1)
+            holder_x = lax.shift_right_logical(holder, n_gy.bit_length() - 1)
+            row = (gy - (holder & (n_gy - 1)) + n_gy) & (n_gy - 1)
+            lane = 6 * ((gx - holder_x + n_gx) & (n_gx - 1)) + 3 * (partner & 1)
+            mine = jnp.where(row_id == row, table, 0.0)
+            for c in range(3):
+                chosen = jnp.sum(
+                    jnp.where(lanes == lane + c, mine, 0.0), axis=(0, 1), keepdims=True
+                )
+                pull = pull + jnp.where((lanes == own) & (row_id == c), chosen - moved, 0.0)
         settled = jnp.concatenate(
             [moved + DASHPOT * pull, jnp.zeros((120, 128), F32)], axis=0
         )
@@ -835,41 +839,28 @@
             results.append((total * scale).reshape(rhs.shape[1:]))
         return results
 
+    sides = (0, span_x - 6)
     for k in range(1, ITERS):
-
-        def step(s, _, k=k):
-            places = [
-                first + 2 * s + u for first in (k, whole_span - 6 - k) for u in range(2)
-            ]
-            for x, result in zip(places, swept(k, places)):
-                stages[k][x] = result
-            return 0
-
-        lax.fori_loop(0, 3, step, 0)
-
-    def stores(s):
-        return [
-            pltpu.make_async_copy(
-                staged.at[:, pl.ds(first + 2 * s, 2)],
-                out_ref.at[:, pl.ds(first + 2 * s, 2)],
-                sems.at[2 * s + side],
-            )
-            for side, first in enumerate((0, span_x - 6))
-        ]
-
-    def final(s, _):
-        places = [first + 2 * s + u for first in (0, span_x - 6) for u in range(2)]
+        places = [k + u for u in range(6)] + [whole_span - 6 - k + u for u in range(6)]
+        for x, result in zip(places, swept(k, places)):
+            stages[k][x] = result
+
+    stores = []
+    for s in range(2):
+        places = [first + 3 * s + u for first in sides for u in range(3)]
         for x, result in zip(places, swept(ITERS, [x + HALO for x in places])):
             for c in range(3):
                 staged[c, x] = result[c, HALO : HALO + span_y, :]
-        for copy in stores(s):
-            copy.start()
-        return 0
-
-    lax.fori_loop(0, 3, final, 0)
-    for s in range(3):
-        for copy in stores(s):
-            copy.wait()
+        for side, first in enumerate(sides):
+            window = slice(first + 3 * s, first + 3 * s + 3)
+            stores.append(
+                pltpu.make_async_copy(
+                    staged.at[:, window], out_ref.at[:, window], sems.at[2 * s + side]
+                )
+            )
+            stores[-1].start()
+    for copy in stores:
+        copy.wait()
     middle.wait()
     motion.wait()
 
@@ -995,9 +986,9 @@
         scratch_shapes=[
             pltpu.VMEM((8, 8, 128), F32),
             pltpu.VMEM((8, 8, 128), F32),
-            pltpu.VMEM((n_gx, 8, 128), F32),
-            pltpu.VMEM((n_gy, 8, 128), F32),
-            pltpu.VMEM((2, 8, 128), F32),
+            pltpu.VMEM((n_gx, 1, 128), F32),
+            pltpu.VMEM((n_gy, 1, 128), F32),
+            pltpu.VMEM((2, 1, 128), F32),
             pltpu.VMEM((8, 128), F32),
             pltpu.VMEM((2, 6, 3, ROWS, extent_z), F32),
             dma((8,)),

time: 69 us -> 68 us (0.986)
  Pallas kernels: 68.4 us -> 67 us
    pallas_call x1, Pallas kernels: 16.7 us -> 15.1 us  [on_device(): pl.pallas_call(marker_kernel, out_shape=(jax.ShapeDtypeStruct(grown, F32)...]
where the time goes in v6:
time: 68 us; the launch traced here: 67.7 us
  Pallas kernels  67 us (99%)
  between operations  0.7 us (1%)
    pallas_call x1, Pallas kernels, on_device(): pl.pallas_call(functools.partial(strip_kernel, n_gx, n_gy, markers // 2),...  30.1 us
    pallas_call x1, Pallas kernels, on_device(): pl.pallas_call(functools.partial(request_kernel, n_gx, n_gy), out_shape=(...  17.2 us
    pallas_call x1, Pallas kernels, on_device(): pl.pallas_call(marker_kernel, out_shape=(jax.ShapeDtypeStruct(grown, F32)...  15.1 us
    pallas_call x1, Pallas kernels, on_device(): pl.pallas_call(functools.partial(relax_kernel, n_gy), out_shape=(jax.Shap...  4.66 us

profile of v6, /device:TPU:1, one launch (start us, length us, event | category | flops | bytes accessed | tf_op | source)
XLA Modules:
  0.0 67.7 jit_solution(17619645648011619599)
XLA Ops:
  0.6 17.2 %requests.1 = (bf16[25,120,512]{2,1,0:T(8,128)(2,1)S(1)}, f32[27,3,40,256]{3,2,1,0:T(8,128)S(1)}, f32[32,2048]{1,0:T(8,128)S(1)}, f32[8,24,256]{2,1,0:T(8,128)S(1)}) custom-call(f32[3,16,32,256]{3,2,1,0:T(8,128)} %v_hbm.1, s32[1,2048]{1,0:T(1,128)} %bitcast.8, s32[1,2048]{1,0:T(1,128)} %bitcast.9, s32[1,2048]{1,0:T(1,128)} %bitcast.10, s32[1,2048]{1,0:T(1,128)} %bitcast.11, ...), custom_call_target="tpu_custom_call" | custom-call | tf_op jit(solution)/shard_map/requests/pallas_call | solution.py:893
  17.8 0.0 copy-start
  17.8 0.0 copy-start.1
  17.8 0.0 copy-start.2
  17.8 15.1 %markers.1 = (f32[27,3,40,256]{3,2,1,0:T(8,128)S(1)}, f32[8,128]{1,0:T(8,128)S(1)}) custom-call(bf16[25,120,512]{2,1,0:T(8,128)(2,1)S(1)} %get-tuple-element.18.fhl, f32[27,3,40,256]{3,2,1,0:T(8,128)S(1)} %get-tuple-element.19.rhs_in, f32[32,2048]{1,0:T(8,128)S(1)} %get-tuple-element.20.home, f32[8,24,256]{2,1,0:T(8,128)S(1)} %get-tuple-element.21.arrived), custom_call_target="tpu_custom_call" | custom-call | tf_op jit(solution)/shard_map/markers/pallas_call | solution.py:948
  32.9 0.0 copy-done
  32.9 0.0 copy-done.1
  33.0 0.0 copy-done.2
  33.0 30.1 %strips.1 = (f32[2,6]{1,0:T(2,128)S(1)}, f32[2,20,3,8,256]{4,3,2,1,0:T(8,128)S(1)}, f32[2,6,3,40,256]{4,3,2,1,0:T(8,128)S(1)}, f32[12,3,40,256]{3,2,1,0:T(8,128)...) custom-call(f32[27,3,40,256]{3,2,1,0:T(8,128)S(1)} %get-tuple-elemen, ...), custom_call_target="tpu_custom_call" | custom-call | tf_op jit(solution)/shard_map/strips/pallas_call | solution.py:972
  63.1 4.7 %relax.1 = (f32[3,16,32,256]{3,2,1,0:T(8,128)}, f32[2,6]{1,0:T(2,128)}) custom-call(f32[27,3,40,256]{3,2,1,0:T(8,128)S(1)} %get-tuple-element.22.rhs.rhs_in, f32[2,20,3,8,256]{4,3,2,1,0:T(8,128)S(1)} %get-tuple-element.24.ybuf, f32[2,6,3,40,256]{4,3,2,1,0:T(8,128)S(1)} %get-tuple-element.25.xbuf, f32[12,3,40,256]{3,2,1,0:T(8,128)S(1)} %get-tuple-element.26.mid_0, ...), custom_call_target="tpu_custom_call" | custom-call | tf_op jit(solution)/shard_map/relax/pallas_call | solution.py:1010
Async XLA Ops:
  17.8 15.1 %copy-start = (f32[6,2]{0,1:T(2,128)S(1)}, f32[6,2]{0,1:T(2,128)}, u32[]{:S(2)}) copy-start(f32[6,2]{0,1:T(2,128)} %param.17) | copy-start | bytes 148
  17.8 15.1 %copy-start.1 = (s32[4]{0:T(128)S(1)}, s32[4]{0:T(128)}, u32[]{:S(2)}) copy-start(s32[4]{0:T(128)} %cs_ref.1) | copy-start | bytes 52
  17.8 15.1 %copy-start.2 = (s32[4]{0:T(128)S(1)}, s32[4]{0:T(128)}, u32[]{:S(2)}) copy-start(s32[4]{0:T(128)} %cp_ref.1) | copy-start | bytes 52

commit v7 on v6

--- a/solution.py
+++ b/solution.py
@@ -24,7 +24,14 @@
 HALO = 4
 LANES = [(dx, dy) for dx in (-1, 0, 1) for dy in (-1, 0, 1) if (dx, dy) != (0, 0)]
 DIAGONALS = [(dx, dy) for dx, dy in LANES if dx * dy != 0]
-RUNS = [((0, 1), (19, 1)), ((1, 2), (17, 2)), ((3, 3), (14, 3)), ((6, 8),)]
+RUNS = [
+    ((0, 1), (19, 1)),
+    ((1, 2), (17, 2)),
+    ((3, 2), (15, 2)),
+    ((5, 1), (14, 1)),
+    ((6, 8),),
+]
+X_RUNS = len(RUNS) - 1
 
 
 def split(values):
@@ -545,13 +552,13 @@
     cs_ref,
     cp_ref,
     nm_ref,
+    xbuf,
+    level_0,
+    level_1,
+    level_2,
+    level_3,
+    done,
     ybuf,
-    xbuf,
-    mid_0,
-    mid_1,
-    mid_2,
-    mid_3,
-    done,
     sums,
     ret,
     agx,
@@ -582,8 +589,6 @@
     barrier = greet(peers)
     inner_low = jnp.where(gy > 0, 1.0, 0.0).astype(F32)
     inner_high = jnp.where(gy < n_gy - 1, 1.0, 0.0).astype(F32)
-    for n in range(8):
-        sums[n] = pltpu.roll(acted[...], 128 - 2 * (n + 1), 1)
     replies = [
         remote(sums.at[n], ret.at[n], ret_send.at[n], ret_recv.at[n], at(-dx, -dy))
         for n, (dx, dy) in enumerate(LANES)
@@ -715,9 +720,11 @@
     for g in range(2):
         for copy in y_copies(g):
             copy.start()
+    for n in range(8):
+        sums[n] = pltpu.roll(acted[...], 128 - 2 * (n + 1), 1)
     for copy in replies:
         copy.start()
-    for g in range(2, 4):
+    for g in range(2, X_RUNS + 1):
         for copy in y_copies(g):
             copy.start()
     for g in range(2):
@@ -727,142 +734,102 @@
         for copy in x_copies(g):
             copy.start()
     sphere_step_one()
-    for copy in y_copies(2):
-        copy.wait()
-    stage(2)
-    for copy in x_copies(2):
-        copy.start()
-    for copy in y_copies(3):
+    for g in range(2, X_RUNS):
+        for copy in y_copies(g):
+            copy.wait()
+        stage(g)
+        for copy in x_copies(g):
+            copy.start()
+    for copy in y_copies(X_RUNS):
         copy.wait()
     inside, scale = wall_masks(gy, n_gy, span_y, rhs.shape[3])
-    span_mid = mid_0.shape[0]
-
-    def begin(i, _):
-        mid_0[i] = (with_strips(i + 4).reshape(inside.shape) * inside).reshape(mid_0.shape[1:])
+    plane = rhs.shape[1:]
+    stages = (level_0, level_1, level_2, level_3)
+    first, last = 6, planes - 3
+
+    def begin(x, _):
+        level_0[x] = (with_strips(x - 2).reshape(inside.shape) * inside).reshape(plane)
         return 0
 
-    lax.fori_loop(0, span_mid, begin, 0)
-    sphere_step_two()
-    stages = (mid_0, mid_1, mid_2, mid_3)
+    lax.fori_loop(first, last + 1, begin, 0)
+
+    def swept(k, x):
+        source = stages[k - 1]
+        return relaxed(level_0[x], source[x - 1], source[x], source[x + 1], scale)
+
+    def finish(x):
+        result = swept(ITERS, x)
+        for c in range(3):
+            done[c, x - HALO - 1] = result[c, HALO : HALO + span_y, :]
+
     for k in range(1, ITERS):
-        source, target = stages[k - 1], stages[k]
-
-        def step(s, _, source=source, target=target, k=k):
+
+        def step(s, _, k=k):
             for u in range(2):
-                i = 2 * s + u
-                target[i] = relaxed(
-                    mid_0[i + k], source[i], source[i + 1], source[i + 2], scale
-                )
+                x = first + k + 2 * s + u
+                stages[k][x] = swept(k, x)
             return 0
 
-        lax.fori_loop(0, (span_mid - 2 * k) // 2, step, 0)
-    for i in range(span_mid - 2 * ITERS):
-        result = relaxed(mid_0[i + ITERS], mid_3[i], mid_3[i + 1], mid_3[i + 2], scale)
-        for c in range(3):
-            done[c, i] = result[c, HALO : HALO + span_y, :]
-    sphere_step_three()
-    for g in range(3):
+        lax.fori_loop(0, (last - first + 1 - 2 * k) // 2, step, 0)
+    for x in range(first + ITERS, last - ITERS + 1):
+        finish(x)
+
+    for g in range(X_RUNS - 1):
         for copy in x_copies(g):
             copy.wait()
+        (low, count), _ = RUNS[g]
+        left = list(range(5 - low - count + 1, 5 - low + 1))
+        right = list(range(planes - 2 + low, planes - 2 + low + count))
+        for x, beside in [(x, xbuf[0, x]) for x in left] + [
+            (x, xbuf[1, x - planes + 2]) for x in right
+        ]:
+            whole = beside + (with_strips(x - 2) if 2 <= x < planes + 2 else rhs[x])
+            level_0[x] = (whole.reshape(inside.shape) * inside).reshape(plane)
+        for k in range(1, ITERS):
+            for x in [x + k for x in left] + [x - k for x in right]:
+                stages[k][x] = swept(k, x)
+        for x in [x + ITERS for x in left] + [x - ITERS for x in right]:
+            finish(x)
+        if g == 0:
+            sphere_step_two()
+        if g == 1:
+            sphere_step_three()
+    for copy in x_copies(X_RUNS - 1):
+        copy.wait()
 
 
 def relax_kernel(
-    n_gy,
-    rhs_in,
-    ybuf,
-    xbuf,
-    mid_0,
-    mid_1,
-    mid_2,
-    mid_3,
-    done,
-    nm_in,
-    out_ref,
-    nm_ref,
-    rhs,
-    one,
-    two,
-    three,
-    staged,
-    ring,
-    sems,
-    done_sem,
-    nm_sem,
+    n_gy, rhs, xbuf, level_0, level_1, level_2, level_3, done, nm_in, out_ref, nm_ref, staged, sems
 ):
     gy = lax.axis_index("gy")
-    planes = ybuf.shape[1]
-    span_x = planes - 4
+    top = level_0.shape[0] - 1
+    span_x = top + 1 - 2 * HALO
     span_y = out_ref.shape[2]
-    whole_span = planes + 4
-    middle = pltpu.make_async_copy(done, out_ref.at[:, 6 : span_x - 6], done_sem)
-    middle.start()
-    motion = pltpu.make_async_copy(nm_in, nm_ref, nm_sem)
-    motion.start()
+    copies = [
+        pltpu.make_async_copy(done, out_ref.at[:, 1 : span_x - 1], sems.at[0]),
+        pltpu.make_async_copy(nm_in, nm_ref, sems.at[1]),
+    ]
+    for copy in copies:
+        copy.start()
     inside, scale = wall_masks(gy, n_gy, span_y, rhs.shape[3])
-    inner_low = jnp.where(gy > 0, 1.0, 0.0).astype(F32)
-    inner_high = jnp.where(gy < n_gy - 1, 1.0, 0.0).astype(F32)
-    for i in range(6):
-        for x, beside in ((i, xbuf[0, i]), (planes - 2 + i, xbuf[1, i])):
-            whole = rhs_in[x] + beside
-            if 2 <= x < planes + 2:
-                low = whole[:, 0:8] + ybuf[0, x - 2] * inner_low
-                high = whole[:, ROWS - 8 : ROWS] + ybuf[1, x - 2] * inner_high
-                whole = jnp.concatenate([low, whole[:, 8 : ROWS - 8], high], axis=1)
-            rhs[x] = (whole.reshape(inside.shape) * inside).reshape(whole.shape)
-    stages = (rhs, one, two, three)
-    for k, (mid, count) in enumerate(((mid_0, 4), (mid_1, 2), (mid_2, 2), (mid_3, 2))):
-        for i in range(count):
-            stages[k][6 + k + i] = mid[i]
-            stages[k][whole_span - 7 - k - i] = mid[mid.shape[0] - 1 - i]
-
-    extent_z = rhs.shape[3]
-    apart = lax.broadcasted_iota(I32, (2 * extent_z, extent_z), 0) - lax.broadcasted_iota(
-        I32, (2 * extent_z, extent_z), 1
-    )
-    apart = apart & (extent_z - 1)
-    ring[...] = jnp.where((apart == 1) | (apart == extent_z - 1), 1.0, 0.0).astype(BF16)
-
-    def swept(k, places):
-        source = stages[k - 1]
-        flat = scale.shape
-        high, low = split(jnp.concatenate([source[x].reshape(flat) for x in places], axis=0))
-        along_z = jnp.dot(
-            jnp.concatenate([high, low], axis=1), ring[...], preferred_element_type=F32
+    plane = rhs.shape[1:]
+    stages = (level_0, level_1, level_2, level_3)
+    for side, (edge, inward) in enumerate(((0, 1), (top, -1))):
+        whole = rhs[edge] + xbuf[side, 0 if side == 0 else 5]
+        outer = (whole.reshape(inside.shape) * inside).reshape(plane)
+        for k in range(1, ITERS + 1):
+            x = edge + inward * k
+            source = stages[k - 1]
+            outer = relaxed(level_0[x], outer, source[x], source[x + inward], scale)
+        x = 0 if side == 0 else span_x - 1
+        for c in range(3):
+            staged[side, c, 0] = outer[c, HALO : HALO + span_y, :]
+        copies.append(
+            pltpu.make_async_copy(staged.at[side], out_ref.at[:, x : x + 1], sems.at[2 + side])
         )
-        results = []
-        for i, x in enumerate(places):
-            centre = source[x].reshape(flat)
-            total = rhs[x].reshape(flat) + source[x - 1].reshape(flat)
-            total = total + source[x + 1].reshape(flat)
-            total = total + pltpu.roll(centre, 1, 0) + pltpu.roll(centre, flat[0] - 1, 0)
-            total = total + along_z[i * flat[0] : (i + 1) * flat[0]]
-            results.append((total * scale).reshape(rhs.shape[1:]))
-        return results
-
-    sides = (0, span_x - 6)
-    for k in range(1, ITERS):
-        places = [k + u for u in range(6)] + [whole_span - 6 - k + u for u in range(6)]
-        for x, result in zip(places, swept(k, places)):
-            stages[k][x] = result
-
-    stores = []
-    for s in range(2):
-        places = [first + 3 * s + u for first in sides for u in range(3)]
-        for x, result in zip(places, swept(ITERS, [x + HALO for x in places])):
-            for c in range(3):
-                staged[c, x] = result[c, HALO : HALO + span_y, :]
-        for side, first in enumerate(sides):
-            window = slice(first + 3 * s, first + 3 * s + 3)
-            stores.append(
-                pltpu.make_async_copy(
-                    staged.at[:, window], out_ref.at[:, window], sems.at[2 * s + side]
-                )
-            )
-            stores[-1].start()
-    for copy in stores:
+        copies[-1].start()
+    for copy in copies:
         copy.wait()
-    middle.wait()
-    motion.wait()
 
 
 def on_device(
@@ -968,22 +935,18 @@
         name="markers",
     )(fhl, started, home, arrived)
     plane = (3, ROWS, extent_z)
-    middle = planes - 8
     new_motion, *strips = pl.pallas_call(
         functools.partial(strip_kernel, n_gx, n_gy, markers // 2),
         out_shape=(
             jax.ShapeDtypeStruct(motion.shape, F32),
-            jax.ShapeDtypeStruct((2, planes, 3, 8, extent_z), F32),
             jax.ShapeDtypeStruct((2, 6, 3, ROWS, extent_z), F32),
-            jax.ShapeDtypeStruct((middle,) + plane, F32),
-            jax.ShapeDtypeStruct((middle - 2,) + plane, F32),
-            jax.ShapeDtypeStruct((middle - 4,) + plane, F32),
-            jax.ShapeDtypeStruct((middle - 6,) + plane, F32),
-            jax.ShapeDtypeStruct((3, middle - 8, span_y, extent_z), F32),
-        ),
+        )
+        + (jax.ShapeDtypeStruct((planes + 4,) + plane, F32),) * 4
+        + (jax.ShapeDtypeStruct((3, span_x - 2, span_y, extent_z), F32),),
         in_specs=[vmem] * 2 + [smem] * 3,
-        out_specs=(vmem,) * 8,
+        out_specs=(vmem,) * 7,
         scratch_shapes=[
+            pltpu.VMEM((2, planes, 3, 8, extent_z), F32),
             pltpu.VMEM((8, 8, 128), F32),
             pltpu.VMEM((8, 8, 128), F32),
             pltpu.VMEM((n_gx, 1, 128), F32),
@@ -997,10 +960,10 @@
             dma((n_gx,)),
             dma((n_gy,)),
             dma((n_gy,)),
-            dma((16,)),
-            dma((16,)),
-            dma((6,)),
-            dma((6,)),
+            dma((4 * len(RUNS),)),
+            dma((4 * len(RUNS),)),
+            dma((2 * X_RUNS,)),
+            dma((2 * X_RUNS,)),
         ],
         compiler_params=pltpu.CompilerParams(
             collective_id=1, has_side_effects=True, vmem_limit_bytes=24 << 20
@@ -1013,15 +976,11 @@
             jax.ShapeDtypeStruct(velocity.shape, F32),
             jax.ShapeDtypeStruct(motion.shape, F32),
         ),
-        in_specs=[vmem] * 9,
+        in_specs=[vmem] * 8,
         out_specs=(hbm, hbm),
-        scratch_shapes=[pltpu.VMEM((planes + 4,) + plane, F32)] * 4
-        + [
-            pltpu.VMEM(velocity.shape, F32),
-            pltpu.VMEM((2 * extent_z, extent_z), BF16),
-            dma((6,)),
-            dma,
-            dma,
+        scratch_shapes=[
+            pltpu.VMEM((2, 3, 1, span_y, extent_z), F32),
+            dma((4,)),
         ],
         compiler_params=pltpu.CompilerParams(vmem_limit_bytes=24 << 20),
         name="relax",

time: 68 us -> 65.5 us (0.963)
  Pallas kernels: 67 us -> 65.1 us
    pallas_call x1, Pallas kernels: 4.66 us -> 1.85 us  [on_device(): pl.pallas_call(functools.partial(relax_kernel, n_gy), out_shape=(jax.Shap...]
    pallas_call x1, Pallas kernels: 15.1 us -> 16.6 us  [on_device(): pl.pallas_call(marker_kernel, out_shape=(jax.ShapeDtypeStruct(grown, F32)...]
where the time goes in v7:
time: 65.5 us; the launch traced here: 65.8 us
  Pallas kernels  65.1 us (99%)
  between operations  0.7 us (1%)
    pallas_call x1, Pallas kernels, on_device(): pl.pallas_call(functools.partial(strip_kernel, n_gx, n_gy, markers // 2),...  29.4 us
    pallas_call x1, Pallas kernels, on_device(): pl.pallas_call(functools.partial(request_kernel, n_gx, n_gy), out_shape=(...  17.2 us
    pallas_call x1, Pallas kernels, on_device(): pl.pallas_call(marker_kernel, out_shape=(jax.ShapeDtypeStruct(grown, F32)...  16.6 us
    pallas_call x1, Pallas kernels, on_device(): pl.pallas_call(functools.partial(relax_kernel, n_gy), out_shape=(jax.Shap...  1.85 us

profile of v7, /device:TPU:1, one launch (start us, length us, event | category | flops | bytes accessed | tf_op | source)
XLA Modules:
  0.0 65.8 jit_solution(16919547752947579062)
XLA Ops:
  0.6 17.2 %requests.1 = (bf16[25,120,512]{2,1,0:T(8,128)(2,1)S(1)}, f32[27,3,40,256]{3,2,1,0:T(8,128)S(1)}, f32[32,2048]{1,0:T(8,128)S(1)}, f32[8,24,256]{2,1,0:T(8,128)S(1)}) custom-call(f32[3,16,32,256]{3,2,1,0:T(8,128)} %v_hbm.1, s32[1,2048]{1,0:T(1,128)} %bitcast.8, s32[1,2048]{1,0:T(1,128)} %bitcast.9, s32[1,2048]{1,0:T(1,128)} %bitcast.10, s32[1,2048]{1,0:T(1,128)} %bitcast.11, ...), custom_call_target="tpu_custom_call" | custom-call | tf_op jit(solution)/shard_map/requests/pallas_call | solution.py:860
  17.8 0.0 copy-start
  17.8 0.0 copy-start.1
  17.8 0.0 copy-start.2
  17.8 16.6 %markers.1 = (f32[27,3,40,256]{3,2,1,0:T(8,128)S(1)}, f32[8,128]{1,0:T(8,128)S(1)}) custom-call(bf16[25,120,512]{2,1,0:T(8,128)(2,1)S(1)} %get-tuple-element.17.fhl, f32[27,3,40,256]{3,2,1,0:T(8,128)S(1)} %get-tuple-element.18.rhs_in, f32[32,2048]{1,0:T(8,128)S(1)} %get-tuple-element.19.home, f32[8,24,256]{2,1,0:T(8,128)S(1)} %get-tuple-element.20.arrived), custom_call_target="tpu_custom_call" | custom-call | tf_op jit(solution)/shard_map/markers/pallas_call | solution.py:915
  34.5 0.0 copy-done
  34.5 0.0 copy-done.1
  34.5 0.0 copy-done.2
  34.5 29.4 %strips.1 = (f32[2,6]{1,0:T(2,128)S(1)}, f32[2,6,3,40,256]{4,3,2,1,0:T(8,128)S(1)}, f32[24,3,40,256]{3,2,1,0:T(8,128)S(1)}, f32[24,3,40,256]{3,2,1,0:T(8,128)S(1...) custom-call(f32[27,3,40,256]{3,2,1,0:T(8,128)S(1)} %get-tuple-element.21.rhs, ...), custom_call_target="tpu_custom_call" | custom-call | tf_op jit(solution)/shard_map/strips/pallas_call | solution.py:938
  64.0 1.8 %relax.1 = (f32[3,16,32,256]{3,2,1,0:T(8,128)}, f32[2,6]{1,0:T(2,128)}) custom-call(f32[27,3,40,256]{3,2,1,0:T(8,128)S(1)} %get-tuple-element.21.rhs, f32[2,6,3,40,256]{4,3,2,1,0:T(8,128)S(1)} %get-tuple-element.23.xbuf, f32[24,3,40,256]{3,2,1,0:T(8,128)S(1)} %get-tuple-element.24.level_0, f32[24,3,40,256]{3,2,1,0:T(8,128)S(1)} %get-tuple-element.25.level_1, ...), custom_call_target="tpu_custom_call" | custom-call | tf_op jit(solution)/shard_map/relax/pallas_call | solution.py:973
Async XLA Ops:
  17.8 16.7 %copy-start = (f32[6,2]{0,1:T(2,128)S(1)}, f32[6,2]{0,1:T(2,128)}, u32[]{:S(2)}) copy-start(f32[6,2]{0,1:T(2,128)} %param.17) | copy-start | bytes 148
  17.8 16.7 %copy-start.1 = (s32[4]{0:T(128)S(1)}, s32[4]{0:T(128)}, u32[]{:S(2)}) copy-start(s32[4]{0:T(128)} %cs_ref.1) | copy-start | bytes 52
  17.8 16.7 %copy-start.2 = (s32[4]{0:T(128)S(1)}, s32[4]{0:T(128)}, u32[]{:S(2)}) copy-start(s32[4]{0:T(128)} %cp_ref.1) | copy-start | bytes 52

commit v8 on v7

--- a/solution.py
+++ b/solution.py
@@ -559,6 +559,7 @@
     level_3,
     done,
     ybuf,
+    zbuf,
     sums,
     ret,
     agx,
@@ -576,6 +577,8 @@
     y_recv,
     x_send,
     x_recv,
+    z_send,
+    z_recv,
 ):
     gx, gy, at = neighbours(n_gx, n_gy)
     here = gx * n_gy + gy
@@ -687,17 +690,22 @@
 
     def x_copies(g):
         (low, count), (high, _) = RUNS[g]
+        to_low, to_high = staged.at[1, pl.ds(low, count)], rhs.at[pl.ds(high + 2, count)]
+        if g == 0:
+            to_low = rhs.at[pl.ds(low + 2, count)]
         high = high - (planes - 6)
+        if g > 0:
+            to_high = staged.at[0, pl.ds(high, count)]
         return [
             remote(
-                staged.at[1, pl.ds(low, count)],
+                to_low,
                 xbuf.at[1, pl.ds(low, count)],
                 x_send.at[2 * g],
                 x_recv.at[2 * g],
                 at(-1, 0),
             ),
             remote(
-                staged.at[0, pl.ds(high, count)],
+                to_high,
                 xbuf.at[0, pl.ds(high, count)],
                 x_send.at[2 * g + 1],
                 x_recv.at[2 * g + 1],
@@ -705,6 +713,12 @@
             ),
         ]
 
+    def corner_copies():
+        return [
+            remote(ybuf.at[:, 0], zbuf.at[1], z_send.at[0], z_recv.at[0], at(-1, 0)),
+            remote(ybuf.at[:, planes - 1], zbuf.at[0], z_send.at[1], z_recv.at[1], at(1, 0)),
+        ]
+
     def with_strips(p):
         whole = rhs[p + 2]
         low = whole[:, 0:8] + ybuf[0, p] * inner_low
@@ -717,9 +731,8 @@
             for p in range(first, first + count):
                 staged[side, p - base] = with_strips(p)
 
-    for g in range(2):
-        for copy in y_copies(g):
-            copy.start()
+    for copy in y_copies(0) + x_copies(0) + y_copies(1):
+        copy.start()
     for n in range(8):
         sums[n] = pltpu.roll(acted[...], 128 - 2 * (n + 1), 1)
     for copy in replies:
@@ -727,12 +740,15 @@
     for g in range(2, X_RUNS + 1):
         for copy in y_copies(g):
             copy.start()
-    for g in range(2):
-        for copy in y_copies(g):
-            copy.wait()
-        stage(g)
-        for copy in x_copies(g):
-            copy.start()
+    for copy in y_copies(0):
+        copy.wait()
+    for copy in corner_copies():
+        copy.start()
+    for copy in y_copies(1):
+        copy.wait()
+    stage(1)
+    for copy in x_copies(1):
+        copy.start()
     sphere_step_one()
     for g in range(2, X_RUNS):
         for copy in y_copies(g):
@@ -775,7 +791,7 @@
         finish(x)
 
     for g in range(X_RUNS - 1):
-        for copy in x_copies(g):
+        for copy in x_copies(g) + (corner_copies() if g == 0 else []):
             copy.wait()
         (low, count), _ = RUNS[g]
         left = list(range(5 - low - count + 1, 5 - low + 1))
@@ -783,6 +799,13 @@
         for x, beside in [(x, xbuf[0, x]) for x in left] + [
             (x, xbuf[1, x - planes + 2]) for x in right
         ]:
+            if g == 0:
+                side = 0 if x < planes // 2 else 1
+                low_rows = beside[:, 0:8] + zbuf[side, 0] * inner_low
+                high_rows = beside[:, ROWS - 8 : ROWS] + zbuf[side, 1] * inner_high
+                beside = jnp.concatenate(
+                    [low_rows, beside[:, 8 : ROWS - 8], high_rows], axis=1
+                )
             whole = beside + (with_strips(x - 2) if 2 <= x < planes + 2 else rhs[x])
             level_0[x] = (whole.reshape(inside.shape) * inside).reshape(plane)
         for k in range(1, ITERS):
@@ -947,6 +970,7 @@
         out_specs=(vmem,) * 7,
         scratch_shapes=[
             pltpu.VMEM((2, planes, 3, 8, extent_z), F32),
+            pltpu.VMEM((2, 2, 3, 8, extent_z), F32),
             pltpu.VMEM((8, 8, 128), F32),
             pltpu.VMEM((8, 8, 128), F32),
             pltpu.VMEM((n_gx, 1, 128), F32),
@@ -964,6 +988,8 @@
             dma((4 * len(RUNS),)),
             dma((2 * X_RUNS,)),
             dma((2 * X_RUNS,)),
+            dma((2,)),
+            dma((2,)),
         ],
         compiler_params=pltpu.CompilerParams(
             collective_id=1, has_side_effects=True, vmem_limit_bytes=24 << 20

time: 65.5 us -> 63.9 us (0.976)
  the two profiles are of different devices: /device:TPU:1 before, /device:TPU:0 now
where the time goes in v8:
time: 63.9 us; the launch traced here: 63.7 us
  Pallas kernels  62.9 us (98%)
  between operations  0.7 us (1%)
    pallas_call x1, Pallas kernels, on_device(): pl.pallas_call(functools.partial(strip_kernel, n_gx, n_gy, markers // 2),...  25.7 us
    pallas_call x1, Pallas kernels, on_device(): pl.pallas_call(marker_kernel, out_shape=(jax.ShapeDtypeStruct(grown, F32)...  18.2 us
    pallas_call x1, Pallas kernels, on_device(): pl.pallas_call(functools.partial(request_kernel, n_gx, n_gy), out_shape=(...  17.2 us
    pallas_call x1, Pallas kernels, on_device(): pl.pallas_call(functools.partial(relax_kernel, n_gy), out_shape=(jax.Shap...  1.85 us

profile of v8, /device:TPU:0, one launch (start us, length us, event | category | flops | bytes accessed | tf_op | source)
XLA Modules:
  0.0 63.7 jit_solution(11713628317730725136)
XLA Ops:
  0.6 17.2 %requests.1 = (bf16[25,120,512]{2,1,0:T(8,128)(2,1)S(1)}, f32[27,3,40,256]{3,2,1,0:T(8,128)S(1)}, f32[32,2048]{1,0:T(8,128)S(1)}, f32[8,24,256]{2,1,0:T(8,128)S(1)}) custom-call(f32[3,16,32,256]{3,2,1,0:T(8,128)} %v_hbm.1, s32[1,2048]{1,0:T(1,128)} %bitcast.8, s32[1,2048]{1,0:T(1,128)} %bitcast.9, s32[1,2048]{1,0:T(1,128)} %bitcast.10, s32[1,2048]{1,0:T(1,128)} %bitcast.11, ...), custom_call_target="tpu_custom_call" | custom-call | tf_op jit(solution)/shard_map/requests/pallas_call | solution.py:883
  17.9 0.0 copy-start
  17.9 0.0 copy-start.1
  17.9 0.0 copy-start.2
  17.9 18.2 %markers.1 = (f32[27,3,40,256]{3,2,1,0:T(8,128)S(1)}, f32[8,128]{1,0:T(8,128)S(1)}) custom-call(bf16[25,120,512]{2,1,0:T(8,128)(2,1)S(1)} %get-tuple-element.17.fhl, f32[27,3,40,256]{3,2,1,0:T(8,128)S(1)} %get-tuple-element.18.rhs_in, f32[32,2048]{1,0:T(8,128)S(1)} %get-tuple-element.19.home, f32[8,24,256]{2,1,0:T(8,128)S(1)} %get-tuple-element.20.arrived), custom_call_target="tpu_custom_call" | custom-call | tf_op jit(solution)/shard_map/markers/pallas_call | solution.py:938
  36.1 0.0 copy-done
  36.1 0.0 copy-done.1
  36.1 0.0 copy-done.2
  36.1 25.7 %strips.1 = (f32[2,6]{1,0:T(2,128)S(1)}, f32[2,6,3,40,256]{4,3,2,1,0:T(8,128)S(1)}, f32[24,3,40,256]{3,2,1,0:T(8,128)S(1)}, f32[24,3,40,256]{3,2,1,0:T(8,128)S(1...) custom-call(f32[27,3,40,256]{3,2,1,0:T(8,128)S(1)} %get-tuple-element.21.rhs, ...), custom_call_target="tpu_custom_call" | custom-call | tf_op jit(solution)/shard_map/strips/pallas_call | solution.py:961
  61.8 1.8 %relax.1 = (f32[3,16,32,256]{3,2,1,0:T(8,128)}, f32[2,6]{1,0:T(2,128)}) custom-call(f32[27,3,40,256]{3,2,1,0:T(8,128)S(1)} %get-tuple-element.21.rhs, f32[2,6,3,40,256]{4,3,2,1,0:T(8,128)S(1)} %get-tuple-element.23.xbuf, f32[24,3,40,256]{3,2,1,0:T(8,128)S(1)} %get-tuple-element.24.level_0, f32[24,3,40,256]{3,2,1,0:T(8,128)S(1)} %get-tuple-element.25.level_1, ...), custom_call_target="tpu_custom_call" | custom-call | tf_op jit(solution)/shard_map/relax/pallas_call | solution.py:999
Async XLA Ops:
  17.9 18.2 %copy-start = (f32[6,2]{0,1:T(2,128)S(1)}, f32[6,2]{0,1:T(2,128)}, u32[]{:S(2)}) copy-start(f32[6,2]{0,1:T(2,128)} %param.17) | copy-start | bytes 148
  17.9 18.2 %copy-start.1 = (s32[4]{0:T(128)S(1)}, s32[4]{0:T(128)}, u32[]{:S(2)}) copy-start(s32[4]{0:T(128)} %cs_ref.1) | copy-start | bytes 52
  17.9 18.2 %copy-start.2 = (s32[4]{0:T(128)S(1)}, s32[4]{0:T(128)}, u32[]{:S(2)}) copy-start(s32[4]{0:T(128)} %cp_ref.1) | copy-start | bytes 52

commit v9 on v8

--- a/solution.py
+++ b/solution.py
@@ -64,6 +64,11 @@
         device_id=peer,
         device_id_type=MESH,
     )
+
+
+def wait_all(whole, send, recv, at):
+    copy = remote(whole, whole, send, recv, at(1, 0))
+    copy.wait()
 
 
 def greet(peers):
@@ -261,7 +266,7 @@
     lax.fori_loop(0, 8, compact, 0)
 
     requests = [
-        remote(snd.at[n], inbox.at[n], pay_send.at[n], pay_recv.at[n], at(dx, dy))
+        remote(snd.at[n], inbox.at[n], pay_send.at[0], pay_recv.at[0], at(dx, dy))
         for n, (dx, dy) in enumerate(LANES)
     ]
     for copy in requests:
@@ -320,8 +325,7 @@
         return 0
 
     lax.fori_loop(0, planes, halve, 0)
-    for copy in requests:
-        copy.wait()
+    wait_all(inbox, pay_send.at[0], pay_recv.at[0], at)
     arrived[...] = inbox[...]
 
 
@@ -593,7 +597,7 @@
     inner_low = jnp.where(gy > 0, 1.0, 0.0).astype(F32)
     inner_high = jnp.where(gy < n_gy - 1, 1.0, 0.0).astype(F32)
     replies = [
-        remote(sums.at[n], ret.at[n], ret_send.at[n], ret_recv.at[n], at(-dx, -dy))
+        remote(sums.at[n], ret.at[n], ret_send.at[0], ret_recv.at[0], at(-dx, -dy))
         for n, (dx, dy) in enumerate(LANES)
     ]
     lanes = lax.broadcasted_iota(I32, (8, 128), 1)
@@ -601,14 +605,13 @@
     pl.semaphore_wait(barrier, len(peers))
 
     def along_x(k):
-        return remote(ag1.at[0], agx.at[k], agx_send.at[k], agx_recv.at[k], at(k, 0))
+        return remote(ag1.at[0], agx.at[k], agx_send.at[0], agx_recv.at[0], at(k, 0))
 
     def along_y(k):
-        return remote(ag1.at[1], agy.at[k], agy_send.at[k], agy_recv.at[k], at(0, k))
+        return remote(ag1.at[1], agy.at[k], agy_send.at[0], agy_recv.at[0], at(0, k))
 
     def sphere_step_one():
-        for copy in replies:
-            copy.wait()
+        wait_all(ret, ret_send.at[0], ret_recv.at[0], at)
         total = acted[...]
         for n in range(8):
             total = total + ret[n]
@@ -630,8 +633,7 @@
             along_x(k).start()
 
     def sphere_step_two():
-        for k in range(1, n_gx):
-            along_x(k).wait()
+        wait_all(agx.at[pl.ds(1, n_gx - 1)], agx_send.at[0], agx_recv.at[0], at)
         total = ag1[0]
         for k in range(1, n_gx):
             total = total + pltpu.roll(agx[k], 6 * k, 1)
@@ -640,8 +642,7 @@
             along_y(k).start()
 
     def sphere_step_three():
-        for k in range(1, n_gy):
-            along_y(k).wait()
+        wait_all(agy.at[pl.ds(1, n_gy - 1)], agy_send.at[0], agy_recv.at[0], at)
         table = jnp.concatenate([ag1[1]] + [agy[k] for k in range(1, n_gy)], axis=0)
         moved = moved_s[...]
         pull = jnp.zeros((8, 128), F32)
@@ -665,15 +666,14 @@
 
     def y_copies(g):
         copies = []
-        for r, (first, count) in enumerate(RUNS[g]):
+        for first, count in RUNS[g]:
             lo = first + 2
-            base = 4 * g + 2 * r
             copies.append(
                 remote(
                     rhs.at[pl.ds(lo, count), :, pl.ds(0, 8)],
                     ybuf.at[1, pl.ds(first, count)],
-                    y_send.at[base],
-                    y_recv.at[base],
+                    y_send.at[g],
+                    y_recv.at[g],
                     at(0, -1),
                 )
             )
@@ -681,12 +681,16 @@
                 remote(
                     rhs.at[pl.ds(lo, count), :, pl.ds(ROWS - 8, 8)],
                     ybuf.at[0, pl.ds(first, count)],
-                    y_send.at[base + 1],
-                    y_recv.at[base + 1],
+                    y_send.at[g],
+                    y_recv.at[g],
                     at(0, 1),
                 )
             )
         return copies
+
+    def wait_y(g):
+        planes_in = sum(count for _, count in RUNS[g])
+        wait_all(ybuf.at[:, pl.ds(0, planes_in)], y_send.at[g], y_recv.at[g], at)
 
     def x_copies(g):
         (low, count), (high, _) = RUNS[g]
@@ -740,24 +744,20 @@
     for g in range(2, X_RUNS + 1):
         for copy in y_copies(g):
             copy.start()
-    for copy in y_copies(0):
-        copy.wait()
+    wait_y(0)
     for copy in corner_copies():
         copy.start()
-    for copy in y_copies(1):
-        copy.wait()
+    wait_y(1)
     stage(1)
     for copy in x_copies(1):
         copy.start()
     sphere_step_one()
     for g in range(2, X_RUNS):
-        for copy in y_copies(g):
-            copy.wait()
+        wait_y(g)
         stage(g)
         for copy in x_copies(g):
             copy.start()
-    for copy in y_copies(X_RUNS):
-        copy.wait()
+    wait_y(X_RUNS)
     inside, scale = wall_masks(gy, n_gy, span_y, rhs.shape[3])
     plane = rhs.shape[1:]
     stages = (level_0, level_1, level_2, level_3)
@@ -913,8 +913,8 @@
             dma((8,)),
             dma((8,)),
             dma((8,)),
-            dma((8,)),
-            dma((8,)),
+            dma((1,)),
+            dma((1,)),
         ],
         compiler_params=pltpu.CompilerParams(
             collective_id=0, has_side_effects=True, vmem_limit_bytes=24 << 20
@@ -978,14 +978,14 @@
             pltpu.VMEM((2, 1, 128), F32),
             pltpu.VMEM((8, 128), F32),
             pltpu.VMEM((2, 6, 3, ROWS, extent_z), F32),
-            dma((8,)),
-            dma((8,)),
-            dma((n_gx,)),
-            dma((n_gx,)),
-            dma((n_gy,)),
-            dma((n_gy,)),
-            dma((4 * len(RUNS),)),
-            dma((4 * len(RUNS),)),
+            dma((1,)),
+            dma((1,)),
+            dma((1,)),
+            dma((1,)),
+            dma((1,)),
+            dma((1,)),
+            dma((len(RUNS),)),
+            dma((len(RUNS),)),
             dma((2 * X_RUNS,)),
             dma((2 * X_RUNS,)),
             dma((2,)),

time: 63.9 us -> 63.4 us (level)
  the two profiles are of different devices: /device:TPU:0 before, /device:TPU:1 now
where the time goes in v9:
time: 63.4 us; the launch traced here: 63.1 us
  Pallas kernels  62.3 us (98%)
  between operations  0.7 us (1%)
    pallas_call x1, Pallas kernels, on_device(): pl.pallas_call(functools.partial(strip_kernel, n_gx, n_gy, markers // 2),...  28.3 us
    pallas_call x1, Pallas kernels, on_device(): pl.pallas_call(functools.partial(request_kernel, n_gx, n_gy), out_shape=(...  17 us
    pallas_call x1, Pallas kernels, on_device(): pl.pallas_call(marker_kernel, out_shape=(jax.ShapeDtypeStruct(grown, F32)...  15.1 us
    pallas_call x1, Pallas kernels, on_device(): pl.pallas_call(functools.partial(relax_kernel, n_gy), out_shape=(jax.Shap...  1.85 us

profile of v9, /device:TPU:1, one launch (start us, length us, event | category | flops | bytes accessed | tf_op | source)
XLA Modules:
  0.0 63.1 jit_solution(8511196443255305023)
XLA Ops:
  0.6 17.0 %requests.1 = (bf16[25,120,512]{2,1,0:T(8,128)(2,1)S(1)}, f32[27,3,40,256]{3,2,1,0:T(8,128)S(1)}, f32[32,2048]{1,0:T(8,128)S(1)}, f32[8,24,256]{2,1,0:T(8,128)S(1)}) custom-call(f32[3,16,32,256]{3,2,1,0:T(8,128)} %v_hbm.1, s32[1,2048]{1,0:T(1,128)} %bitcast.8, s32[1,2048]{1,0:T(1,128)} %bitcast.9, s32[1,2048]{1,0:T(1,128)} %bitcast.10, s32[1,2048]{1,0:T(1,128)} %bitcast.11, ...), custom_call_target="tpu_custom_call" | custom-call | tf_op jit(solution)/shard_map/requests/pallas_call | solution.py:883
  17.7 0.0 copy-start
  17.7 0.0 copy-start.1
  17.7 0.0 copy-start.2
  17.7 15.1 %markers.1 = (f32[27,3,40,256]{3,2,1,0:T(8,128)S(1)}, f32[8,128]{1,0:T(8,128)S(1)}) custom-call(bf16[25,120,512]{2,1,0:T(8,128)(2,1)S(1)} %get-tuple-element.17.fhl, f32[27,3,40,256]{3,2,1,0:T(8,128)S(1)} %get-tuple-element.18.rhs_in, f32[32,2048]{1,0:T(8,128)S(1)} %get-tuple-element.19.home, f32[8,24,256]{2,1,0:T(8,128)S(1)} %get-tuple-element.20.arrived), custom_call_target="tpu_custom_call" | custom-call | tf_op jit(solution)/shard_map/markers/pallas_call | solution.py:938
  32.9 0.0 copy-done
  32.9 0.0 copy-done.1
  32.9 0.0 copy-done.2
  32.9 28.3 %strips.1 = (f32[2,6]{1,0:T(2,128)S(1)}, f32[2,6,3,40,256]{4,3,2,1,0:T(8,128)S(1)}, f32[24,3,40,256]{3,2,1,0:T(8,128)S(1)}, f32[24,3,40,256]{3,2,1,0:T(8,128)S(1...) custom-call(f32[27,3,40,256]{3,2,1,0:T(8,128)S(1)} %get-tuple-element.21.rhs, ...), custom_call_target="tpu_custom_call" | custom-call | tf_op jit(solution)/shard_map/strips/pallas_call | solution.py:961
  61.2 1.8 %relax.1 = (f32[3,16,32,256]{3,2,1,0:T(8,128)}, f32[2,6]{1,0:T(2,128)}) custom-call(f32[27,3,40,256]{3,2,1,0:T(8,128)S(1)} %get-tuple-element.21.rhs, f32[2,6,3,40,256]{4,3,2,1,0:T(8,128)S(1)} %get-tuple-element.23.xbuf, f32[24,3,40,256]{3,2,1,0:T(8,128)S(1)} %get-tuple-element.24.level_0, f32[24,3,40,256]{3,2,1,0:T(8,128)S(1)} %get-tuple-element.25.level_1, ...), custom_call_target="tpu_custom_call" | custom-call | tf_op jit(solution)/shard_map/relax/pallas_call | solution.py:999
Async XLA Ops:
  17.7 15.2 %copy-start = (f32[6,2]{0,1:T(2,128)S(1)}, f32[6,2]{0,1:T(2,128)}, u32[]{:S(2)}) copy-start(f32[6,2]{0,1:T(2,128)} %param.17) | copy-start | bytes 148
  17.7 15.2 %copy-start.1 = (s32[4]{0:T(128)S(1)}, s32[4]{0:T(128)}, u32[]{:S(2)}) copy-start(s32[4]{0:T(128)} %cs_ref.1) | copy-start | bytes 52
  17.7 15.2 %copy-start.2 = (s32[4]{0:T(128)S(1)}, s32[4]{0:T(128)}, u32[]{:S(2)}) copy-start(s32[4]{0:T(128)} %cp_ref.1) | copy-start | bytes 52

commit v10 on v9

--- a/solution.py
+++ b/solution.py
@@ -399,11 +399,8 @@
         pay3[q] = terms(filled)
     acted[...] = jnp.zeros_like(acted)
 
-    def start_from(p, _):
+    for p in range(rhs.shape[0]):
         rhs[p] = rhs_in[p]
-        return 0
-
-    lax.fori_loop(0, rhs.shape[0], start_from, 0)
     slot_id = lax.broadcasted_iota(I32, (TILE, TILE), 0).astype(F32)
 
     def gather(n):

time: 63.4 us -> 62.4 us (0.984)
  Pallas kernels: 62.3 us -> 61.1 us
    pallas_call x1, Pallas kernels: 28.3 us -> 27.3 us  [on_device(): pl.pallas_call(functools.partial(strip_kernel, n_gx, n_gy, markers // 2),...]
where the time goes in v10:
time: 62.4 us; the launch traced here: 61.9 us
  Pallas kernels  61.1 us (98%)
  between operations  0.7 us (1%)
    pallas_call x1, Pallas kernels, on_device(): pl.pallas_call(functools.partial(strip_kernel, n_gx, n_gy, markers // 2),...  27.3 us
    pallas_call x1, Pallas kernels, on_device(): pl.pallas_call(functools.partial(request_kernel, n_gx, n_gy), out_shape=(...  17 us
    pallas_call x1, Pallas kernels, on_device(): pl.pallas_call(marker_kernel, out_shape=(jax.ShapeDtypeStruct(grown, F32)...  15 us
    pallas_call x1, Pallas kernels, on_device(): pl.pallas_call(functools.partial(relax_kernel, n_gy), out_shape=(jax.Shap...  1.85 us

profile of v10, /device:TPU:1, one launch (start us, length us, event | category | flops | bytes accessed | tf_op | source)
XLA Modules:
  0.0 61.9 jit_solution(15467330819284351185)
XLA Ops:
  0.6 17.0 %requests.1 = (bf16[25,120,512]{2,1,0:T(8,128)(2,1)S(1)}, f32[27,3,40,256]{3,2,1,0:T(8,128)S(1)}, f32[32,2048]{1,0:T(8,128)S(1)}, f32[8,24,256]{2,1,0:T(8,128)S(1)}) custom-call(f32[3,16,32,256]{3,2,1,0:T(8,128)} %v_hbm.1, s32[1,2048]{1,0:T(1,128)} %bitcast.8, s32[1,2048]{1,0:T(1,128)} %bitcast.9, s32[1,2048]{1,0:T(1,128)} %bitcast.10, s32[1,2048]{1,0:T(1,128)} %bitcast.11, ...), custom_call_target="tpu_custom_call" | custom-call | tf_op jit(solution)/shard_map/requests/pallas_call | solution.py:880
  17.7 0.0 copy-start
  17.7 0.0 copy-start.1
  17.7 0.0 copy-start.2
  17.7 15.0 %markers.1 = (f32[27,3,40,256]{3,2,1,0:T(8,128)S(1)}, f32[8,128]{1,0:T(8,128)S(1)}) custom-call(bf16[25,120,512]{2,1,0:T(8,128)(2,1)S(1)} %get-tuple-element.17.fhl, f32[27,3,40,256]{3,2,1,0:T(8,128)S(1)} %get-tuple-element.18.rhs_in, f32[32,2048]{1,0:T(8,128)S(1)} %get-tuple-element.19.home, f32[8,24,256]{2,1,0:T(8,128)S(1)} %get-tuple-element.20.arrived), custom_call_target="tpu_custom_call" | custom-call | tf_op jit(solution)/shard_map/markers/pallas_call | solution.py:935
  32.7 0.0 copy-done
  32.7 0.0 copy-done.1
  32.7 0.0 copy-done.2
  32.8 27.3 %strips.1 = (f32[2,6]{1,0:T(2,128)S(1)}, f32[2,6,3,40,256]{4,3,2,1,0:T(8,128)S(1)}, f32[24,3,40,256]{3,2,1,0:T(8,128)S(1)}, f32[24,3,40,256]{3,2,1,0:T(8,128)S(1...) custom-call(f32[27,3,40,256]{3,2,1,0:T(8,128)S(1)} %get-tuple-element.21.rhs, ...), custom_call_target="tpu_custom_call" | custom-call | tf_op jit(solution)/shard_map/strips/pallas_call | solution.py:958
  60.0 1.8 %relax.1 = (f32[3,16,32,256]{3,2,1,0:T(8,128)}, f32[2,6]{1,0:T(2,128)}) custom-call(f32[27,3,40,256]{3,2,1,0:T(8,128)S(1)} %get-tuple-element.21.rhs, f32[2,6,3,40,256]{4,3,2,1,0:T(8,128)S(1)} %get-tuple-element.23.xbuf, f32[24,3,40,256]{3,2,1,0:T(8,128)S(1)} %get-tuple-element.24.level_0, f32[24,3,40,256]{3,2,1,0:T(8,128)S(1)} %get-tuple-element.25.level_1, ...), custom_call_target="tpu_custom_call" | custom-call | tf_op jit(solution)/shard_map/relax/pallas_call | solution.py:996
Async XLA Ops:
  17.7 15.1 %copy-start = (f32[6,2]{0,1:T(2,128)S(1)}, f32[6,2]{0,1:T(2,128)}, u32[]{:S(2)}) copy-start(f32[6,2]{0,1:T(2,128)} %param.17) | copy-start | bytes 148
  17.7 15.1 %copy-start.1 = (s32[4]{0:T(128)S(1)}, s32[4]{0:T(128)}, u32[]{:S(2)}) copy-start(s32[4]{0:T(128)} %cs_ref.1) | copy-start | bytes 52
  17.7 15.1 %copy-start.2 = (s32[4]{0:T(128)S(1)}, s32[4]{0:T(128)}, u32[]{:S(2)}) copy-start(s32[4]{0:T(128)} %cp_ref.1) | copy-start | bytes 52
